TPU v7x, 32 devices: a whole 2x2x4 slice. The times are simulated.
32 devices in a mesh: fsdp: 4 (over y, x), ctx: 4 (over z), tp: 2 (over core).
Axes of the slice: x: 2, y: 2, z: 4, core: 2. Of those that a mesh axis runs over, the one named last changes fastest.
Arguments:
- tokens: bfloat16 [8, 1024, 768], P('fsdp', 'ctx'), may hold values from -6 to 6
- lengths: int32 [8], P('fsdp'), may hold values from 256 to 1024, as said below
- cotangent: bfloat16 [8, 1024, 768], P('fsdp', 'ctx'), may hold values from -6 to 6
- ln1_gain: float32 [768], replicated, may hold values from 0.5 to 1.5
- ln1_bias: float32 [768], replicated, may hold values from -1.8 to 1.8
- qkv_weight: bfloat16 [768, 3, 768], P('fsdp', None, 'tp'), may hold values from -0.21875 to 0.21875
- conv_kernel: float32 [3, 3, 768], P(None, None, 'tp'), may hold values from -3.5 to 3.5
- conv_bias: float32 [3, 768], P(None, 'tp'), may hold values from -1.8 to 1.8
- out_weight: bfloat16 [768, 768], P('tp', 'fsdp'), may hold values from -1.75 to 1.75
- ln2_gain: float32 [768], replicated, may hold values from 0.5 to 1.5
- ln2_bias: float32 [768], replicated, may hold values from -1.8 to 1.8
- up_weight: bfloat16 [768, 3072], P('fsdp', 'tp'), may hold values from -0.21875 to 0.21875
- down_weight: bfloat16 [3072, 768], P('tp', 'fsdp'), may hold values from -0.109375 to 0.109375
Outputs:
- result: bfloat16 [8, 1024, 768], P('fsdp', 'ctx')
- input_grad: float32 [8, 1024, 768], P('fsdp', 'ctx')
- ln1_gain_grad: float32 [768], replicated
- ln1_bias_grad: float32 [768], replicated
- qkv_weight_grad: float32 [768, 3, 768], P('fsdp', None, 'tp')
- conv_kernel_grad: float32 [3, 3, 768], P(None, None, 'tp')
- conv_bias_grad: float32 [3, 768], P(None, 'tp')
- out_weight_grad: float32 [768, 768], P('tp', 'fsdp')
- ln2_gain_grad: float32 [768], replicated
- ln2_bias_grad: float32 [768], replicated
- up_weight_grad: float32 [768, 3072], P('fsdp', 'tp')
- down_weight_grad: float32 [3072, 768], P('tp', 'fsdp')
Inputs may be any that keep to these rules, and one draw needn't show every extreme that they name: `lengths`: some slot holds 1024 tokens and some other slot 256.
All inputs are finite; a program needn't handle non-finite values.
Results may differ from a plain program's by a relative error of at most 0.014.
The roundings to bfloat16 on the way count: a program that leaves them out, or rounds other values in their place, can miss the bound.
Values may be sent and summed in bfloat16 or wider, within the bound.
A program may use at most 256 MiB of HBM per device.

v0:
```python
import jax
import jax.numpy as jnp
from jax import lax
from jax.sharding import PartitionSpec as P

HD = 64


EPSILON = 1e-05
SCALING = 0.125
MASKED = -1e30


def shifted(block, axis, distance):
    devices = range(lax.axis_size(axis))
    route = [(i - distance, i) for i in devices if i - distance in devices]
    return lax.ppermute(block, axis, route)


def layer_norm(row_data, norm_gain, shift_bias):
    centred = row_data - jnp.mean(row_data, axis=-1, keepdims=True)
    recip = lax.rsqrt(jnp.mean(centred * centred, axis=-1, keepdims=True) + EPSILON)
    normed = centred * recip
    return (normed * norm_gain + shift_bias, normed, recip)


def norm_back(grad_in, normed, recip, norm_gain):
    scaled = grad_in * norm_gain
    return recip * (
        scaled
        - jnp.mean(scaled, axis=-1, keepdims=True)
        - normed * jnp.mean(scaled * normed, axis=-1, keepdims=True)
    )


def tile_scores(query_part, key_part, query_pos, key_pos, lengths):
    scores = (
        jnp.einsum("mqhd,mkhd->mhqk", query_part, key_part, preferred_element_type=jnp.float32)
        * SCALING
    )
    allowed = (key_pos[None, None, :] <= query_pos[None, :, None]) & (
        key_pos[None, None, :] < lengths[:, None, None]
    )
    return jnp.where(allowed[:, None], scores, MASKED)


def tile_grads(
    query_part, key_part, value_part, grad_part, log_part, delta_part, query_pos, key_pos, lengths
):
    probs_full = jnp.exp(tile_scores(query_part, key_part, query_pos, key_pos, lengths) - log_part)
    prob_grad = jnp.einsum(
        "mqhd,mkhd->mhqk", grad_part, value_part, preferred_element_type=jnp.float32
    )
    score_grad = (probs_full * (prob_grad - delta_part)).astype(jnp.bfloat16)
    return (probs_full, prob_grad, score_grad)


def local(
    tokens,
    lengths,
    cotangent,
    ln1_gain,
    ln1_bias,
    qkv_weight,
    conv_kernel,
    conv_bias,
    out_weight,
    ln2_gain,
    ln2_bias,
    up_weight,
    down_weight,
):
    batches, block_rows, model_width = tokens.shape
    all_rows = batches * block_rows
    qkv_full, out_full, up_full_w, down_full_w = (
        lax.all_gather(qkv_weight, "fsdp", axis=0, tiled=True),
        lax.all_gather(out_weight, "fsdp", axis=1, tiled=True),
        lax.all_gather(up_weight, "fsdp", axis=0, tiled=True),
        lax.all_gather(down_weight, "fsdp", axis=1, tiled=True),
    )
    local_width = qkv_full.shape[2]
    local_heads = local_width // HD
    ctx_count = lax.axis_size("ctx")
    slot_span = block_rows * ctx_count
    group_blocks = 4
    key_span = block_rows * group_blocks
    ctx_index = lax.axis_index("ctx")
    positions = ctx_index * block_rows + jnp.arange(block_rows, dtype=jnp.int32)
    span_iota = jnp.arange(key_span, dtype=jnp.int32)
    block_count = (ctx_index * block_rows + block_rows + key_span - 1) // key_span
    token_valid = positions[None, :] < lengths[:, None]

    def span_slice(array_data, block, axis_pos):
        return lax.dynamic_slice_in_dim(array_data, block * key_span, key_span, axis_pos)

    inputs = tokens.astype(jnp.float32).reshape(all_rows, model_width)
    first_out, first_hat, first_recip = layer_norm(inputs, ln1_gain, ln1_bias)
    first_low = first_out.astype(jnp.bfloat16)
    pre_low = jnp.einsum(
        "td,dcn->tcn", first_low, qkv_full, preferred_element_type=jnp.float32
    ).astype(jnp.bfloat16)
    pre_low = pre_low.reshape(batches, block_rows, 3, local_width)
    earlier = shifted(pre_low[:, block_rows - 2 :], "ctx", 1)
    extended = jnp.concatenate([earlier, pre_low], axis=1).astype(jnp.float32)
    conv_out = (
        conv_bias
        + conv_kernel[0] * extended[:, 2:]
        + conv_kernel[1] * extended[:, 1:-1]
        + conv_kernel[2] * extended[:, :-2]
    ).astype(jnp.bfloat16)
    query_heads = conv_out[:, :, 0].reshape(batches, block_rows, local_heads, HD)
    own_pairs = conv_out[:, :, 1:]
    whole_pairs = lax.all_gather(own_pairs, "ctx", axis=1, tiled=True)
    key_heads = whole_pairs[:, :, 0].reshape(batches, slot_span, local_heads, HD)
    value_heads = whole_pairs[:, :, 1].reshape(batches, slot_span, local_heads, HD)

    def stat_step(block, carry):
        row_max, total = carry
        key_pos = block * key_span + span_iota
        scores = tile_scores(
            query_heads, span_slice(key_heads, block, 1), positions, key_pos, lengths
        )
        new_max = jnp.maximum(row_max, jnp.max(scores, axis=-1, keepdims=True))
        total = total * jnp.exp(row_max - new_max) + jnp.sum(
            jnp.exp(scores - new_max), axis=-1, keepdims=True
        )
        return (new_max, total)

    stat_shape = (batches, local_heads, block_rows, 1)
    row_max, total = lax.fori_loop(
        0,
        block_count,
        stat_step,
        (jnp.full(stat_shape, MASKED, jnp.float32), jnp.zeros(stat_shape, jnp.float32)),
    )
    log_total = row_max + jnp.log(total)

    def value_step(block, accum):
        key_pos = block * key_span + span_iota
        scores = tile_scores(
            query_heads, span_slice(key_heads, block, 1), positions, key_pos, lengths
        )
        probs_low = jnp.exp(scores - log_total).astype(jnp.bfloat16)
        return accum + jnp.einsum(
            "mhqk,mkhd->mqhd",
            probs_low,
            span_slice(value_heads, block, 1),
            preferred_element_type=jnp.float32,
        )

    attn_acc = lax.fori_loop(
        0, block_count, value_step, jnp.zeros((batches, block_rows, local_heads, HD), jnp.float32)
    )
    attn_low = attn_acc.reshape(all_rows, local_width).astype(jnp.bfloat16)
    attn_out = lax.psum(jnp.dot(attn_low, out_full, preferred_element_type=jnp.float32), "tp")
    middle = inputs + attn_out
    second_out, second_hat, second_recip = layer_norm(middle, ln2_gain, ln2_bias)
    second_low = second_out.astype(jnp.bfloat16)
    up_full = jnp.dot(second_low, up_full_w, preferred_element_type=jnp.float32)
    rectified = jnp.maximum(up_full, 0.0)
    act_low = (rectified * rectified).astype(jnp.bfloat16)
    ffn_out = lax.psum(jnp.dot(act_low, down_full_w, preferred_element_type=jnp.float32), "tp")
    result = (middle + ffn_out).reshape(batches, block_rows, model_width).astype(jnp.bfloat16)
    grad_out = (
        cotangent.astype(jnp.float32) * token_valid[:, :, None].astype(jnp.float32)
    ).reshape(all_rows, model_width)
    grad_low = grad_out.astype(jnp.bfloat16)
    down_wgrad = jnp.einsum("tf,td->fd", act_low, grad_low, preferred_element_type=jnp.float32)
    act_grad = jnp.einsum("td,fd->tf", grad_low, down_full_w, preferred_element_type=jnp.float32)
    up_grad_low = (act_grad * 2.0 * rectified).astype(jnp.bfloat16)
    up_wgrad = jnp.einsum("td,tf->df", second_low, up_grad_low, preferred_element_type=jnp.float32)
    second_grad = lax.psum(
        jnp.einsum("tf,df->td", up_grad_low, up_full_w, preferred_element_type=jnp.float32), "tp"
    )
    gain_two_grad = jnp.sum(second_grad * second_hat, axis=0)
    bias_two_grad = jnp.sum(second_grad, axis=0)
    middle_grad = grad_out + norm_back(second_grad, second_hat, second_recip, ln2_gain)
    middle_low = middle_grad.astype(jnp.bfloat16)
    out_wgrad = jnp.einsum("tn,td->nd", attn_low, middle_low, preferred_element_type=jnp.float32)
    attn_flat = jnp.einsum(
        "td,nd->tn", middle_low, out_full, preferred_element_type=jnp.float32
    ).astype(jnp.bfloat16)
    attn_grad = attn_flat.reshape(batches, block_rows, local_heads, HD)

    def delta_step(block, accum):
        key_pos = block * key_span + span_iota
        probs_full = jnp.exp(
            tile_scores(query_heads, span_slice(key_heads, block, 1), positions, key_pos, lengths)
            - log_total
        )
        prob_grad = jnp.einsum(
            "mqhd,mkhd->mhqk",
            attn_grad,
            span_slice(value_heads, block, 1),
            preferred_element_type=jnp.float32,
        )
        return accum + jnp.sum(probs_full * prob_grad, axis=-1, keepdims=True)

    delta = lax.fori_loop(0, block_count, delta_step, jnp.zeros(stat_shape, jnp.float32))
    query_zero = jnp.zeros((batches, block_rows, local_heads, HD), jnp.float32)

    def back_step(block, carry):
        accum, buffer = carry
        key_pos = block * key_span + span_iota
        key_part = span_slice(key_heads, block, 1)
        probs_full, prob_grad, score_grad = tile_grads(
            query_heads,
            key_part,
            span_slice(value_heads, block, 1),
            attn_grad,
            log_total,
            delta,
            positions,
            key_pos,
            lengths,
        )
        probs_again = probs_full.astype(jnp.bfloat16)
        accum = (
            accum
            + jnp.einsum(
                "mhqk,mkhd->mqhd", score_grad, key_part, preferred_element_type=jnp.float32
            )
            * SCALING
        )
        key_term = (
            jnp.einsum(
                "mhqk,mqhd->mkhd", score_grad, query_heads, preferred_element_type=jnp.float32
            )
            * SCALING
        )
        value_term = jnp.einsum(
            "mhqk,mqhd->mkhd", probs_again, attn_grad, preferred_element_type=jnp.float32
        )
        stacked = jnp.stack(
            [
                key_term.reshape(batches, key_span, local_width),
                value_term.reshape(batches, key_span, local_width),
            ],
            axis=2,
        )
        buffer = lax.dynamic_update_slice_in_dim(buffer, stacked, block * key_span, 1)
        return (accum, buffer)

    buffer_zero = jnp.zeros((batches, slot_span, 2, local_width), jnp.float32)
    query_grad, pair_terms = lax.fori_loop(0, block_count, back_step, (query_zero, buffer_zero))
    pair_grad = lax.psum_scatter(pair_terms, "ctx", scatter_dimension=1, tiled=True)
    mixed_grad = jnp.concatenate(
        [query_grad.reshape(batches, block_rows, 1, local_width), pair_grad], axis=2
    )
    later = shifted(mixed_grad[:, :2], "ctx", -1)
    ahead = jnp.concatenate([mixed_grad, later], axis=1)
    pre_grad = (
        conv_kernel[0] * ahead[:, :block_rows]
        + conv_kernel[1] * ahead[:, 1 : block_rows + 1]
        + conv_kernel[2] * ahead[:, 2:]
    ).astype(jnp.bfloat16)
    kernel_grad = jnp.stack(
        [
            jnp.sum(extended[:, 2 - offset : 2 - offset + block_rows] * mixed_grad, axis=(0, 1))
            for offset in range(3)
        ]
    )
    shift_grad = jnp.sum(mixed_grad, axis=(0, 1))
    pre_grad = pre_grad.reshape(all_rows, 3, local_width)
    qkv_wgrad = jnp.einsum("td,tcn->dcn", first_low, pre_grad, preferred_element_type=jnp.float32)
    first_grad = lax.psum(
        jnp.einsum("tcn,dcn->td", pre_grad, qkv_full, preferred_element_type=jnp.float32), "tp"
    )
    gain_one_grad = jnp.sum(first_grad * first_hat, axis=0)
    bias_one_grad = jnp.sum(first_grad, axis=0)
    input_grad = middle_grad + norm_back(first_grad, first_hat, first_recip, ln1_gain)
    input_grad = input_grad.reshape(batches, block_rows, model_width)
    summed = lax.psum(
        (
            qkv_wgrad,
            out_wgrad,
            up_wgrad,
            down_wgrad,
            gain_one_grad,
            bias_one_grad,
            kernel_grad,
            shift_grad,
            gain_two_grad,
            bias_two_grad,
        ),
        ("fsdp", "ctx"),
    )
    share_rows = model_width // lax.axis_size("fsdp")
    owner_start = lax.axis_index("fsdp") * share_rows
    qkv_share = lax.dynamic_slice_in_dim(summed[0], owner_start, share_rows, 0)
    out_share = lax.dynamic_slice_in_dim(summed[1], owner_start, share_rows, 1)
    up_share = lax.dynamic_slice_in_dim(summed[2], owner_start, share_rows, 0)
    down_share = lax.dynamic_slice_in_dim(summed[3], owner_start, share_rows, 1)
    small_sums = summed[4:]
    return (
        result,
        input_grad,
        small_sums[0],
        small_sums[1],
        qkv_share,
        small_sums[2],
        small_sums[3],
        out_share,
        small_sums[4],
        small_sums[5],
        up_share,
        down_share,
    )


def solution(mesh):
    placed = (
        P("fsdp", "ctx", None),
        P("fsdp"),
        P("fsdp", "ctx", None),
        P(),
        P(),
        P("fsdp", None, "tp"),
        P(None, None, "tp"),
        P(None, "tp"),
        P("tp", "fsdp"),
        P(),
        P(),
        P("fsdp", "tp"),
        P("tp", "fsdp"),
    )
    return jax.shard_map(
        local,
        mesh=mesh,
        in_specs=placed,
        out_specs=(
            P("fsdp", "ctx", None),
            P("fsdp", "ctx", None),
            P(),
            P(),
            P("fsdp", None, "tp"),
            P(None, None, "tp"),
            P(None, "tp"),
            P("tp", "fsdp"),
            P(),
            P(),
            P("fsdp", "tp"),
            P("tp", "fsdp"),
        ),
        check_vma=False,
    )
```

profile of v0, /device:TPU:0, one launch (start us, length us, event | category | flops | bytes accessed | tf_op | source)
XLA Modules:
  0.0 906.1 jit_solution(3532479969276561310)
XLA Ops:
  11.3 34.0 %all-gather.5.cloned.1.call-done = bf16[768,3,384]{2,0,1:T(8,128)(2,1)} async-done(((bf16[192,3,384]{2,0,1:T(8,128)(2,1)}), bf16[768,3,384]{2,0,1:T(8,128)(2,1)}) %all-gather.5.cloned.1.call-update) | async-done | bytes 1769488 | tf_op jit(solution)/shard_map/all_gather | solution.py:76
  57.1 11.0 %all_gather.17 = bf16[384,768]{0,1:T(8,128)(2,1)S(1)} all-gather(bf16[384,192]{0,1:T(8,128)(2,1)S(1)} %copy-done.26), channel_id=1, replica_groups=mesh['fsdp'=4,'ctx'=4,'tp'=2] {'fsdp'}, dimensions={1}, use_global_device_ids=true | all-gather | bytes 737280 | tf_op jit(solution)/shard_map/all_gather | solution.py:77
  68.1 53.2 %all-gather.7.cloned.1.call-done = bf16[2,1024,2,384]{1,3,0,2:T(8,128)(2,1)} async-done(((bf16[2,256,2,384]{1,3,0,2:T(8,128)(2,1)}), bf16[2,1024,2,384]{1,3,0,2:T(8,128)(2,1)}) %all-gather.7.cloned.1.call-update) | async-done | bytes 3145744 | tf_op jit(solution)/shard_map/all_gather | solution.py:113
  124.7 6.7 while.48
  132.4 8.3 while.49
  133.1 7.6 fusion.144
  147.9 15.0 %all-reduce.8.cloned.1.call-done = f32[512,768]{1,0:T(8,128)} async-done(((f32[512,768]{1,0:T(8,128)}), f32[512,768]{1,0:T(8,128)}) %all-reduce.8.cloned.1.call-update) | async-done | bytes 1572880 | tf_op jit(solution)/shard_map/psum | solution.py:155
  165.1 38.3 %all-gather.9.cloned.1.call-done = bf16[768,1536]{1,0:T(8,128)(2,1)} async-done(((bf16[192,1536]{1,0:T(8,128)(2,1)}), bf16[768,1536]{1,0:T(8,128)(2,1)}) %all-gather.9.cloned.1.call-update) | async-done | bytes 2359312 | tf_op jit(solution)/shard_map/all_gather | solution.py:78
  203.5 4.8 convolution_maximum_fusion
  208.3 34.5 %all-gather.11.cloned.1.call-done = bf16[1536,768]{0,1:T(8,128)(2,1)} async-done(((bf16[1536,192]{0,1:T(8,128)(2,1)}), bf16[1536,768]{0,1:T(8,128)(2,1)}) %all-gather.11.cloned.1.call-update) | async-done | bytes 2359312 | tf_op jit(solution)/shard_map/all_gather | solution.py:79
  251.3 20.3 %all-reduce.10.cloned.1.call-done = f32[512,768]{1,0:T(8,128)} async-done(((f32[512,768]{1,0:T(8,128)}), f32[512,768]{1,0:T(8,128)}) %all-reduce.10.cloned.1.call-update) | async-done | bytes 1572880 | tf_op jit(solution)/shard_map/psum | solution.py:172
  277.8 14.6 %while.50 = (s32[]{:T(128)}, f32[2,6,256,1]{2,0,1,3:T(2,128)S(1)}, s32[]{:T(128)}, s32[2]{0:T(128)S(1)}, bf16[2,256,6,64]{1,3,2,0:T(8,128)(2,1)S(1)}, /*index=5*...) while((s32[]{:T(128)}, f32[2,6,256,1]{2,0,1,3:T(2,128)S(1)}, ...), condition=%wide.region_17.18_spmd.clone, body=%wide.region_15.17_spmd.clone.sunk | while | flops 821824768 | bytes 37042356 | solution.py:199
  277.8 6.3 fusion.149
  284.8 7.7 multiply_reduce_fusion.10
  296.0 25.8 %while.51 = (s32[]{:T(128)}, f32[2,256,6,64]{1,3,2,0:T(8,128)S(1)}, f32[2,1024,2,384]{1,3,0,2:T(8,128)}, s32[]{:T(128)}, s32[2]{0:T(128)S(1)}, /*index=5*/bf16[2...) while((s32[]{:T(128)}, f32[2,256,6,64]{1,3,2,0:T(8,128)S(1)}, ...), condition=%wide.region_19.20_spmd.clone, body=%wide.region_18.19_spmd.clone.sunk | while | flops 2048265472 | bytes 123263216 | solution.py:245
  296.5 6.3 fusion.160
  303.4 8.4 multiply_convert_fusion.5
  321.9 112.1 %reduce-scatter.2.cloned.1.call-done = f32[2,256,2,384]{1,3,0,2:T(8,128)} async-done(((f32[2,1024,2,384]{1,3,0,2:T(8,128)}), f32[2,256,2,384]{1,3,0,2:T(8,128)}) %reduce-scatter.2.cloned.1.call-update) | async-done | bytes 1572880 | tf_op jit(solution)/shard_map/reduce_scatter | solution.py:246
  437.0 5.3 fusion.66
  446.1 4.6 multiply_reduce_fusion.3
  457.7 5.3 fusion.72
  471.8 10.5 %all-reduce.14.cloned.1.call-done = (f32[512,768]{1,0:T(8,128)}, f32[512,768]{1,0:T(8,128)}) async-done(((f32[512,768]{1,0:T(8,128)}, f32[512,768]{1,0:T(8,128)}), (f32[512,768]{1,0:T(8,128)}, f32[512,768]{1,0:T(8,128)})) %all-reduce.14.cloned.1.call-update) | async-done | bytes 3145744 | tf_op jit(solution)/shard_map/psum | solution.py:162
  484.6 82.0 %all-reduce = (f32[768]{0:T(1024)}, f32[768]{0:T(1024)}, f32[3,3,384]{2,1,0:T(4,128)}, f32[3,384]{1,0:T(4,128)}, f32[768]{0:T(1024)}, /*index=5*/f32[768]{0:T(1024)}) all-reduce(f32[768]{0:T(1024)S(1)} %get-tuple-element.486, f32[768]{0:T(1024)S(1)} %get-tuple-element.492, ...), channel_id=1, replica_groups=mesh['fsdp'=4,'ctx'=4,'tp'=2] {'fsdp','ctx'}, use_global_device_ids=true, to_apply=%region_25.26 | all-reduce | flops 7680 | bytes 61440 | tf_op jit(solution)/shard_map/psum | solution.py:273
  570.9 320.0 %all-reduce.12.cloned.1.call-done = (f32[768,3,384]{2,0,1:T(8,128)}, f32[384,768]{0,1:T(8,128)}, f32[768,1536]{1,0:T(8,128)}, f32[1536,768]{0,1:T(8,128)}) async-done(((f32[768,3,384]{2,0,1:T(8,128)}, f32[384,768]{0,1:T(8,128)}, f32[768,1536]{1,0:T(8,128)}, f32[1536,768]{0,1:T(8,128)}), (f32[768,3,384]{2,0,1:T(8,128)}, f32[384,768]{0,1:T(8,128)}, f32[768,1536]{1,0:T(8,128)}, ...) | async-done | bytes 14155792 | tf_op jit(solution)/shard_map/psum | solution.py:273
  (244 shorter events, 103.2 us)
Async XLA Ops:
  7.2 38.0 %all-gather.5.cloned.1.call-start = ((), (), s32[]{:S(2)}) async-start(), calls=%async_computation.1 | async-start | bytes 2211840 | tf_op jit(solution)/shard_map/all_gather | solution.py:76
  7.9 113.4 %all-gather.7.cloned.1.call-start = ((), (), s32[]{:S(2)}) async-start(), calls=%async_computation.2 | async-start | bytes 3932160 | tf_op jit(solution)/shard_map/all_gather | solution.py:113
  11.3 40.1 %copy-start.43 = (f32[3,3,384]{2,1,0:T(4,128)S(1)}, f32[3,3,384]{2,1,0:T(4,128)}, u32[]{:S(2)}) copy-start(f32[3,3,384]{2,1,0:T(4,128)} %param.27) | copy-start | bytes 41476
  47.9 4.8 collective-permute-start
  56.0 12.1 %copy-start = (bf16[2,256,3,384]{1,3,0,2:T(8,128)(2,1)}, bf16[2,256,3,384]{1,3,0,2:T(8,128)(2,1)S(1)}, u32[]{:S(2)}) copy-start(bf16[2,256,3,384]{1,3,0,2:T(8,128)(2,1)S(1)} %add_convert_fusion) | copy-start | bytes 3538948
  57.0 106.0 %all-reduce.8.cloned.1.call-start = ((), (), s32[]{:S(2)}) async-start(), calls=%async_computation.3 | async-start | bytes 3145728 | tf_op jit(solution)/shard_map/psum | solution.py:155
  68.1 74.3 %copy-start.16 = (bf16[384,768]{0,1:T(8,128)(2,1)}, bf16[384,768]{0,1:T(8,128)(2,1)S(1)}, u32[]{:S(2)}) copy-start(bf16[384,768]{0,1:T(8,128)(2,1)S(1)} %all_gather.17) | copy-start | bytes 1769476
  68.1 56.6 %copy-start.25 = (s32[2]{0:T(128)S(1)}, s32[2]{0:T(128)}, u32[]{:S(2)}) copy-start(s32[2]{0:T(128)} %param.22) | copy-start | bytes 28
  144.2 59.3 %all-gather.9.cloned.1.call-start = ((), (), s32[]{:S(2)}) async-start(), calls=%async_computation.4 | async-start | bytes 2949120 | tf_op jit(solution)/shard_map/all_gather | solution.py:78
  144.8 98.0 %all-gather.11.cloned.1.call-start = ((), (), s32[]{:S(2)}) async-start(), calls=%async_computation.5 | async-start | bytes 2949120 | tf_op jit(solution)/shard_map/all_gather | solution.py:79
  145.4 126.2 %all-reduce.10.cloned.1.call-start = ((), (), s32[]{:S(2)}) async-start(), calls=%async_computation.6 | async-start | bytes 3145728 | tf_op jit(solution)/shard_map/psum | solution.py:172
  164.8 109.6 %copy-start.3 = (f32[512,768]{1,0:T(8,128)}, f32[512,768]{1,0:T(8,128)S(1)}, u32[]{:S(2)}) copy-start(f32[512,768]{1,0:T(8,128)S(1)} %get-tuple-element.584) | copy-start | bytes 4718596
  164.8 38.7 %copy-start.48 = (f32[768]{0:T(1024)S(1)}, f32[768]{0:T(1024)}, u32[]{:S(2)}) copy-start(f32[768]{0:T(1024)} %param.30) | copy-start | bytes 9220
  164.8 109.6 %copy-start.39 = (f32[512]{0:T(512)}, f32[512]{0:T(512)S(1)}, u32[]{:S(2)}) copy-start(f32[512]{0:T(512)S(1)} %broadcast_multiply_fusion.4) | copy-start | bytes 6148
  165.1 109.3 %copy-start.41 = (f32[512]{0:T(512)}, f32[512]{0:T(512)S(1)}, u32[]{:S(2)}) copy-start(f32[512]{0:T(512)S(1)} %add_rsqrt_fusion) | copy-start | bytes 6148
  251.0 183.0 %reduce-scatter.2.cloned.1.call-start = ((), (), s32[]{:S(2)}) async-start(), calls=%async_computation.7 | async-start | bytes 7864320 | tf_op jit(solution)/shard_map/reduce_scatter | solution.py:246
  303.1 10.7 %slice-start = ((s8[12582912]{0:T(1024)(128)(4,1)}), s8[4194304]{0:T(1024)(128)(4,1)S(1)}, s32[]{:S(2)}) async-start(s8[12582912]{0:T(1024)(128)(4,1)} %bitcast.193), calls=%async_computation.10 | async-start | bytes 8388608 | tf_op jit(solution)/shard_map/while
  321.9 160.5 %all-reduce.14.cloned.1.call-start = ((), (), s32[]{:S(2)}) async-start(), calls=%async_computation.9 | async-start | bytes 6291456 | tf_op jit(solution)/shard_map/psum | solution.py:162
  435.6 6.8 collective-permute-start.1
  456.4 434.5 %all-reduce.12.cloned.1.call-start = ((), (), s32[]{:S(2)}) async-start(), calls=%async_computation.8 | async-start | bytes 28311552 | tf_op jit(solution)/shard_map/psum | solution.py:273
  471.8 10.6 %copy-start.36 = (f32[1,2,2,128]{3,1,2,0:T(2,128)S(1)}, f32[1,2,2,128]{3,1,2,0:T(2,128)}, u32[]{:S(2)}) copy-start(f32[1,2,2,128]{3,1,2,0:T(2,128)} %copy-done.35) | copy-start | bytes 6148
  471.8 10.6 %copy-start.38 = (f32[1,2,2,128]{3,1,2,0:T(2,128)S(1)}, f32[1,2,2,128]{3,1,2,0:T(2,128)}, u32[]{:S(2)}) copy-start(f32[1,2,2,128]{3,1,2,0:T(2,128)} %copy-done.37) | copy-start | bytes 6148
  471.8 12.8 %copy-start.44 = (f32[768]{0:T(1024)S(1)}, f32[768]{0:T(1024)}, u32[]{:S(2)}) copy-start(f32[768]{0:T(1024)} %get-tuple-element.484) | copy-start | bytes 9220
  471.8 12.7 %copy-start.45 = (f32[768]{0:T(1024)S(1)}, f32[768]{0:T(1024)}, u32[]{:S(2)}) copy-start(f32[768]{0:T(1024)} %get-tuple-element.491) | copy-start | bytes 9220
  (50 other events, 142.5 us)
Sparse Core Ops, SparseCore 0:
  9.9 35.2 all-gather.4
  57.1 64.2 all-gather.6
  144.3 18.5 all-reduce.7
  164.8 38.6 all-gather.8
  205.3 37.4 all-gather.10
  251.1 20.4 all-reduce.9
  322.0 111.9 reduce-scatter.1
  456.5 25.8 all-reduce.13
  490.5 400.3 all-reduce.11
where the time goes:
time: 914 us; the launch traced here: 906 us
  waiting for transfers between devices  640 us (70%)
  blocking collectives  93 us (10%)
  matrix products  85.2 us (9%)
  other arithmetic  36.6 us (4%)
  local copies, waits for them, and re-layouts  29.8 us (3%)
  between operations  14.8 us (2%)
    psum x1, waiting for transfers between devices, local(): lax.psum((qkv_wgrad, out_wgrad, up_wgrad, down_wgrad, gain_one_grad, bias...  320 us
    reduce_scatter x1, waiting for transfers between devices, local(): lax.psum_scatter(pair_terms, 'ctx', scatter_dimension=1, tiled=True)  112 us
    psum x1, blocking collectives, local(): lax.psum((qkv_wgrad, out_wgrad, up_wgrad, down_wgrad, gain_one_grad, bias...  82 us
    all_gather x1, waiting for transfers between devices, local(): whole_pairs = lax.all_gather(own_pairs, 'ctx', axis=1, tiled=True)  53.2 us
    all_gather x1, waiting for transfers between devices, local(): lax.all_gather(up_weight, 'fsdp', axis=0, tiled=True)  38.3 us
    all_gather x1, waiting for transfers between devices, local(): lax.all_gather(down_weight, 'fsdp', axis=1, tiled=True)  34.5 us
    all_gather x1, waiting for transfers between devices, local(): lax.all_gather(qkv_weight, 'fsdp', axis=0, tiled=True)  34 us
    psum x1, waiting for transfers between devices, local(): lax.psum(jnp.einsum('tf,df->td', up_grad_low, up_full_w, preferred_elemen...  20.3 us
  transfers between devices with their start and end apart: 11, of which 10 were waited for; matrix products, arithmetic and copies ran while one was open for 4% of the time, Pallas kernels for 0%

commit v1 on v0

--- a/solution.py
+++ b/solution.py
@@ -1,6 +1,8 @@
 import jax
 import jax.numpy as jnp
 from jax import lax
+from jax.experimental import pallas as pl
+from jax.experimental.pallas import tpu as pltpu
 from jax.sharding import PartitionSpec as P
 
 HD = 64
@@ -9,6 +11,322 @@
 EPSILON = 1e-05
 SCALING = 0.125
 MASKED = -1e30
+
+
+BF = jnp.bfloat16
+F32 = jnp.float32
+MESH = pl.DeviceIdType.MESH
+ANY = pl.BlockSpec(memory_space=pl.ANY)
+VMEM = pl.BlockSpec(memory_space=pltpu.VMEM)
+SMEM = pl.BlockSpec(memory_space=pltpu.SMEM)
+
+
+def mm(left, right, left_dim, right_dim):
+    return lax.dot_general(
+        left, right, (((left_dim,), (right_dim,)), ((), ())), preferred_element_type=F32
+    )
+
+
+def remote(source, target, send_sem, recv_sem, device):
+    return pltpu.make_async_remote_copy(
+        src_ref=source,
+        dst_ref=target,
+        send_sem=send_sem,
+        recv_sem=recv_sem,
+        device_id=device,
+        device_id_type=MESH,
+    )
+
+
+def place():
+    f, c, t = lax.axis_index("fsdp"), lax.axis_index("ctx"), lax.axis_index("tp")
+    fx = f + 1 - 2 * lax.rem(f, 2)
+    fy = lax.rem(f + 2, 4)
+    fd = lax.rem(fx + 2, 4)
+    return f, c, t, fx, fy, fd
+
+
+def greet(peers):
+    barrier = pltpu.get_barrier_semaphore()
+    for peer in peers:
+        pl.semaphore_signal(barrier, inc=1, device_id=peer, device_id_type=MESH)
+    pl.semaphore_wait(barrier, len(peers))
+
+
+def norm_rows(x, gain, bias):
+    centred = x - jnp.mean(x, axis=-1, keepdims=True)
+    recip = lax.rsqrt(jnp.mean(centred * centred, axis=-1, keepdims=True) + EPSILON)
+    normed = centred * recip
+    return normed * gain + bias, normed, recip
+
+
+def forward_kernel(
+    lens, tok, wq3, wo, wu, wd, gain, bias, taps3, shift3,
+    wq_all, wo_all, wu_all, wd_all, attn, heads, pre_all, first_all,
+    tok_buf, wq_buf, wq, taps, shift, att, prev,
+    own_sem, tok_send, tok_recv, pass_send, pass_recv, w_send, w_recv, att_send, att_recv,
+):
+    f, c, t, fx, fy, fd = place()
+    slot = lax.div(c, 2)
+    other = 1 - t
+    ctx_peers = [lax.rem(c + d, 4) for d in (1, 2, 3)]
+    greet(
+        [(fx, c, t), (fy, c, t), (f, c, other)] + [(f, p, t) for p in ctx_peers]
+    )
+    half_rows = tok.shape[1] // 2
+    mine = pl.ds(pl.multiple_of(t * half_rows, half_rows), half_rows)
+    theirs = pl.ds(pl.multiple_of(other * half_rows, half_rows), half_rows)
+
+    shards = [wq, wo, wu, wd]
+    wholes = [wq_all, wo_all, wu_all, wd_all]
+
+    def direct(w, kind):
+        target = (fx, c, t) if kind == 0 else (fy, c, t)
+        return remote(shards[w], wholes[w].at[f], w_send.at[w, kind], w_recv.at[w, kind], target)
+
+    def part(w, kind):
+        rows = wholes[w].shape[1] // 2
+        return pl.ds(0, rows) if kind == 2 else pl.ds(rows, rows)
+
+    def relay(w, kind):
+        origin, target = (fx, (fy, c, t)) if kind == 2 else (fy, (fx, c, t))
+        view = wholes[w].at[origin, part(w, kind)]
+        return remote(view, view, w_send.at[w, kind], w_recv.at[w, kind], target)
+
+    def landed(w, kind):
+        if kind < 2:
+            view = wholes[w].at[fx if kind == 0 else fy]
+        else:
+            view = wholes[w].at[fd, part(w, kind)]
+        remote(view, view, w_send.at[w, kind], w_recv.at[w, kind], (f, c, other)).wait_recv()
+
+    def send_direct(w):
+        direct(w, 0).start()
+        direct(w, 1).start()
+
+    def pass_on(w):
+        landed(w, 0)
+        relay(w, 2).start()
+        landed(w, 1)
+        relay(w, 3).start()
+
+    def tok_copy(d):
+        target = lax.rem(c + d, 4)
+        return remote(
+            tok.at[lax.div(target, 2), mine],
+            tok_buf.at[c, mine],
+            tok_send.at[d],
+            tok_recv.at[d],
+            (f, target, t),
+        )
+
+    def tok_pass(source, d):
+        view = tok_buf.at[source, mine]
+        return remote(view, view, pass_send.at[d], pass_recv.at[d], (f, c, other))
+
+    for d in (1, 2, 3):
+        tok_copy(d).start()
+    load_wq = pltpu.make_async_copy(wq3, wq_buf, own_sem.at[0])
+    load_wq.start()
+    load_tok = pltpu.make_async_copy(tok.at[slot], tok_buf.at[c], own_sem.at[1])
+    load_tok.start()
+    keep = [
+        pltpu.make_async_copy(shards[w], wholes[w].at[f], own_sem.at[2 + w]) for w in range(4)
+    ]
+    for w in range(1, 4):
+        keep[w].start()
+    load_wq.wait()
+    part_width = wq_buf.shape[2] // 2
+    for half in (0, 1):
+
+        @pl.when(lax.rem(c, 2) == half)
+        def _():
+            lanes = slice(half * part_width, (half + 1) * part_width)
+            for kind in range(3):
+                target = slice(kind * part_width, (kind + 1) * part_width)
+                wq[:, target] = wq_buf[kind, :, lanes]
+                shift[0:1, target] = shift3[kind : kind + 1, lanes]
+                for tap in range(3):
+                    taps[tap : tap + 1, target] = taps3[tap, kind : kind + 1, lanes]
+
+    send_direct(0)
+    send_direct(1)
+    keep[0].start()
+
+    def first_norm(block):
+        out, _, _ = norm_rows(tok_buf[block].astype(F32), gain[...], bias[...])
+        first_all[block] = out.astype(BF)
+
+    load_tok.wait()
+    first_norm(c)
+
+    pass_on(0)
+    send_direct(2)
+
+    end = lax.div(c, 3)
+    start = lax.div(3 - c, 3)
+    d_near = 1 + 2 * start
+    d_mid = 3 - start - end
+    d_far = 2 - start + end
+    for d in (d_near, d_mid, d_far):
+        source = lax.rem(c - d + 4, 4)
+        view = tok_buf.at[source, mine]
+        remote(view, view, tok_send.at[d], tok_recv.at[d], (f, c, other)).wait_recv()
+        tok_pass(source, d).start()
+        view = tok_buf.at[source, theirs]
+        remote(view, view, pass_send.at[d], pass_recv.at[d], (f, c, other)).wait_recv()
+        first_norm(source)
+
+    keep[0].wait()
+    landed(0, 2)
+    landed(0, 3)
+    prev[...] = jnp.zeros_like(prev)
+    width = wq_all.shape[2]
+
+    def project(block, carry):
+        weights = wq_all[...].reshape(-1, width)
+        pre = mm(first_all[block], weights, 1, 0).astype(BF)
+        pre_all[block] = pre
+        pre = pre.astype(F32)
+        joined = jnp.concatenate([prev[...], pre], axis=0)
+        prev[...] = pre[-8:]
+        out = (
+            shift[0:1]
+            + taps[0:1] * pre
+            + taps[1:2] * pltpu.roll(joined, 1, 0)[8:]
+            + taps[2:3] * pltpu.roll(joined, 2, 0)[8:]
+        ).astype(BF)
+        rows = pre.shape[0]
+        at = pl.ds(pl.multiple_of(block * rows, rows), rows)
+        for head in range(width // HD):
+            piece = out[:, head * HD : (head + 1) * HD]
+            if head < width // HD // 3:
+                piece = (piece.astype(F32) * SCALING).astype(BF)
+            heads[head, at, :] = piece
+        return carry
+
+    blocks = tok_buf.shape[0]
+    block_rows = tok_buf.shape[1]
+    lax.fori_loop(0, blocks, project, 0)
+    pass_on(1)
+    send_direct(3)
+
+    count = width // HD // 3
+    length = lens[slot]
+    tile = 128
+    tiles = block_rows // tile
+
+    def att_copy(block):
+        return remote(
+            att.at[block],
+            attn.at[c],
+            att_send.at[block],
+            att_recv.at[lax.rem(block - c + 4, 4)],
+            (f, block, t),
+        )
+
+    for block in reversed(range(blocks)):
+        keys = (block + 1) * block_rows
+
+        def attend(n, carry, block=block, keys=keys):
+            head, piece = lax.div(n, tiles), lax.rem(n, tiles)
+            at = pl.multiple_of(block * block_rows + piece * tile, tile)
+            scores = mm(heads[head, pl.ds(at, tile), :], heads[count + head, 0:keys, :], 1, 1)
+            col = lax.broadcasted_iota(jnp.int32, scores.shape, 1)
+            row = at + lax.broadcasted_iota(jnp.int32, (tile, 1), 0)
+            scores = jnp.where(col < jnp.minimum(row + 1, length), scores, MASKED)
+            powers = jnp.exp(scores - jnp.max(scores, axis=-1, keepdims=True))
+            probs = powers * (1.0 / jnp.sum(powers, axis=-1, keepdims=True))
+            out = mm(probs.astype(BF), heads[2 * count + head, 0:keys, :], 1, 0)
+            att[
+                block,
+                pl.ds(pl.multiple_of(head * HD, HD), HD),
+                pl.ds(pl.multiple_of(piece * tile, tile), tile),
+            ] = out.T.astype(BF)
+            return carry
+
+        lax.fori_loop(0, count * tiles, attend, 0)
+
+        @pl.when(block != c)
+        def _():
+            att_copy(block).start()
+
+        if block == blocks - 1:
+            pass_on(2)
+
+    pass_on(3)
+    own = pltpu.make_async_copy(att.at[c], attn.at[c], own_sem.at[6])
+    own.start()
+    own.wait()
+    for d in (1, 2, 3):
+        source = lax.rem(c - d + 4, 4)
+        remote(
+            attn.at[source], attn.at[source], att_send.at[0], att_recv.at[d], (f, c, other)
+        ).wait_recv()
+        tok_copy(d).wait_send()
+        tok_pass(lax.rem(c - d + 4, 4), d).wait_send()
+    for block in range(blocks):
+
+        @pl.when(block != c)
+        def _():
+            att_copy(block).wait_send()
+
+    for w in range(4):
+        if w:
+            landed(w, 2)
+            landed(w, 3)
+            keep[w].wait()
+        direct(w, 0).wait_send()
+        direct(w, 1).wait_send()
+        relay(w, 2).wait_send()
+        relay(w, 3).wait_send()
+
+
+def forward_call(lens, tok, wq3, wo, wu, wd, gain, bias, taps3, shift3):
+    slots, block_rows, model = tok.shape
+    blocks = 4
+    rows, width = wq3.shape[1], 3 * (wq3.shape[2] // 2)
+    dma = pltpu.SemaphoreType.DMA
+
+    def whole(shard):
+        return jax.ShapeDtypeStruct((4,) + shard, BF)
+
+    attn_width = width // 3
+    return pl.pallas_call(
+        forward_kernel,
+        name="forward",
+        out_shape=[
+            whole((rows, width)),
+            whole(wo.shape),
+            whole(wu.shape),
+            whole(wd.shape),
+            whole((attn_width, block_rows)),
+            jax.ShapeDtypeStruct((width // HD, blocks * block_rows, HD), BF),
+            whole((block_rows, width)),
+            whole((block_rows, model)),
+        ],
+        in_specs=[SMEM, ANY, ANY, ANY, ANY, ANY, VMEM, VMEM, VMEM, VMEM],
+        out_specs=[VMEM, ANY, ANY, ANY, ANY, VMEM, VMEM, VMEM],
+        scratch_shapes=[
+            pltpu.VMEM((blocks, block_rows, model), BF),
+            pltpu.VMEM(wq3.shape, BF),
+            pltpu.VMEM((rows, width), BF),
+            pltpu.VMEM((8, width), F32),
+            pltpu.VMEM((8, width), F32),
+            pltpu.VMEM((blocks, attn_width, block_rows), BF),
+            pltpu.VMEM((8, width), F32),
+            dma((7,)),
+            dma((4,)),
+            dma((4,)),
+            dma((4,)),
+            dma((4,)),
+            dma((4, 4)),
+            dma((4, 4)),
+            dma((4,)),
+            dma((4,)),
+        ],
+        compiler_params=pltpu.CompilerParams(collective_id=0, has_side_effects=True),
+    )(lens, tok, wq3, wo, wu, wd, gain, bias, taps3, shift3)
 
 
 def shifted(block, axis, distance):
@@ -308,6 +626,246 @@
     )
 
 
+def local_fast(
+    tokens,
+    lengths,
+    cotangent,
+    ln1_gain,
+    ln1_bias,
+    qkv_weight,
+    conv_kernel,
+    conv_bias,
+    out_weight,
+    ln2_gain,
+    ln2_bias,
+    up_weight,
+    down_weight,
+):
+    batches, block_rows, model_width = tokens.shape
+    all_rows = batches * block_rows
+    gathered = forward_call(
+        lengths, tokens, qkv_weight.transpose(1, 0, 2), out_weight.T, up_weight, down_weight.T,
+        ln1_gain[None], ln1_bias[None], conv_kernel, conv_bias,
+    )
+    qkv_full = lax.all_gather(qkv_weight, "fsdp", axis=0, tiled=True)
+    out_full = gathered[1].reshape(model_width, -1).T
+    up_full_w = gathered[2].reshape(model_width, -1)
+    down_full_w = gathered[3].reshape(model_width, -1).T
+    local_width = qkv_full.shape[2]
+    local_heads = local_width // HD
+    ctx_count = lax.axis_size("ctx")
+    slot_span = block_rows * ctx_count
+    group_blocks = 4
+    key_span = block_rows * group_blocks
+    ctx_index = lax.axis_index("ctx")
+    positions = ctx_index * block_rows + jnp.arange(block_rows, dtype=jnp.int32)
+    span_iota = jnp.arange(key_span, dtype=jnp.int32)
+    block_count = (ctx_index * block_rows + block_rows + key_span - 1) // key_span
+    token_valid = positions[None, :] < lengths[:, None]
+
+    def span_slice(array_data, block, axis_pos):
+        return lax.dynamic_slice_in_dim(array_data, block * key_span, key_span, axis_pos)
+
+    inputs = tokens.astype(jnp.float32).reshape(all_rows, model_width)
+    first_out, first_hat, first_recip = layer_norm(inputs, ln1_gain, ln1_bias)
+    first_low = first_out.astype(jnp.bfloat16)
+    pre_low = jnp.einsum(
+        "td,dcn->tcn", first_low, qkv_full, preferred_element_type=jnp.float32
+    ).astype(jnp.bfloat16)
+    pre_low = pre_low.reshape(batches, block_rows, 3, local_width)
+    earlier = shifted(pre_low[:, block_rows - 2 :], "ctx", 1)
+    extended = jnp.concatenate([earlier, pre_low], axis=1).astype(jnp.float32)
+    conv_out = (
+        conv_bias
+        + conv_kernel[0] * extended[:, 2:]
+        + conv_kernel[1] * extended[:, 1:-1]
+        + conv_kernel[2] * extended[:, :-2]
+    ).astype(jnp.bfloat16)
+    query_heads = conv_out[:, :, 0].reshape(batches, block_rows, local_heads, HD)
+    own_pairs = conv_out[:, :, 1:]
+    whole_pairs = lax.all_gather(own_pairs, "ctx", axis=1, tiled=True)
+    key_heads = whole_pairs[:, :, 0].reshape(batches, slot_span, local_heads, HD)
+    value_heads = whole_pairs[:, :, 1].reshape(batches, slot_span, local_heads, HD)
+
+    def stat_step(block, carry):
+        row_max, total = carry
+        key_pos = block * key_span + span_iota
+        scores = tile_scores(
+            query_heads, span_slice(key_heads, block, 1), positions, key_pos, lengths
+        )
+        new_max = jnp.maximum(row_max, jnp.max(scores, axis=-1, keepdims=True))
+        total = total * jnp.exp(row_max - new_max) + jnp.sum(
+            jnp.exp(scores - new_max), axis=-1, keepdims=True
+        )
+        return (new_max, total)
+
+    stat_shape = (batches, local_heads, block_rows, 1)
+    row_max, total = lax.fori_loop(
+        0,
+        block_count,
+        stat_step,
+        (jnp.full(stat_shape, MASKED, jnp.float32), jnp.zeros(stat_shape, jnp.float32)),
+    )
+    log_total = row_max + jnp.log(total)
+
+    attn_low = gathered[4].reshape(batches, local_width, block_rows)
+    attn_low = attn_low.transpose(0, 2, 1).reshape(all_rows, local_width)
+    attn_out = lax.psum(jnp.dot(attn_low, out_full, preferred_element_type=jnp.float32), "tp")
+    middle = inputs + attn_out
+    second_out, second_hat, second_recip = layer_norm(middle, ln2_gain, ln2_bias)
+    second_low = second_out.astype(jnp.bfloat16)
+    up_full = jnp.dot(second_low, up_full_w, preferred_element_type=jnp.float32)
+    rectified = jnp.maximum(up_full, 0.0)
+    act_low = (rectified * rectified).astype(jnp.bfloat16)
+    ffn_out = lax.psum(jnp.dot(act_low, down_full_w, preferred_element_type=jnp.float32), "tp")
+    result = (middle + ffn_out).reshape(batches, block_rows, model_width).astype(jnp.bfloat16)
+    grad_out = (
+        cotangent.astype(jnp.float32) * token_valid[:, :, None].astype(jnp.float32)
+    ).reshape(all_rows, model_width)
+    grad_low = grad_out.astype(jnp.bfloat16)
+    down_wgrad = jnp.einsum("tf,td->fd", act_low, grad_low, preferred_element_type=jnp.float32)
+    act_grad = jnp.einsum("td,fd->tf", grad_low, down_full_w, preferred_element_type=jnp.float32)
+    up_grad_low = (act_grad * 2.0 * rectified).astype(jnp.bfloat16)
+    up_wgrad = jnp.einsum("td,tf->df", second_low, up_grad_low, preferred_element_type=jnp.float32)
+    second_grad = lax.psum(
+        jnp.einsum("tf,df->td", up_grad_low, up_full_w, preferred_element_type=jnp.float32), "tp"
+    )
+    gain_two_grad = jnp.sum(second_grad * second_hat, axis=0)
+    bias_two_grad = jnp.sum(second_grad, axis=0)
+    middle_grad = grad_out + norm_back(second_grad, second_hat, second_recip, ln2_gain)
+    middle_low = middle_grad.astype(jnp.bfloat16)
+    out_wgrad = jnp.einsum("tn,td->nd", attn_low, middle_low, preferred_element_type=jnp.float32)
+    attn_flat = jnp.einsum(
+        "td,nd->tn", middle_low, out_full, preferred_element_type=jnp.float32
+    ).astype(jnp.bfloat16)
+    attn_grad = attn_flat.reshape(batches, block_rows, local_heads, HD)
+
+    def delta_step(block, accum):
+        key_pos = block * key_span + span_iota
+        probs_full = jnp.exp(
+            tile_scores(query_heads, span_slice(key_heads, block, 1), positions, key_pos, lengths)
+            - log_total
+        )
+        prob_grad = jnp.einsum(
+            "mqhd,mkhd->mhqk",
+            attn_grad,
+            span_slice(value_heads, block, 1),
+            preferred_element_type=jnp.float32,
+        )
+        return accum + jnp.sum(probs_full * prob_grad, axis=-1, keepdims=True)
+
+    delta = lax.fori_loop(0, block_count, delta_step, jnp.zeros(stat_shape, jnp.float32))
+    query_zero = jnp.zeros((batches, block_rows, local_heads, HD), jnp.float32)
+
+    def back_step(block, carry):
+        accum, buffer = carry
+        key_pos = block * key_span + span_iota
+        key_part = span_slice(key_heads, block, 1)
+        probs_full, prob_grad, score_grad = tile_grads(
+            query_heads,
+            key_part,
+            span_slice(value_heads, block, 1),
+            attn_grad,
+            log_total,
+            delta,
+            positions,
+            key_pos,
+            lengths,
+        )
+        probs_again = probs_full.astype(jnp.bfloat16)
+        accum = (
+            accum
+            + jnp.einsum(
+                "mhqk,mkhd->mqhd", score_grad, key_part, preferred_element_type=jnp.float32
+            )
+            * SCALING
+        )
+        key_term = (
+            jnp.einsum(
+                "mhqk,mqhd->mkhd", score_grad, query_heads, preferred_element_type=jnp.float32
+            )
+            * SCALING
+        )
+        value_term = jnp.einsum(
+            "mhqk,mqhd->mkhd", probs_again, attn_grad, preferred_element_type=jnp.float32
+        )
+        stacked = jnp.stack(
+            [
+                key_term.reshape(batches, key_span, local_width),
+                value_term.reshape(batches, key_span, local_width),
+            ],
+            axis=2,
+        )
+        buffer = lax.dynamic_update_slice_in_dim(buffer, stacked, block * key_span, 1)
+        return (accum, buffer)
+
+    buffer_zero = jnp.zeros((batches, slot_span, 2, local_width), jnp.float32)
+    query_grad, pair_terms = lax.fori_loop(0, block_count, back_step, (query_zero, buffer_zero))
+    pair_grad = lax.psum_scatter(pair_terms, "ctx", scatter_dimension=1, tiled=True)
+    mixed_grad = jnp.concatenate(
+        [query_grad.reshape(batches, block_rows, 1, local_width), pair_grad], axis=2
+    )
+    later = shifted(mixed_grad[:, :2], "ctx", -1)
+    ahead = jnp.concatenate([mixed_grad, later], axis=1)
+    pre_grad = (
+        conv_kernel[0] * ahead[:, :block_rows]
+        + conv_kernel[1] * ahead[:, 1 : block_rows + 1]
+        + conv_kernel[2] * ahead[:, 2:]
+    ).astype(jnp.bfloat16)
+    kernel_grad = jnp.stack(
+        [
+            jnp.sum(extended[:, 2 - offset : 2 - offset + block_rows] * mixed_grad, axis=(0, 1))
+            for offset in range(3)
+        ]
+    )
+    shift_grad = jnp.sum(mixed_grad, axis=(0, 1))
+    pre_grad = pre_grad.reshape(all_rows, 3, local_width)
+    qkv_wgrad = jnp.einsum("td,tcn->dcn", first_low, pre_grad, preferred_element_type=jnp.float32)
+    first_grad = lax.psum(
+        jnp.einsum("tcn,dcn->td", pre_grad, qkv_full, preferred_element_type=jnp.float32), "tp"
+    )
+    gain_one_grad = jnp.sum(first_grad * first_hat, axis=0)
+    bias_one_grad = jnp.sum(first_grad, axis=0)
+    input_grad = middle_grad + norm_back(first_grad, first_hat, first_recip, ln1_gain)
+    input_grad = input_grad.reshape(batches, block_rows, model_width)
+    summed = lax.psum(
+        (
+            qkv_wgrad,
+            out_wgrad,
+            up_wgrad,
+            down_wgrad,
+            gain_one_grad,
+            bias_one_grad,
+            kernel_grad,
+            shift_grad,
+            gain_two_grad,
+            bias_two_grad,
+        ),
+        ("fsdp", "ctx"),
+    )
+    share_rows = model_width // lax.axis_size("fsdp")
+    owner_start = lax.axis_index("fsdp") * share_rows
+    qkv_share = lax.dynamic_slice_in_dim(summed[0], owner_start, share_rows, 0)
+    out_share = lax.dynamic_slice_in_dim(summed[1], owner_start, share_rows, 1)
+    up_share = lax.dynamic_slice_in_dim(summed[2], owner_start, share_rows, 0)
+    down_share = lax.dynamic_slice_in_dim(summed[3], owner_start, share_rows, 1)
+    small_sums = summed[4:]
+    return (
+        result,
+        input_grad,
+        small_sums[0],
+        small_sums[1],
+        qkv_share,
+        small_sums[2],
+        small_sums[3],
+        out_share,
+        small_sums[4],
+        small_sums[5],
+        up_share,
+        down_share,
+    )
+
+
 def solution(mesh):
     placed = (
         P("fsdp", "ctx", None),
@@ -324,8 +882,9 @@
         P("fsdp", "tp"),
         P("tp", "fsdp"),
     )
+    ctx, fsdp, tp = mesh.shape["ctx"], mesh.shape["fsdp"], mesh.shape["tp"]
     return jax.shard_map(
-        local,
+        local_fast if (fsdp, ctx, tp) == (4, 4, 2) else local,
         mesh=mesh,
         in_specs=placed,
         out_specs=(

time: 914 us -> 820 us (0.90)
  waiting for transfers between devices: 640 us -> 515 us
  Pallas kernels: 0 us -> 62.8 us
  matrix products: 85.2 us -> 57.3 us
  blocking collectives: 93 us -> 82.4 us
    all_gather x4 -> x2, waiting for transfers between devices: 160 us -> 56 us  [the longest x1 52 us: local_fast(): whole_pairs = lax.all_gather(own_pairs, 'ctx', axis=1, tiled=True)]
    pallas_call x0 -> x1, Pallas kernels: none -> 62.8 us  [forward_call(): pl.pallas_call(forward_kernel, name='forward', out_shape=[whole((rows, wi...]
    psum x4, waiting for transfers between devices: 366 us -> 349 us  [the longest x1 319 us: local_fast(): lax.psum((qkv_wgrad, out_wgrad, up_wgrad, down_wgrad, gain_one_grad, bias...]
    dot_general x13 -> x12, matrix products: 47.4 us -> 33.3 us  [the longest x1 5.32 us: local_fast(): jnp.dot(act_low, down_full_w, preferred_element_type=jnp.float32)]
    all_gather x1 -> x0, blocking collectives: 11 us -> none  [local(): lax.all_gather(out_weight, 'fsdp', axis=1, tiled=True)]
  transfers between devices with their start and end apart: 11 -> 9, of which waited for: 10 -> 7; matrix products, arithmetic and copies ran while one was open for 4% -> 6% of each run, Pallas kernels for 0% -> 0%
where the time goes in v1:
time: 820 us; the launch traced here: 812 us
  waiting for transfers between devices  515 us (63%)
  blocking collectives  82.4 us (10%)
  Pallas kernels  62.8 us (8%)
  matrix products  57.3 us (7%)
  other arithmetic  36.9 us (4%)
  local copies, waits for them, and re-layouts  35.1 us (4%)
  between operations  16.7 us (2%)
    psum x1, waiting for transfers between devices, local_fast(): lax.psum((qkv_wgrad, out_wgrad, up_wgrad, down_wgrad, gain_one_grad, bias...  319 us
    reduce_scatter x1, waiting for transfers between devices, local_fast(): lax.psum_scatter(pair_terms, 'ctx', scatter_dimension=1, tiled=True)  109 us
    psum x1, blocking collectives, local_fast(): lax.psum((qkv_wgrad, out_wgrad, up_wgrad, down_wgrad, gain_one_grad, bias...  82.4 us
    pallas_call x1, Pallas kernels, forward_call(): pl.pallas_call(forward_kernel, name='forward', out_shape=[whole((rows, wi...  62.8 us
    all_gather x1, waiting for transfers between devices, local_fast(): whole_pairs = lax.all_gather(own_pairs, 'ctx', axis=1, tiled=True)  52 us
  transfers between devices with their start and end apart: 9, of which 7 were waited for; matrix products, arithmetic and copies ran while one was open for 6% of the time, Pallas kernels for 0%

profile of v1, /device:TPU:0, one launch (start us, length us, event | category | flops | bytes accessed | tf_op | source)
XLA Modules:
  0.0 811.8 jit_solution(13987985629408520069)
XLA Ops:
  10.6 62.8 %forward.1 = (bf16[4,192,576]{2,1,0:T(8,128)(2,1)}, bf16[4,192,384]{2,1,0:T(8,128)(2,1)}, bf16[4,192,1536]{2,1,0:T(8,128)(2,1)}, bf16[4,192,1536]{2,1,0:T(8,128)...) custom-call(s32[2]{0:T(128)} %lens.1, ...), custom_call_target="tpu_custom_call" | custom-call | tf_op jit(solution)/shard_map/forward/pallas_call | solution.py:295
  81.7 14.7 %all-reduce.8.cloned.1.call-done = f32[512,768]{1,0:T(8,128)} async-done(((f32[512,768]{1,0:T(8,128)}), f32[512,768]{1,0:T(8,128)}) %all-reduce.8.cloned.1.call-update) | async-done | bytes 1572880 | tf_op jit(solution)/shard_map/psum | solution.py:713
  106.6 4.0 all-gather.3.cloned.1.call-done
  113.3 3.6 collective-permute-start
  123.1 5.1 all-reduce.10.cloned.1.call-done
  134.6 52.0 %all-gather.5.cloned.1.call-done = bf16[2,1024,2,384]{1,3,0,2:T(8,128)(2,1)} async-done(((bf16[2,256,2,384]{1,3,0,2:T(8,128)(2,1)}), bf16[2,1024,2,384]{1,3,0,2:T(8,128)(2,1)}) %all-gather.5.cloned.1.call-update) | async-done | bytes 3145744 | tf_op jit(solution)/shard_map/all_gather | solution.py:686
  189.5 7.9 while.37
  193.2 3.6 exponential_reduce_fusion.2
  198.8 7.8 while.38
  201.9 4.7 multiply_reduce_fusion.10
  208.5 3.4 broadcast_in_dim.65
  212.0 19.1 %while.39 = (s32[]{:T(128)}, f32[2,256,6,64]{1,3,2,0:T(8,128)S(1)}, f32[2,1024,2,384]{1,3,0,2:T(8,128)}, s32[]{:T(128)}, s32[2]{0:T(128)S(1)}, /*index=5*/bf16[2...) while((s32[]{:T(128)}, f32[2,256,6,64]{1,3,2,0:T(8,128)S(1)}, ...), condition=%wide.region_17.18_spmd.clone, body=%wide.region_16.17_spmd.clone.sunk | while | flops 2048265472 | bytes 87087288 | solution.py:803
  214.6 3.4 fusion.140
  218.1 6.5 multiply_convert_fusion.5
  227.8 3.2 pad_maximum_fusion.5
  231.1 108.9 %reduce-scatter.2.cloned.1.call-done = f32[2,256,2,384]{1,3,0,2:T(8,128)} async-done(((f32[2,1024,2,384]{1,3,0,2:T(8,128)}), f32[2,256,2,384]{1,3,0,2:T(8,128)}) %reduce-scatter.2.cloned.1.call-update) | async-done | bytes 1572880 | tf_op jit(solution)/shard_map/reduce_scatter | solution.py:804
  343.2 5.3 fusion.54
  352.3 4.6 multiply_reduce_fusion.3
  363.0 5.3 fusion.61
  368.4 3.6 fusion.53
  373.7 3.4 convolution_bitcast_fusion
  377.2 10.0 %all-reduce.14.cloned.1.call-done = (f32[512,768]{1,0:T(8,128)}, f32[512,768]{1,0:T(8,128)}) async-done(((f32[512,768]{1,0:T(8,128)}, f32[512,768]{1,0:T(8,128)}), (f32[512,768]{1,0:T(8,128)}, f32[512,768]{1,0:T(8,128)})) %all-reduce.14.cloned.1.call-update) | async-done | bytes 3145744 | tf_op jit(solution)/shard_map/psum | solution.py:720
  389.4 82.4 %all-reduce = (f32[768]{0:T(1024)}, f32[768]{0:T(1024)}, f32[3,3,384]{2,1,0:T(4,128)}, f32[3,384]{1,0:T(4,128)}, f32[768]{0:T(1024)}, /*index=5*/f32[768]{0:T(1024)}) all-reduce(f32[768]{0:T(1024)S(1)} %get-tuple-element.399, f32[768]{0:T(1024)S(1)} %get-tuple-element.405, ...), channel_id=1, replica_groups=mesh['fsdp'=4,'ctx'=4,'tp'=2] {'fsdp','ctx'}, use_global_device_ids=true, to_apply=%region_23.24 | all-reduce | flops 7680 | bytes 61440 | tf_op jit(solution)/shard_map/psum | solution.py:831
  476.1 319.3 %all-reduce.12.cloned.1.call-done = (f32[768,3,384]{2,0,1:T(8,128)}, f32[384,768]{0,1:T(8,128)}, f32[768,1536]{1,0:T(8,128)}, f32[1536,768]{0,1:T(8,128)}) async-done(((f32[768,3,384]{2,0,1:T(8,128)}, f32[384,768]{0,1:T(8,128)}, f32[768,1536]{1,0:T(8,128)}, f32[1536,768]{0,1:T(8,128)}), (f32[768,3,384]{2,0,1:T(8,128)}, f32[384,768]{0,1:T(8,128)}, f32[768,1536]{1,0:T(8,128)}, ...) | async-done | bytes 14155792 | tf_op jit(solution)/shard_map/psum | solution.py:831
  (238 shorter events, 84.6 us)
Async XLA Ops:
  8.0 88.3 %all-reduce.8.cloned.1.call-start = ((), (), s32[]{:S(2)}) async-start(), calls=%async_computation.1 | async-start | bytes 3145728 | tf_op jit(solution)/shard_map/psum | solution.py:713
  77.6 32.9 %all-gather.3.cloned.1.call-start = ((), (), s32[]{:S(2)}) async-start(), calls=%async_computation.3 | async-start | bytes 2211840 | tf_op jit(solution)/shard_map/all_gather | solution.py:650
  78.2 50.0 %all-reduce.10.cloned.1.call-start = ((), (), s32[]{:S(2)}) async-start(), calls=%async_computation.2 | async-start | bytes 3145728 | tf_op jit(solution)/shard_map/psum | solution.py:730
  80.0 16.4 %copy-start.40 = (f32[1,2,2,128]{3,1,2,0:T(2,128)}, f32[1,2,2,128]{3,1,2,0:T(2,128)S(1)}, u32[]{:S(2)}) copy-start(f32[1,2,2,128]{3,1,2,0:T(2,128)S(1)} %copy.98) | copy-start | bytes 6148
  80.0 16.4 %copy-start.42 = (f32[1,2,2,128]{3,1,2,0:T(2,128)}, f32[1,2,2,128]{3,1,2,0:T(2,128)S(1)}, u32[]{:S(2)}) copy-start(f32[1,2,2,128]{3,1,2,0:T(2,128)S(1)} %copy.97) | copy-start | bytes 6148
  80.0 16.4 %copy-start.32 = (f32[768]{0:T(1024)S(1)}, f32[768]{0:T(1024)}, u32[]{:S(2)}) copy-start(f32[768]{0:T(1024)} %param.22) | copy-start | bytes 9220
  80.0 16.3 %copy-start.51 = (f32[768]{0:T(1024)S(1)}, f32[768]{0:T(1024)}, u32[]{:S(2)}) copy-start(f32[768]{0:T(1024)} %param.23) | copy-start | bytes 9220
  98.6 32.6 %copy-start.3 = (f32[512,768]{1,0:T(8,128)}, f32[512,768]{1,0:T(8,128)S(1)}, u32[]{:S(2)}) copy-start(f32[512,768]{1,0:T(8,128)S(1)} %get-tuple-element.479) | copy-start | bytes 4718596
  98.6 32.5 %copy-start.44 = (f32[512]{0:T(512)}, f32[512]{0:T(512)S(1)}, u32[]{:S(2)}) copy-start(f32[512]{0:T(512)S(1)} %broadcast_multiply_fusion.5) | copy-start | bytes 6148
  98.9 32.2 %copy-start.47 = (f32[512]{0:T(512)}, f32[512]{0:T(512)S(1)}, u32[]{:S(2)}) copy-start(f32[512]{0:T(512)S(1)} %add_rsqrt_fusion.1) | copy-start | bytes 6148
  106.5 80.1 %all-gather.5.cloned.1.call-start = ((), (), s32[]{:S(2)}) async-start(), calls=%async_computation.4 | async-start | bytes 3932160 | tf_op jit(solution)/shard_map/all_gather | solution.py:686
  110.6 6.3 copy-start.31
  113.3 5.2 collective-permute-start
  122.9 217.1 %reduce-scatter.2.cloned.1.call-start = ((), (), s32[]{:S(2)}) async-start(), calls=%async_computation.5 | async-start | bytes 7864320 | tf_op jit(solution)/shard_map/reduce_scatter | solution.py:804
  134.6 55.0 %slice-start = ((bf16[2,256,3,384]{1,3,0,2:T(8,128)(2,1)}), bf16[2,256,1,384]{1,3,0,2:T(8,128)(2,1)S(1)}, s32[]{:S(2)}) async-start(bf16[2,256,3,384]{1,3,0,2:T(8,128)(2,1)} %copy-done), calls=%async_computation.8 | async-start | bytes 786432 | tf_op jit(solution)/shard_map/slice | solution.py:684
  231.1 156.1 %all-reduce.14.cloned.1.call-start = ((), (), s32[]{:S(2)}) async-start(), calls=%async_computation.7 | async-start | bytes 6291456 | tf_op jit(solution)/shard_map/psum | solution.py:720
  341.6 6.9 collective-permute-start.1
  343.2 6.8 copy-start.10
  361.2 434.2 %all-reduce.12.cloned.1.call-start = ((), (), s32[]{:S(2)}) async-start(), calls=%async_computation.6 | async-start | bytes 28311552 | tf_op jit(solution)/shard_map/psum | solution.py:831
  363.0 5.3 copy-start.14
  377.1 10.1 %copy-start.41 = (f32[1,2,2,128]{3,1,2,0:T(2,128)S(1)}, f32[1,2,2,128]{3,1,2,0:T(2,128)}, u32[]{:S(2)}) copy-start(f32[1,2,2,128]{3,1,2,0:T(2,128)} %copy-done.40) | copy-start | bytes 6148
  377.1 10.1 %copy-start.43 = (f32[1,2,2,128]{3,1,2,0:T(2,128)S(1)}, f32[1,2,2,128]{3,1,2,0:T(2,128)}, u32[]{:S(2)}) copy-start(f32[1,2,2,128]{3,1,2,0:T(2,128)} %copy-done.42) | copy-start | bytes 6148
  377.1 12.2 %copy-start.49 = (f32[768]{0:T(1024)S(1)}, f32[768]{0:T(1024)}, u32[]{:S(2)}) copy-start(f32[768]{0:T(1024)} %get-tuple-element.397) | copy-start | bytes 9220
  377.1 12.2 %copy-start.50 = (f32[768]{0:T(1024)S(1)}, f32[768]{0:T(1024)}, u32[]{:S(2)}) copy-start(f32[768]{0:T(1024)} %get-tuple-element.404) | copy-start | bytes 9220
  (53 other events, 112.9 us)
Sparse Core Ops, SparseCore 0:
  77.7 18.5 all-reduce.7
  106.6 21.5 all-reduce.9
  361.3 25.8 all-reduce.13
  395.1 400.2 all-reduce.11
Sparse Core Ops, SparseCore 1:
  80.0 30.6 all-gather.2
  123.0 63.5 all-gather.4
  231.2 108.8 reduce-scatter.1

commit v2 on v1

--- a/solution.py
+++ b/solution.py
@@ -11,6 +11,50 @@
 EPSILON = 1e-05
 SCALING = 0.125
 MASKED = -1e30
+
+
+def shifted(block, axis, distance):
+    devices = range(lax.axis_size(axis))
+    route = [(i - distance, i) for i in devices if i - distance in devices]
+    return lax.ppermute(block, axis, route)
+
+
+def layer_norm(row_data, norm_gain, shift_bias):
+    centred = row_data - jnp.mean(row_data, axis=-1, keepdims=True)
+    recip = lax.rsqrt(jnp.mean(centred * centred, axis=-1, keepdims=True) + EPSILON)
+    normed = centred * recip
+    return (normed * norm_gain + shift_bias, normed, recip)
+
+
+def norm_back(grad_in, normed, recip, norm_gain):
+    scaled = grad_in * norm_gain
+    return recip * (
+        scaled
+        - jnp.mean(scaled, axis=-1, keepdims=True)
+        - normed * jnp.mean(scaled * normed, axis=-1, keepdims=True)
+    )
+
+
+def tile_scores(query_part, key_part, query_pos, key_pos, lengths):
+    scores = (
+        jnp.einsum("mqhd,mkhd->mhqk", query_part, key_part, preferred_element_type=jnp.float32)
+        * SCALING
+    )
+    allowed = (key_pos[None, None, :] <= query_pos[None, :, None]) & (
+        key_pos[None, None, :] < lengths[:, None, None]
+    )
+    return jnp.where(allowed[:, None], scores, MASKED)
+
+
+def tile_grads(
+    query_part, key_part, value_part, grad_part, log_part, delta_part, query_pos, key_pos, lengths
+):
+    probs_full = jnp.exp(tile_scores(query_part, key_part, query_pos, key_pos, lengths) - log_part)
+    prob_grad = jnp.einsum(
+        "mqhd,mkhd->mhqk", grad_part, value_part, preferred_element_type=jnp.float32
+    )
+    score_grad = (probs_full * (prob_grad - delta_part)).astype(jnp.bfloat16)
+    return (probs_full, prob_grad, score_grad)
 
 
 BF = jnp.bfloat16
@@ -329,48 +373,606 @@
     )(lens, tok, wq3, wo, wu, wd, gain, bias, taps3, shift3)
 
 
-def shifted(block, axis, distance):
-    devices = range(lax.axis_size(axis))
-    route = [(i - distance, i) for i in devices if i - distance in devices]
-    return lax.ppermute(block, axis, route)
-
-
-def layer_norm(row_data, norm_gain, shift_bias):
-    centred = row_data - jnp.mean(row_data, axis=-1, keepdims=True)
-    recip = lax.rsqrt(jnp.mean(centred * centred, axis=-1, keepdims=True) + EPSILON)
-    normed = centred * recip
-    return (normed * norm_gain + shift_bias, normed, recip)
-
-
-def norm_back(grad_in, normed, recip, norm_gain):
-    scaled = grad_in * norm_gain
-    return recip * (
-        scaled
-        - jnp.mean(scaled, axis=-1, keepdims=True)
-        - normed * jnp.mean(scaled * normed, axis=-1, keepdims=True)
-    )
-
-
-def tile_scores(query_part, key_part, query_pos, key_pos, lengths):
-    scores = (
-        jnp.einsum("mqhd,mkhd->mhqk", query_part, key_part, preferred_element_type=jnp.float32)
-        * SCALING
-    )
-    allowed = (key_pos[None, None, :] <= query_pos[None, :, None]) & (
-        key_pos[None, None, :] < lengths[:, None, None]
-    )
-    return jnp.where(allowed[:, None], scores, MASKED)
-
-
-def tile_grads(
-    query_part, key_part, value_part, grad_part, log_part, delta_part, query_pos, key_pos, lengths
+def flipped_pair(index):
+    return index + 1 - 2 * lax.rem(index, 2)
+
+
+def backward_kernel(
+    lens, tok_in, cot_in, attn_in, wo_in, wu_in, wd_in, wq_in, heads_in, pre_in, first_in,
+    gain1, gain2, bias2, taps3,
+    result, input_grad, down_out, up_out, out_out, qkv_out, small_out,
+    tok, cot, attn, wo, wu, wd, wq, heads, pre_all, first_all,
+    low, part_a, part_a_in, part_b, part_b_in, act_grad, middle, middle_grad,
+    second, grad_low, act, up_grad, middle_low, flat, flat_in,
+    g_down, g_up, g_out, g_qkv,
+    near, far_send, far, z_own, z_in, q_own, q_in, q_sum,
+    key_acc, value_acc, query_t, later, mixed_low, pre_grad, taps, conv_acc,
+    fg_in, fg_low, fg_all, small_send, small_in,
+    load_sem, part_send, part_recv, flat_send, flat_recv,
+    near_send, near_recv, far_ssem, far_recv, z_send, z_recv, q_send, q_recv,
+    fg_ssem, fg_recv, own_send, own_recv, in_send, in_recv, sm_send, sm_recv,
 ):
-    probs_full = jnp.exp(tile_scores(query_part, key_part, query_pos, key_pos, lengths) - log_part)
-    prob_grad = jnp.einsum(
-        "mqhd,mkhd->mhqk", grad_part, value_part, preferred_element_type=jnp.float32
-    )
-    score_grad = (probs_full * (prob_grad - delta_part)).astype(jnp.bfloat16)
-    return (probs_full, prob_grad, score_grad)
+    f, c, t, fx, fy, fd = place()
+    slot = lax.div(c, 2)
+    half = lax.rem(c, 2)
+    other = 1 - t
+    partner = (f, c, other)
+    greet([(fx, c, t), (fy, c, t), partner] + [(f, lax.rem(c + d, 4), t) for d in (1, 2, 3)])
+    slots, block_rows, model = tok.shape
+    units = act.shape[2]
+    width = wq.shape[1]
+    count = width // HD // 3
+    blocks = 4
+    tile = 128
+    tiles = block_rows // tile
+    half_rows = block_rows // 2
+    mine = pl.ds(pl.multiple_of(t * half_rows, half_rows), half_rows)
+    theirs = pl.ds(pl.multiple_of(other * half_rows, half_rows), half_rows)
+
+    loads = {}
+    for at, (name, source, target) in enumerate(
+        [
+            ("attn", attn_in, attn), ("wo", wo_in, wo), ("cot", cot_in, cot), ("wd", wd_in, wd),
+            ("tok", tok_in, tok), ("wu", wu_in, wu), ("heads", heads_in, heads),
+            ("wq", wq_in, wq), ("pre", pre_in, pre_all), ("first", first_in, first_all),
+        ]
+    ):
+        loads[name] = pltpu.make_async_copy(source, target, load_sem.at[at])
+        loads[name].start()
+
+    def swap(source, target, kind, s):
+        return remote(
+            source.at[s], target.at[s], part_send.at[kind, s], part_recv.at[kind, s], partner
+        )
+
+    loads["attn"].wait()
+    loads["wo"].wait()
+
+    def attn_out(s, carry):
+        rows = jnp.concatenate([attn[2 * s], attn[2 * s + 1]], axis=0).T
+        low[s] = rows
+        part_a[s] = mm(rows, wo[...], 1, 1)
+        swap(part_a, part_a_in, 0, s).start()
+        return carry
+
+    lax.fori_loop(0, slots, attn_out, 0)
+    loads["cot"].wait()
+    loads["wd"].wait()
+
+    def down_back(s, carry):
+        row = c * block_rows + lax.broadcasted_iota(jnp.int32, (block_rows, 1), 0)
+        grad = jnp.where(row < lens[s], cot[s].astype(F32), 0.0).astype(BF)
+        grad_low[s] = grad
+        act_grad[s] = mm(grad, wd[...], 1, 0)
+        return carry
+
+    lax.fori_loop(0, slots, down_back, 0)
+    loads["tok"].wait()
+    loads["wu"].wait()
+
+    def feed(s, carry):
+        swap(part_a, part_a_in, 0, s).wait()
+        mid = tok[s].astype(F32) + (part_a[s] + part_a_in[s])
+        middle[s] = mid
+        out, _, _ = norm_rows(mid, gain2[...], bias2[...])
+        low_out = out.astype(BF)
+        second[s] = low_out
+        rect = jnp.maximum(mm(low_out, wu[...], 1, 0), 0.0)
+        act[s] = (rect * rect).astype(BF)
+        grad = (act_grad[s] * 2.0 * rect).astype(BF)
+        up_grad[s] = grad
+        part_b[s] = mm(grad, wu[...], 1, 1)
+        swap(part_b, part_b_in, 1, s).start()
+        return carry
+
+    lax.fori_loop(0, slots, feed, 0)
+
+    def weight_grad(target, left, right):
+        def step(j, carry):
+            at = pl.ds(pl.multiple_of(j * 128, 128), 128)
+            rows = slots * block_rows
+            lhs = left[:, :, at].reshape(rows, 128)
+            rhs = right[...].reshape(rows, right.shape[2])
+            target[at, :] = mm(lhs, rhs, 0, 0).astype(BF)
+            return carry
+
+        lax.fori_loop(0, model // 128, step, 0)
+
+    grads = [g_down, g_up, g_out, g_qkv]
+    finals = [down_out, up_out, out_out]
+    share = model // 4
+    rows_half = share // 2
+    cuts = [2, 2, 1, 1]
+    inner = lax.rem(lax.div(c + 1, 2), 2)
+    z_outer = jnp.where(c == 1, 0, 3)
+    z_near = jnp.where(c == 0, 1, jnp.where(c == 3, 2, 3 - c))
+
+    def rows_of(w, owner, side, u):
+        size = rows_half // cuts[w]
+        start = owner * share + side * rows_half + u * size
+        return pl.ds(pl.multiple_of(start, 16), size)
+
+    def cut(w, u):
+        size = rows_half // cuts[w]
+        return pl.ds(u * size, size)
+
+    def near_copy(w, kind, u):
+        owner = (fx, fd, fy, fd)[kind]
+        target = (fx, c, t) if kind < 2 else (fy, c, t)
+        return remote(
+            grads[w].at[rows_of(w, owner, kind // 2, u)],
+            near[w].at[kind, cut(w, u)],
+            near_send[w].at[kind, u],
+            near_recv[w].at[kind, u],
+            target,
+        )
+
+    def far_copy(w, side, u):
+        return remote(
+            far_send[w].at[side, cut(w, u)],
+            far[w].at[side, cut(w, u)],
+            far_ssem[w].at[side, u],
+            far_recv[w].at[side, u],
+            (fy, c, t) if side == 0 else (fx, c, t),
+        )
+
+    def first_hop(w):
+        for kinds in ((1, 3), (0, 2)):
+            for u in range(cuts[w]):
+                for kind in kinds:
+                    near_copy(w, kind, u).start()
+
+    def second_hop(w):
+        for u in range(cuts[w]):
+            for side in (0, 1):
+                kind = 1 + 2 * side
+                near_copy(w, kind, u).wait_recv()
+                owner = fy if side == 0 else fx
+                own = grads[w][rows_of(w, owner, side, u), :].astype(F32)
+                come = near[w][kind, cut(w, u), :].astype(F32)
+                far_send[w][side, cut(w, u), :] = (own + come).astype(BF)
+                far_copy(w, side, u).start()
+
+    def own_sum(w, side, u):
+        near_copy(w, 2 * side, u).wait_recv()
+        far_copy(w, side, u).wait_recv()
+        own = grads[w][rows_of(w, f, side, u), :].astype(F32)
+        return own + near[w][2 * side, cut(w, u), :] + far[w][side, cut(w, u), :]
+
+    def z_rows(w, side, u):
+        size = rows_half // cuts[w]
+        return pl.ds(side * rows_half + u * size, size)
+
+    def z_copy(w, stage, side, u):
+        view = z_rows(w, side, u)
+        source = (z_own[w], z_own[w], finals[w])[stage].at[view]
+        target = (z_in[w].at[0, view], z_in[w].at[1, view], finals[w].at[view])[stage]
+        device = (z_near, z_near, z_outer)[stage]
+        return remote(
+            source, target, z_send[w].at[stage, side, u], z_recv[w].at[stage, side, u],
+            (f, device, t),
+        )
+
+    def each(w):
+        return [(side, u) for u in range(cuts[w]) for side in (0, 1)]
+
+    def z_first(w):
+        for side, u in each(w):
+            z_own[w][z_rows(w, side, u), :] = own_sum(w, side, u).astype(BF)
+
+            @pl.when(inner == 0)
+            def _():
+                z_copy(w, 0, side, u).start()
+
+    def z_second(w):
+        @pl.when(inner == 1)
+        def _():
+            for side, u in each(w):
+                z_copy(w, 0, side, u).wait_recv()
+                at = z_rows(w, side, u)
+                total = z_own[w][at, :].astype(F32) + z_in[w][0, at, :]
+                z_own[w][at, :] = total.astype(BF)
+                z_copy(w, 1, side, u).start()
+
+    def z_third(w):
+        @pl.when(inner == 1)
+        def _():
+            for side, u in each(w):
+                z_copy(w, 1, side, u).wait_recv()
+                at = z_rows(w, side, u)
+                total = z_own[w][at, :].astype(F32) + z_in[w][1, at, :]
+                finals[w][at, :] = total.astype(BF)
+                z_copy(w, 2, side, u).start()
+
+    def z_done(w):
+        @pl.when(inner == 1)
+        def _():
+            for side, u in each(w):
+                z_copy(w, 1, side, u).wait_send()
+                z_copy(w, 2, side, u).wait_send()
+
+        @pl.when(inner == 0)
+        def _():
+            for side, u in each(w):
+                z_copy(w, 0, side, u).wait_send()
+                z_copy(w, 2, side, u).wait_recv()
+
+    def hops_done(w):
+        for u in range(cuts[w]):
+            for kind in range(4):
+                near_copy(w, kind, u).wait_send()
+            for side in (0, 1):
+                far_copy(w, side, u).wait_send()
+
+    weight_grad(g_down, grad_low, act)
+    first_hop(0)
+
+    def flat_copy(s, h):
+        return remote(
+            flat.at[s, h], flat_in.at[c], flat_send.at[s, h],
+            flat_recv.at[lax.rem(2 * s + h - c + 4, 4)], (f, 2 * s + h, t),
+        )
+
+    small_send[0] = jnp.zeros(small_send.shape[1:], F32)
+    in_half = (
+        lax.div(lax.broadcasted_iota(jnp.int32, (block_rows, 1), 0), half_rows) == t
+    ).astype(F32)
+
+    def norm_two_back(s, carry):
+        swap(part_b, part_b_in, 1, s).wait()
+        grad = part_b[s] + part_b_in[s]
+        _, normed, recip = norm_rows(middle[s], gain2[...], bias2[...])
+        kept = grad * in_half
+        small_send[0, 2:3, :] += jnp.sum(kept * normed, axis=0, keepdims=True)
+        small_send[0, 3:4, :] += jnp.sum(kept, axis=0, keepdims=True)
+        back = grad_low[s].astype(F32) + norm_back(grad, normed, recip, gain2[...])
+        middle_grad[s] = back
+        back = back.astype(BF)
+        middle_low[s] = back
+        flat_rows = mm(back, wo[...], 1, 0).T.astype(BF)
+        for h in (0, 1):
+            flat[s, h] = flat_rows[h * (width // 3) : (h + 1) * (width // 3)]
+
+            @pl.when(2 * s + h != c)
+            def _():
+                flat_copy(s, h).start()
+
+            @pl.when(2 * s + h == c)
+            def _():
+                flat_in[c] = flat[s, h]
+
+        return carry
+
+    lax.fori_loop(0, slots, norm_two_back, 0)
+    weight_grad(g_up, second, up_grad)
+    second_hop(0)
+    first_hop(1)
+    weight_grad(g_out, middle_low, low)
+    first_hop(2)
+
+    def down(s, carry):
+        swap_out = swap(part_a, part_a_in, 2, s)
+        part_a[s] = mm(act[s], wd[...], 1, 1)
+        swap_out.start()
+        return carry
+
+    lax.fori_loop(0, slots, down, 0)
+
+    for name in ("heads", "wq", "pre", "first"):
+        loads[name].wait()
+    part_width = width // 3
+    for h in (0, 1):
+
+        @pl.when(half == h)
+        def _():
+            lanes = slice(h * part_width, (h + 1) * part_width)
+            for kind in range(3):
+                for tap in range(3):
+                    taps[tap : tap + 1, kind * part_width : (kind + 1) * part_width] = taps3[
+                        tap, kind : kind + 1, lanes
+                    ]
+
+    key_acc[...] = jnp.zeros_like(key_acc)
+    value_acc[...] = jnp.zeros_like(value_acc)
+    later[...] = jnp.zeros_like(later)
+    conv_acc[...] = jnp.zeros_like(conv_acc)
+    length = lens[slot]
+
+    def fg_view(block, rows):
+        lanes = pl.ds(block % 2 * model, model)
+        return act_grad.at[block // 2, rows, lanes]
+
+    def own_copy(block):
+        return remote(
+            fg_view(block, theirs), fg_in.at[block], own_send.at[block], own_recv.at[block],
+            partner,
+        )
+
+    def fg_copy(block):
+        return remote(
+            fg_low.at[block], fg_all.at[c], fg_ssem.at[block],
+            fg_recv.at[lax.rem(block - c + 4, 4)], (f, block, t),
+        )
+
+    def hand_over(block):
+        own_copy(block).wait_recv()
+        fg_low[block] = (fg_view(block, mine)[...] + fg_in[block]).astype(BF)
+
+        @pl.when(block != c)
+        def _():
+            fg_copy(block).start()
+
+        @pl.when(block == c)
+        def _():
+            fg_all[c] = fg_low[block]
+
+    for block in reversed(range(blocks)):
+
+        @pl.when(block != c)
+        def _():
+            remote(
+                flat_in.at[block], flat_in.at[block], flat_send.at[0, 0],
+                flat_recv.at[lax.rem(c - block + 4, 4)], partner,
+            ).wait_recv()
+
+        keys = (block + 1) * block_rows
+
+        def attend(n, carry, block=block, keys=keys):
+            head, piece = lax.div(n, tiles), lax.rem(n, tiles)
+            at = pl.multiple_of(block * block_rows + piece * tile, tile)
+            query = heads[head, pl.ds(at, tile), :]
+            key = heads[count + head, 0:keys, :]
+            scores = mm(query, key, 1, 1)
+            col = lax.broadcasted_iota(jnp.int32, scores.shape, 1)
+            row = at + lax.broadcasted_iota(jnp.int32, (tile, 1), 0)
+            scores = jnp.where(col < jnp.minimum(row + 1, length), scores, MASKED)
+            powers = jnp.exp(scores - jnp.max(scores, axis=-1, keepdims=True))
+            probs = powers * (1.0 / jnp.sum(powers, axis=-1, keepdims=True))
+            lanes = pl.ds(pl.multiple_of(piece * tile, tile), tile)
+            channels = pl.ds(pl.multiple_of(head * HD, HD), HD)
+            grad_t = flat_in[block, channels, lanes]
+            prob_grad = mm(grad_t.T, heads[2 * count + head, 0:keys, :], 1, 1)
+            delta = jnp.sum(probs * prob_grad, axis=-1, keepdims=True)
+            score_grad = (probs * (prob_grad - delta)).astype(BF)
+            query_t[channels, lanes] = (mm(score_grad, key, 1, 0) * SCALING).T
+            key_acc[head, :, 0:keys] += mm(query.T, score_grad, 1, 0)
+            value_acc[head, :, 0:keys] += mm(grad_t, probs.astype(BF), 1, 0)
+            return carry
+
+        lax.fori_loop(0, count * tiles, attend, 0)
+        span = slice(block * block_rows, (block + 1) * block_rows)
+        mixed = jnp.concatenate(
+            [
+                query_t[...],
+                key_acc[:, :, span].reshape(part_width, block_rows),
+                value_acc[:, :, span].reshape(part_width, block_rows),
+            ],
+            axis=0,
+        )
+        mixed_low[...] = mixed.T
+        mixed = mixed_low[...]
+        joined = jnp.concatenate([mixed, later[...]], axis=0)
+        next_one = pltpu.roll(joined, block_rows + 7, 0)[:block_rows]
+        next_two = pltpu.roll(joined, block_rows + 6, 0)[:block_rows]
+        later[...] = mixed[:8]
+        before = pre_all[block].astype(F32)
+        for at, shifted_mixed in enumerate((mixed, next_one, next_two)):
+            conv_acc[at : at + 1, :] += jnp.sum(before * shifted_mixed, axis=0, keepdims=True)
+        conv_acc[3:4, :] += jnp.sum(mixed, axis=0, keepdims=True)
+        grad = (taps[0:1] * mixed + taps[1:2] * next_one + taps[2:3] * next_two).astype(BF)
+        pre_grad[block] = grad
+        fg_view(block, pl.ds(0, block_rows))[...] = mm(grad, wq[...], 1, 1)
+        own_copy(block).start()
+        if block == 3:
+            z_first(0)
+        if block == 2:
+            hand_over(3)
+            second_hop(1)
+            z_second(0)
+        if block == 1:
+            hand_over(2)
+            second_hop(2)
+            z_third(0)
+        if block == 0:
+            hand_over(1)
+
+    def qkv_grad(j, carry):
+        at = pl.ds(pl.multiple_of(j * 128, 128), 128)
+        rows = blocks * block_rows
+        lhs = first_all[:, :, at].reshape(rows, 128)
+        g_qkv[at, :] = mm(lhs, pre_grad[...].reshape(rows, width), 0, 0).astype(BF)
+        return carry
+
+    lax.fori_loop(0, model // 128, qkv_grad, 0)
+    first_hop(3)
+    hand_over(0)
+    z_first(1)
+    second_hop(3)
+
+    for s in range(slots):
+        swap(part_a, part_a_in, 2, s).wait()
+        result[s] = (middle[s] + (part_a[s] + part_a_in[s])).astype(BF)
+
+    z_second(1)
+    z_first(2)
+    z_second(2)
+
+    def q_copy(stage):
+        if stage == 0:
+            return remote(
+                q_own, q_in, q_send.at[0], q_recv.at[0], (f, lax.rem(c + 2, 4), t)
+            )
+        return remote(
+            q_sum.at[half], q_sum.at[half], q_send.at[1], q_recv.at[1],
+            (f, flipped_pair(c), t),
+        )
+
+    for side in (0, 1):
+        q_own[side * rows_half : (side + 1) * rows_half, :] = own_sum(3, side, 0).astype(BF)
+    q_copy(0).start()
+
+    for d in (1, 2, 3):
+        source = lax.rem(c - d + 4, 4)
+        remote(
+            fg_all.at[source], fg_all.at[source], fg_ssem.at[0], fg_recv.at[d], partner
+        ).wait_recv()
+
+    def in_copy(s):
+        view = input_grad.at[s, mine]
+        return remote(view, view, in_send.at[s], in_recv.at[s], partner)
+
+    for s in range(slots):
+        grad = fg_all[2 * s].astype(F32) + fg_all[2 * s + 1]
+        rows = tok[s, mine, :].astype(F32)
+        _, normed, recip = norm_rows(rows, gain1[...], gain1[...])
+        small_send[0, 0:1, :] += jnp.sum(grad * normed, axis=0, keepdims=True)
+        small_send[0, 1:2, :] += jnp.sum(grad, axis=0, keepdims=True)
+        input_grad[s, mine, :] = middle_grad[s, mine, :] + norm_back(
+            grad, normed, recip, gain1[...]
+        )
+        in_copy(s).start()
+
+    for h in (0, 1):
+
+        @pl.when(half == h)
+        def _():
+            lanes = slice(h * part_width, (h + 1) * part_width)
+            for kind in range(3):
+                channels = slice(kind * part_width, (kind + 1) * part_width)
+                for tap in range(3):
+                    row = 4 + 3 * tap + kind
+                    small_send[0, row : row + 1, lanes] = conv_acc[tap : tap + 1, channels]
+                small_send[0, 13 + kind : 14 + kind, lanes] = conv_acc[3:4, channels]
+
+    peers = [
+        (fx, c, t), (fy, c, t), (f, flipped_pair(c), t), (f, lax.rem(c + 2, 4), t), partner
+    ]
+
+    def small_copy(stage):
+        return remote(
+            small_send.at[stage], small_in.at[stage], sm_send.at[stage], sm_recv.at[stage],
+            peers[stage],
+        )
+
+    def small_add(stage):
+        small_copy(stage).wait()
+        if stage < 4:
+            small_send[stage + 1] = small_send[stage] + small_in[stage]
+            small_copy(stage + 1).start()
+        else:
+            small_out[0:4] = small_send[4, 0:4] + small_in[4, 0:4]
+            small_out[4:16] = small_send[4, 4:16]
+
+    small_copy(0).start()
+    z_third(1)
+    small_add(0)
+    z_third(2)
+    small_add(1)
+    q_copy(0).wait()
+    q_sum[half] = (q_own[...].astype(F32) + q_in[...]).astype(BF)
+    q_copy(1).start()
+    small_add(2)
+    small_add(3)
+    small_add(4)
+    remote(
+        q_sum.at[1 - half], q_sum.at[1 - half], q_send.at[1], q_recv.at[1], partner
+    ).wait_recv()
+    q_copy(1).wait_send()
+    for h in (0, 1):
+        for kind in range(3):
+            qkv_out[kind, :, h * part_width : (h + 1) * part_width] = q_sum[
+                h, :, kind * part_width : (kind + 1) * part_width
+            ]
+
+    for w in range(4):
+        hops_done(w)
+    for w in range(3):
+        z_done(w)
+    for s in range(slots):
+        in_copy(s).wait_send()
+        view = input_grad.at[s, theirs]
+        remote(view, view, in_send.at[s], in_recv.at[s], partner).wait_recv()
+        for h in (0, 1):
+
+            @pl.when(2 * s + h != c)
+            def _():
+                flat_copy(s, h).wait_send()
+
+    for block in range(blocks):
+        own_copy(block).wait_send()
+
+        @pl.when(block != c)
+        def _():
+            fg_copy(block).wait_send()
+
+
+def backward_call(
+    lens, tok, cot, attn, wo, wu, wd, wq, heads, pre_all, first_all, gain1, gain2, bias2, taps3
+):
+    slots, block_rows, model = tok.shape
+    units, width, channels = wu.shape[1], wq.shape[1], wo.shape[1]
+    share = model // 4
+    part = width // 3
+    tall = (slots, block_rows, model)
+    wide = (slots, block_rows, units)
+    half = block_rows // 2
+    columns = [units, units, channels, width]
+    cuts = [2, 2, 1, 1]
+    dma = pltpu.SemaphoreType.DMA
+
+    def vmem(shape, kind=BF):
+        return pltpu.VMEM(tuple(shape), kind)
+
+    return pl.pallas_call(
+        backward_kernel,
+        name="backward",
+        out_shape=[
+            jax.ShapeDtypeStruct(tall, BF),
+            jax.ShapeDtypeStruct(tall, F32),
+            jax.ShapeDtypeStruct((share, units), BF),
+            jax.ShapeDtypeStruct((share, units), BF),
+            jax.ShapeDtypeStruct((share, channels), BF),
+            jax.ShapeDtypeStruct((3, share, channels), BF),
+            jax.ShapeDtypeStruct((16, model), F32),
+        ],
+        in_specs=[SMEM] + [ANY] * 10 + [VMEM] * 4,
+        out_specs=[VMEM] * 7,
+        scratch_shapes=[
+            vmem(tall), vmem(tall), vmem(attn.shape), vmem(wo.shape), vmem(wu.shape),
+            vmem(wd.shape), vmem(wq.shape), vmem(heads.shape), vmem(pre_all.shape),
+            vmem(first_all.shape),
+            vmem((slots, block_rows, channels)), vmem(tall, F32), vmem(tall, F32),
+            vmem(tall, F32), vmem(tall, F32), vmem(wide, F32), vmem(tall, F32), vmem(tall, F32),
+            vmem(tall), vmem(tall), vmem(wide), vmem(wide), vmem(tall),
+            vmem((slots, 2, part, block_rows)), vmem((4, part, block_rows)),
+            vmem((model, units)), vmem((model, units)), vmem((model, channels)),
+            vmem((model, width)),
+            [vmem((4, share // 2, n)) for n in columns],
+            [vmem((2, share // 2, n)) for n in columns],
+            [vmem((2, share // 2, n)) for n in columns],
+            [vmem((share, n)) for n in columns[:3]],
+            [vmem((2, share, n)) for n in columns[:3]],
+            vmem((share, width)), vmem((share, width)), vmem((2, share, width)),
+            vmem((part // HD, HD, 4 * block_rows), F32),
+            vmem((part // HD, HD, 4 * block_rows), F32),
+            vmem((part, block_rows), F32), vmem((8, width), F32),
+            vmem((block_rows, width), F32), vmem((4, block_rows, width)),
+            vmem((8, width), F32), vmem((8, width), F32),
+            vmem((4, half, model), F32),
+            vmem((4, half, model)), vmem((4, half, model)),
+            vmem((5, 16, model), F32), vmem((5, 16, model), F32),
+            dma((10,)), dma((3, slots)), dma((3, slots)), dma((slots, 2)), dma((4,)),
+            [dma((4, n)) for n in cuts], [dma((4, n)) for n in cuts],
+            [dma((2, n)) for n in cuts], [dma((2, n)) for n in cuts],
+            [dma((3, 2, n)) for n in cuts[:3]], [dma((3, 2, n)) for n in cuts[:3]],
+            dma((2,)), dma((2,)),
+            dma((4,)), dma((4,)), dma((4,)), dma((4,)), dma((slots,)), dma((slots,)),
+            dma((5,)), dma((5,)),
+        ],
+        compiler_params=pltpu.CompilerParams(
+            collective_id=1, has_side_effects=True, vmem_limit_bytes=67043328
+        ),
+    )(lens, tok, cot, attn, wo, wu, wd, wq, heads, pre_all, first_all, gain1, gain2, bias2, taps3)
 
 
 def local(
@@ -641,228 +1243,33 @@
     up_weight,
     down_weight,
 ):
-    batches, block_rows, model_width = tokens.shape
-    all_rows = batches * block_rows
-    gathered = forward_call(
+    model = tokens.shape[2]
+    gain1, bias1 = ln1_gain[None], ln1_bias[None]
+    wq_all, wo_all, wu_all, wd_all, attn, heads, pre_all, first_all = forward_call(
         lengths, tokens, qkv_weight.transpose(1, 0, 2), out_weight.T, up_weight, down_weight.T,
-        ln1_gain[None], ln1_bias[None], conv_kernel, conv_bias,
-    )
-    qkv_full = lax.all_gather(qkv_weight, "fsdp", axis=0, tiled=True)
-    out_full = gathered[1].reshape(model_width, -1).T
-    up_full_w = gathered[2].reshape(model_width, -1)
-    down_full_w = gathered[3].reshape(model_width, -1).T
-    local_width = qkv_full.shape[2]
-    local_heads = local_width // HD
-    ctx_count = lax.axis_size("ctx")
-    slot_span = block_rows * ctx_count
-    group_blocks = 4
-    key_span = block_rows * group_blocks
-    ctx_index = lax.axis_index("ctx")
-    positions = ctx_index * block_rows + jnp.arange(block_rows, dtype=jnp.int32)
-    span_iota = jnp.arange(key_span, dtype=jnp.int32)
-    block_count = (ctx_index * block_rows + block_rows + key_span - 1) // key_span
-    token_valid = positions[None, :] < lengths[:, None]
-
-    def span_slice(array_data, block, axis_pos):
-        return lax.dynamic_slice_in_dim(array_data, block * key_span, key_span, axis_pos)
-
-    inputs = tokens.astype(jnp.float32).reshape(all_rows, model_width)
-    first_out, first_hat, first_recip = layer_norm(inputs, ln1_gain, ln1_bias)
-    first_low = first_out.astype(jnp.bfloat16)
-    pre_low = jnp.einsum(
-        "td,dcn->tcn", first_low, qkv_full, preferred_element_type=jnp.float32
-    ).astype(jnp.bfloat16)
-    pre_low = pre_low.reshape(batches, block_rows, 3, local_width)
-    earlier = shifted(pre_low[:, block_rows - 2 :], "ctx", 1)
-    extended = jnp.concatenate([earlier, pre_low], axis=1).astype(jnp.float32)
-    conv_out = (
-        conv_bias
-        + conv_kernel[0] * extended[:, 2:]
-        + conv_kernel[1] * extended[:, 1:-1]
-        + conv_kernel[2] * extended[:, :-2]
-    ).astype(jnp.bfloat16)
-    query_heads = conv_out[:, :, 0].reshape(batches, block_rows, local_heads, HD)
-    own_pairs = conv_out[:, :, 1:]
-    whole_pairs = lax.all_gather(own_pairs, "ctx", axis=1, tiled=True)
-    key_heads = whole_pairs[:, :, 0].reshape(batches, slot_span, local_heads, HD)
-    value_heads = whole_pairs[:, :, 1].reshape(batches, slot_span, local_heads, HD)
-
-    def stat_step(block, carry):
-        row_max, total = carry
-        key_pos = block * key_span + span_iota
-        scores = tile_scores(
-            query_heads, span_slice(key_heads, block, 1), positions, key_pos, lengths
-        )
-        new_max = jnp.maximum(row_max, jnp.max(scores, axis=-1, keepdims=True))
-        total = total * jnp.exp(row_max - new_max) + jnp.sum(
-            jnp.exp(scores - new_max), axis=-1, keepdims=True
-        )
-        return (new_max, total)
-
-    stat_shape = (batches, local_heads, block_rows, 1)
-    row_max, total = lax.fori_loop(
-        0,
-        block_count,
-        stat_step,
-        (jnp.full(stat_shape, MASKED, jnp.float32), jnp.zeros(stat_shape, jnp.float32)),
-    )
-    log_total = row_max + jnp.log(total)
-
-    attn_low = gathered[4].reshape(batches, local_width, block_rows)
-    attn_low = attn_low.transpose(0, 2, 1).reshape(all_rows, local_width)
-    attn_out = lax.psum(jnp.dot(attn_low, out_full, preferred_element_type=jnp.float32), "tp")
-    middle = inputs + attn_out
-    second_out, second_hat, second_recip = layer_norm(middle, ln2_gain, ln2_bias)
-    second_low = second_out.astype(jnp.bfloat16)
-    up_full = jnp.dot(second_low, up_full_w, preferred_element_type=jnp.float32)
-    rectified = jnp.maximum(up_full, 0.0)
-    act_low = (rectified * rectified).astype(jnp.bfloat16)
-    ffn_out = lax.psum(jnp.dot(act_low, down_full_w, preferred_element_type=jnp.float32), "tp")
-    result = (middle + ffn_out).reshape(batches, block_rows, model_width).astype(jnp.bfloat16)
-    grad_out = (
-        cotangent.astype(jnp.float32) * token_valid[:, :, None].astype(jnp.float32)
-    ).reshape(all_rows, model_width)
-    grad_low = grad_out.astype(jnp.bfloat16)
-    down_wgrad = jnp.einsum("tf,td->fd", act_low, grad_low, preferred_element_type=jnp.float32)
-    act_grad = jnp.einsum("td,fd->tf", grad_low, down_full_w, preferred_element_type=jnp.float32)
-    up_grad_low = (act_grad * 2.0 * rectified).astype(jnp.bfloat16)
-    up_wgrad = jnp.einsum("td,tf->df", second_low, up_grad_low, preferred_element_type=jnp.float32)
-    second_grad = lax.psum(
-        jnp.einsum("tf,df->td", up_grad_low, up_full_w, preferred_element_type=jnp.float32), "tp"
-    )
-    gain_two_grad = jnp.sum(second_grad * second_hat, axis=0)
-    bias_two_grad = jnp.sum(second_grad, axis=0)
-    middle_grad = grad_out + norm_back(second_grad, second_hat, second_recip, ln2_gain)
-    middle_low = middle_grad.astype(jnp.bfloat16)
-    out_wgrad = jnp.einsum("tn,td->nd", attn_low, middle_low, preferred_element_type=jnp.float32)
-    attn_flat = jnp.einsum(
-        "td,nd->tn", middle_low, out_full, preferred_element_type=jnp.float32
-    ).astype(jnp.bfloat16)
-    attn_grad = attn_flat.reshape(batches, block_rows, local_heads, HD)
-
-    def delta_step(block, accum):
-        key_pos = block * key_span + span_iota
-        probs_full = jnp.exp(
-            tile_scores(query_heads, span_slice(key_heads, block, 1), positions, key_pos, lengths)
-            - log_total
-        )
-        prob_grad = jnp.einsum(
-            "mqhd,mkhd->mhqk",
-            attn_grad,
-            span_slice(value_heads, block, 1),
-            preferred_element_type=jnp.float32,
-        )
-        return accum + jnp.sum(probs_full * prob_grad, axis=-1, keepdims=True)
-
-    delta = lax.fori_loop(0, block_count, delta_step, jnp.zeros(stat_shape, jnp.float32))
-    query_zero = jnp.zeros((batches, block_rows, local_heads, HD), jnp.float32)
-
-    def back_step(block, carry):
-        accum, buffer = carry
-        key_pos = block * key_span + span_iota
-        key_part = span_slice(key_heads, block, 1)
-        probs_full, prob_grad, score_grad = tile_grads(
-            query_heads,
-            key_part,
-            span_slice(value_heads, block, 1),
-            attn_grad,
-            log_total,
-            delta,
-            positions,
-            key_pos,
-            lengths,
-        )
-        probs_again = probs_full.astype(jnp.bfloat16)
-        accum = (
-            accum
-            + jnp.einsum(
-                "mhqk,mkhd->mqhd", score_grad, key_part, preferred_element_type=jnp.float32
-            )
-            * SCALING
-        )
-        key_term = (
-            jnp.einsum(
-                "mhqk,mqhd->mkhd", score_grad, query_heads, preferred_element_type=jnp.float32
-            )
-            * SCALING
-        )
-        value_term = jnp.einsum(
-            "mhqk,mqhd->mkhd", probs_again, attn_grad, preferred_element_type=jnp.float32
-        )
-        stacked = jnp.stack(
-            [
-                key_term.reshape(batches, key_span, local_width),
-                value_term.reshape(batches, key_span, local_width),
-            ],
-            axis=2,
-        )
-        buffer = lax.dynamic_update_slice_in_dim(buffer, stacked, block * key_span, 1)
-        return (accum, buffer)
-
-    buffer_zero = jnp.zeros((batches, slot_span, 2, local_width), jnp.float32)
-    query_grad, pair_terms = lax.fori_loop(0, block_count, back_step, (query_zero, buffer_zero))
-    pair_grad = lax.psum_scatter(pair_terms, "ctx", scatter_dimension=1, tiled=True)
-    mixed_grad = jnp.concatenate(
-        [query_grad.reshape(batches, block_rows, 1, local_width), pair_grad], axis=2
-    )
-    later = shifted(mixed_grad[:, :2], "ctx", -1)
-    ahead = jnp.concatenate([mixed_grad, later], axis=1)
-    pre_grad = (
-        conv_kernel[0] * ahead[:, :block_rows]
-        + conv_kernel[1] * ahead[:, 1 : block_rows + 1]
-        + conv_kernel[2] * ahead[:, 2:]
-    ).astype(jnp.bfloat16)
-    kernel_grad = jnp.stack(
-        [
-            jnp.sum(extended[:, 2 - offset : 2 - offset + block_rows] * mixed_grad, axis=(0, 1))
-            for offset in range(3)
-        ]
-    )
-    shift_grad = jnp.sum(mixed_grad, axis=(0, 1))
-    pre_grad = pre_grad.reshape(all_rows, 3, local_width)
-    qkv_wgrad = jnp.einsum("td,tcn->dcn", first_low, pre_grad, preferred_element_type=jnp.float32)
-    first_grad = lax.psum(
-        jnp.einsum("tcn,dcn->td", pre_grad, qkv_full, preferred_element_type=jnp.float32), "tp"
-    )
-    gain_one_grad = jnp.sum(first_grad * first_hat, axis=0)
-    bias_one_grad = jnp.sum(first_grad, axis=0)
-    input_grad = middle_grad + norm_back(first_grad, first_hat, first_recip, ln1_gain)
-    input_grad = input_grad.reshape(batches, block_rows, model_width)
-    summed = lax.psum(
-        (
-            qkv_wgrad,
-            out_wgrad,
-            up_wgrad,
-            down_wgrad,
-            gain_one_grad,
-            bias_one_grad,
-            kernel_grad,
-            shift_grad,
-            gain_two_grad,
-            bias_two_grad,
-        ),
-        ("fsdp", "ctx"),
-    )
-    share_rows = model_width // lax.axis_size("fsdp")
-    owner_start = lax.axis_index("fsdp") * share_rows
-    qkv_share = lax.dynamic_slice_in_dim(summed[0], owner_start, share_rows, 0)
-    out_share = lax.dynamic_slice_in_dim(summed[1], owner_start, share_rows, 1)
-    up_share = lax.dynamic_slice_in_dim(summed[2], owner_start, share_rows, 0)
-    down_share = lax.dynamic_slice_in_dim(summed[3], owner_start, share_rows, 1)
-    small_sums = summed[4:]
+        gain1, bias1, conv_kernel, conv_bias,
+    )
+    wq_all, wo_all, wu_all, wd_all = (
+        w.reshape(model, w.shape[2]) for w in (wq_all, wo_all, wu_all, wd_all)
+    )
+    result, input_grad, down, up, out, qkv, small = backward_call(
+        lengths, tokens, cotangent, attn, wo_all, wu_all, wd_all, wq_all, heads, pre_all,
+        first_all, gain1, ln2_gain[None], ln2_bias[None], conv_kernel,
+    )
+    channels = out.shape[1]
     return (
         result,
         input_grad,
-        small_sums[0],
-        small_sums[1],
-        qkv_share,
-        small_sums[2],
-        small_sums[3],
-        out_share,
-        small_sums[4],
-        small_sums[5],
-        up_share,
-        down_share,
+        small[0],
+        small[1],
+        qkv.astype(F32).transpose(1, 0, 2),
+        small[4:13, :channels].reshape(3, 3, channels),
+        small[13:16, :channels],
+        out.astype(F32).T,
+        small[2],
+        small[3],
+        up.astype(F32),
+        down.astype(F32).T,
     )
 
 

time: 820 us -> 205 us (0.25)
  waiting for transfers between devices: 515 us -> 0 us
  Pallas kernels: 62.8 us -> 186 us
  blocking collectives: 82.4 us -> 0 us
  matrix products: 57.3 us -> 0 us
  other arithmetic: 36.9 us -> 5.98 us
  local copies, waits for them, and re-layouts: 35.1 us -> 11.3 us
  between operations: 16.7 us -> 0.68 us
    psum x4 -> x0, waiting for transfers between devices: 349 us -> none  [the longest x1 319 us: local_fast(): lax.psum((qkv_wgrad, out_wgrad, up_wgrad, down_wgrad, gain_one_grad, bias...]
    pallas_call x0 -> x1, Pallas kernels: none -> 123 us  [backward_call(): pl.pallas_call(backward_kernel, name='backward', out_shape=[jax.ShapeDtyp...]
    reduce_scatter x1 -> x0, waiting for transfers between devices: 109 us -> none  [local_fast(): lax.psum_scatter(pair_terms, 'ctx', scatter_dimension=1, tiled=True)]
    psum x1 -> x0, blocking collectives: 82.4 us -> none  [local_fast(): lax.psum((qkv_wgrad, out_wgrad, up_wgrad, down_wgrad, gain_one_grad, bias...]
    dot_general x20 -> x0, matrix products: 57.3 us -> none  [the longest x1 6.5 us: tile_grads(): jnp.einsum('mqhd,mkhd->mhqk', grad_part, value_part, preferred_element_ty...]
    all_gather x2 -> x0, waiting for transfers between devices: 56 us -> none  [the longest x1 52 us: local_fast(): whole_pairs = lax.all_gather(own_pairs, 'ctx', axis=1, tiled=True)]
    reduce_sum x8 -> x0, other arithmetic: 16.3 us -> none  [the longest x1 4.61 us: local_fast(): jnp.sum(extended[:, 2 - offset:2 - offset + block_rows] * mixed_grad, axi...]
    dynamic_slice x4 -> x0, local copies, waits for them, and re-layouts: 8.55 us -> none  [the longest x1 2.36 us: local_fast(): up_share = lax.dynamic_slice_in_dim(summed[2], owner_start, share_rows, 0)]
  transfers between devices with their start and end apart: 9 -> 0, of which waited for: 7 -> 0; matrix products, arithmetic and copies ran while one was open for 6% -> 0% of each run, Pallas kernels for 0% -> 0%
where the time goes in v2:
time: 205 us; the launch traced here: 204 us
  Pallas kernels  186 us (91%)
  local copies, waits for them, and re-layouts  11.3 us (6%)
  other arithmetic  5.98 us (3%)
    pallas_call x1, Pallas kernels, backward_call(): pl.pallas_call(backward_kernel, name='backward', out_shape=[jax.ShapeDtyp...  123 us
    pallas_call x1, Pallas kernels, forward_call(): pl.pallas_call(forward_kernel, name='forward', out_shape=[whole((rows, wi...  62.8 us

profile of v2, /device:TPU:0, one launch (start us, length us, event | category | flops | bytes accessed | tf_op | source)
XLA Modules:
  0.0 204.1 jit_solution(7906281923462217071)
XLA Ops:
  0.6 1.3 broadcast_in_dim.12.gain.gain1
  1.9 1.3 broadcast_in_dim.13.bias
  3.2 1.3 broadcast_in_dim.14.gain2
  4.4 1.3 broadcast_in_dim.15.bias2
  5.7 62.8 %forward.1 = (bf16[4,192,576]{2,1,0:T(8,128)(2,1)}, bf16[4,192,384]{2,1,0:T(8,128)(2,1)}, bf16[4,192,1536]{2,1,0:T(8,128)(2,1)}, bf16[4,192,1536]{2,1,0:T(8,128)...) custom-call(s32[2]{0:T(128)} %lens.3, ...), custom_call_target="tpu_custom_call" | custom-call | tf_op jit(solution)/shard_map/forward/pallas_call | solution.py:339
  68.5 123.3 %backward.1 = (bf16[2,256,768]{2,1,0:T(8,128)(2,1)}, f32[2,256,768]{2,1,0:T(8,128)}, bf16[192,1536]{1,0:T(8,128)(2,1)}, bf16[192,1536]{1,0:T(8,128)(2,1)}, bf16[...) custom-call(s32[2]{0:T(128)} %lens.3, bf16[2,256,768]{2,1,0:T(8,128)(2,1)} %tok_in.1, ...), custom_call_target="tpu_custom_call" | custom-call | tf_op jit(solution)/shard_map/backward/pallas_call | solution.py:926
  191.9 0.0 copy-start.3
  191.9 1.4 slice.21
  193.2 1.5 slice_reduce_fusion
  194.8 0.7 slice.20
  195.5 0.6 reshape.43
  196.1 1.6 convert_bitcast_fusion.2
  197.8 0.0 copy-start.2
  197.8 2.0 %convert_bitcast_fusion.1 = f32[192,3,384]{2,0,1:T(8,128)} fusion(bf16[3,192,384]{2,1,0:T(8,128)(2,1)} %get-tuple-element.38), kind=kLoop, calls=%fused_computation.1 | loop fusion | flops 221184 | bytes 1327104 | tf_op jit(solution)/shard_map/transpose | solution.py:1265
  199.8 0.0 copy-done.3
  199.8 0.0 copy-start.1
  199.8 1.1 convert_element_type.2
  201.0 0.0 copy-done.2
  201.0 0.0 copy-start
  201.0 1.1 convert_bitcast_fusion
  202.1 0.0 copy-done.1
  202.1 0.9 copy.27
  203.0 0.0 copy-done
  203.0 1.1 copy.28
Async XLA Ops:
  191.9 7.9 %copy-start.3 = (bf16[192,1536]{1,0:T(8,128)(2,1)S(1)}, bf16[192,1536]{1,0:T(8,128)(2,1)}, u32[]{:S(2)}) copy-start(bf16[192,1536]{1,0:T(8,128)(2,1)} %get-tuple-element.40) | copy-start | bytes 1769476
  197.8 3.2 %copy-start.2 = (bf16[192,1536]{1,0:T(8,128)(2,1)S(1)}, bf16[192,1536]{1,0:T(8,128)(2,1)}, u32[]{:S(2)}) copy-start(bf16[192,1536]{1,0:T(8,128)(2,1)} %get-tuple-element.41) | copy-start | bytes 1769476
  199.8 2.3 %copy-start.1 = (bf16[2,256,768]{2,1,0:T(8,128)(2,1)S(1)}, bf16[2,256,768]{2,1,0:T(8,128)(2,1)}, u32[]{:S(2)}) copy-start(bf16[2,256,768]{2,1,0:T(8,128)(2,1)} %get-tuple-element.58) | copy-start | bytes 2359300
  201.0 2.0 copy-start

commit v3 on v0

--- a/solution.py
+++ b/solution.py
@@ -1,6 +1,8 @@
 import jax
 import jax.numpy as jnp
 from jax import lax
+from jax.experimental import pallas as pl
+from jax.experimental.pallas import tpu as pltpu
 from jax.sharding import PartitionSpec as P
 
 HD = 64
@@ -53,6 +55,883 @@
     )
     score_grad = (probs_full * (prob_grad - delta_part)).astype(jnp.bfloat16)
     return (probs_full, prob_grad, score_grad)
+
+
+def norm_rows(x, gain, bias):
+    centred = x - jnp.mean(x, axis=-1, keepdims=True)
+    recip = lax.rsqrt(jnp.mean(centred * centred, axis=-1, keepdims=True) + EPSILON)
+    normed = centred * recip
+    return normed * gain + bias, normed, recip
+
+
+BF = jnp.bfloat16
+F32 = jnp.float32
+MESH = pl.DeviceIdType.MESH
+ANY = pl.BlockSpec(memory_space=pl.ANY)
+VMEM = pl.BlockSpec(memory_space=pltpu.VMEM)
+SMEM = pl.BlockSpec(memory_space=pltpu.SMEM)
+CUTS = (2, 2, 1, 2)
+DOWN, UP, OUT, QKV = range(4)
+
+
+def mm(left, right, left_dim, right_dim):
+    return lax.dot_general(
+        left, right, (((left_dim,), (right_dim,)), ((), ())), preferred_element_type=F32
+    )
+
+
+def remote(source, target, send_sem, recv_sem, device):
+    return pltpu.make_async_remote_copy(
+        src_ref=source,
+        dst_ref=target,
+        send_sem=send_sem,
+        recv_sem=recv_sem,
+        device_id=device,
+        device_id_type=MESH,
+    )
+
+
+def span(start, size):
+    return pl.ds(pl.multiple_of(start, 16), size)
+
+
+def lanes_at(start, size):
+    return pl.ds(pl.multiple_of(start, 128), size)
+
+
+def layer_kernel(
+    lens, tok_in, cot_in, wq_in, wo_in, wu_in, wd_in,
+    gain1, bias1, gain2, bias2, taps3, shift3,
+    result, input_grad, down_out, up_out, out_out, q_sum, early_out, late_out,
+    tok, cot, wq_buf, wq, wo, wu, wd, taps, shift, prev,
+    first_all, pre_all, heads, att, attn,
+    low, part_a, part_a_in, part_b, part_b_in, wide_a, middle, middle_grad,
+    second, grad_low, act, up_grad, middle_low, flat, flat_in,
+    g_down, g_up, g_out, g_qkv, near, far_send, far, z_own, z_in, q_own, q_in,
+    key_acc, value_acc, query_t, later, mixed_low, pre_grad, conv_acc,
+    fg_in, fg_low, fg_all, early, early_xy, early_z, late, late_xy, late_z,
+    load_sem, tok_send, tok_recv, pass_send, pass_recv, w_send, w_recv, att_send, att_recv,
+    part_send, part_recv, flat_send, flat_recv,
+    near_send, near_recv, far_ssem, far_recv, z_send, z_recv, q_send, q_recv,
+    fg_ssem, fg_recv, own_send, own_recv, in_send, in_recv, sm_send, sm_recv,
+):
+    f, c, t = lax.axis_index("fsdp"), lax.axis_index("ctx"), lax.axis_index("tp")
+    fx = f + 1 - 2 * lax.rem(f, 2)
+    fy = lax.rem(f + 2, 4)
+    fd = lax.rem(fx + 2, 4)
+    slot = lax.div(c, 2)
+    half = lax.rem(c, 2)
+    other = 1 - t
+    partner = (f, c, other)
+    barrier = pltpu.get_barrier_semaphore()
+    peers = [(fx, c, t), (fy, c, t), (fd, c, t), partner]
+    peers += [(f, lax.rem(c + d, 4), t) for d in (1, 2, 3)]
+    for peer in peers:
+        pl.semaphore_signal(barrier, inc=1, device_id=peer, device_id_type=MESH)
+
+    slots, block_rows, model = tok.shape
+    width = wq.shape[1]
+    part_width = width // 3
+    count = part_width // HD
+    blocks = 4
+    tile = 128
+    tiles = block_rows // tile
+    half_rows = block_rows // 2
+    share = model // 4
+    rows_half = share // 2
+    mine = span(t * half_rows, half_rows)
+    theirs = span(other * half_rows, half_rows)
+
+    def arrived(view, sem):
+        remote(view, view, tok_send.at[0], sem, partner).wait_recv()
+
+    wholes = [wd, wu, wo, wq]
+    shard_rows = span(f * share, share)
+    loads = {}
+    for at, (name, source, target) in enumerate(
+        [
+            ("wq", wq_in, wq_buf),
+            ("tok", tok_in, tok),
+            (OUT, wo_in, wo.at[shard_rows]),
+            (UP, wu_in, wu.at[shard_rows]),
+            (DOWN, wd_in, wd.at[shard_rows]),
+            ("cot", cot_in, cot),
+        ]
+    ):
+        loads[name] = pltpu.make_async_copy(source, target, load_sem.at[at])
+        loads[name].start()
+    pl.semaphore_wait(barrier, len(peers))
+
+    def tok_copy(d):
+        target = lax.rem(c + d, 4)
+        return remote(
+            tok_in.at[lax.div(target, 2), mine],
+            first_all.at[c, mine],
+            tok_send.at[d],
+            tok_recv.at[d],
+            (f, target, t),
+        )
+
+    def tok_pass(source, d):
+        view = first_all.at[source, mine]
+        return remote(view, view, pass_send.at[d], pass_recv.at[d], partner)
+
+    for d in (1, 3, 2):
+        tok_copy(d).start()
+
+    def shard_part(owner, kind):
+        if kind < 2:
+            return span(owner * share, share)
+        return span(owner * share + (kind - 2) * rows_half, rows_half)
+
+    def direct(w, kind):
+        view = wholes[w].at[shard_rows]
+        target = (fx, c, t) if kind == 0 else (fy, c, t)
+        return remote(view, view, w_send.at[w, kind], w_recv.at[w, kind], target)
+
+    def relay(w, kind):
+        origin, target = (fx, (fy, c, t)) if kind == 2 else (fy, (fx, c, t))
+        view = wholes[w].at[shard_part(origin, kind)]
+        return remote(view, view, w_send.at[w, kind], w_recv.at[w, kind], target)
+
+    def landed(w, kind):
+        owner = (fx, fy, fd, fd)[kind]
+        arrived(wholes[w].at[shard_part(owner, kind)], w_recv.at[w, kind])
+
+    def send_direct(w):
+        direct(w, 0).start()
+        direct(w, 1).start()
+
+    def pass_on(w):
+        landed(w, 0)
+        relay(w, 2).start()
+        landed(w, 1)
+        relay(w, 3).start()
+
+    loads["wq"].wait()
+    for h in (0, 1):
+
+        @pl.when(half == h)
+        def _():
+            lanes = slice(h * part_width, (h + 1) * part_width)
+            for kind in range(3):
+                target = slice(kind * part_width, (kind + 1) * part_width)
+                wq[shard_rows, target] = wq_buf[kind, :, lanes]
+                shift[0:1, target] = shift3[kind : kind + 1, lanes]
+                for tap in range(3):
+                    taps[tap : tap + 1, target] = taps3[tap, kind : kind + 1, lanes]
+
+    send_direct(QKV)
+    loads[OUT].wait()
+    send_direct(OUT)
+
+    def first_norm(x):
+        return norm_rows(x.astype(F32), gain1[...], bias1[...])[0].astype(BF)
+
+    loads["tok"].wait()
+    first_all[c] = first_norm(tok[slot])
+    loads[UP].wait()
+    pass_on(QKV)
+    send_direct(UP)
+    end = lax.div(c, 3)
+    start = lax.div(3 - c, 3)
+    for d in (1 + 2 * start, 3 - start - end, 2 - start + end):
+        source = lax.rem(c - d + 4, 4)
+        arrived(first_all.at[source, mine], tok_recv.at[d])
+        first_all[source, mine, :] = first_norm(first_all[source, mine, :])
+        tok_pass(source, d).start()
+
+    pass_on(OUT)
+    for d in (1 + 2 * start, 3 - start - end, 2 - start + end):
+        source = lax.rem(c - d + 4, 4)
+        arrived(first_all.at[source, theirs], pass_recv.at[d])
+    landed(QKV, 2)
+    landed(QKV, 3)
+    prev[...] = jnp.zeros_like(prev)
+
+    def project(block, carry):
+        pre = mm(first_all[block], wq[...], 1, 0).astype(BF)
+        pre_all[block] = pre
+        pre = pre.astype(F32)
+        joined = jnp.concatenate([prev[...], pre], axis=0)
+        prev[...] = pre[-8:]
+        out = (
+            shift[0:1]
+            + taps[0:1] * pre
+            + taps[1:2] * pltpu.roll(joined, 1, 0)[8:]
+            + taps[2:3] * pltpu.roll(joined, 2, 0)[8:]
+        ).astype(BF)
+        at = span(block * block_rows, block_rows)
+        for head in range(3 * count):
+            piece = out[:, head * HD : (head + 1) * HD]
+            if head < count:
+                piece = (piece.astype(F32) * SCALING).astype(BF)
+            heads[head, at, :] = piece
+        return carry
+
+    lax.fori_loop(0, blocks, project, 0)
+    length = lens[slot]
+
+    def soft(head, at, keys):
+        query = heads[head, span(at, tile), :]
+        key = heads[count + head, 0:keys, :]
+        scores = mm(query, key, 1, 1)
+        col = lax.broadcasted_iota(jnp.int32, scores.shape, 1)
+        row = at + lax.broadcasted_iota(jnp.int32, (tile, 1), 0)
+        scores = jnp.where(col < jnp.minimum(row + 1, length), scores, MASKED)
+        powers = jnp.exp(scores - jnp.max(scores, axis=-1, keepdims=True))
+        probs = powers * (1.0 / jnp.sum(powers, axis=-1, keepdims=True))
+        return query, key, probs
+
+    def att_copy(block):
+        return remote(
+            att.at[block],
+            attn.at[c],
+            att_send.at[block],
+            att_recv.at[lax.rem(block - c + 4, 4)],
+            (f, block, t),
+        )
+
+    for block in reversed(range(blocks)):
+        keys = (block + 1) * block_rows
+
+        def attend(n, carry, block=block, keys=keys):
+            head, piece = lax.div(n, tiles), lax.rem(n, tiles)
+            _, _, probs = soft(head, block * block_rows + piece * tile, keys)
+            out = mm(probs.astype(BF), heads[2 * count + head, 0:keys, :], 1, 0)
+            att[block, span(head * HD, HD), lanes_at(piece * tile, tile)] = out.T.astype(BF)
+            return carry
+
+        lax.fori_loop(0, count * tiles, attend, 0)
+
+        @pl.when(block != c)
+        def _():
+            att_copy(block).start()
+
+        @pl.when(block == c)
+        def _():
+            attn[c] = att[block]
+
+        if block == 2:
+            pass_on(UP)
+            loads[DOWN].wait()
+            send_direct(DOWN)
+
+    loads["cot"].wait()
+
+    def mask_grad(s, carry):
+        row = c * block_rows + lax.broadcasted_iota(jnp.int32, (block_rows, 1), 0)
+        grad_low[s] = jnp.where(row < lens[s], cot[s].astype(F32), 0.0).astype(BF)
+        return carry
+
+    lax.fori_loop(0, slots, mask_grad, 0)
+
+    def swap(source, target, kind, s):
+        return remote(
+            source.at[s], target.at[s], part_send.at[kind, s], part_recv.at[kind, s], partner
+        )
+
+    for kind in (2, 3):
+        landed(OUT, kind)
+    for d in (1, 2, 3):
+        arrived(attn.at[lax.rem(c - d + 4, 4)], att_recv.at[d])
+
+    def attn_out(s, carry):
+        rows = jnp.concatenate([attn[2 * s], attn[2 * s + 1]], axis=0).T
+        low[s] = rows
+        part_a[s] = mm(rows, wo[...], 1, 1)
+        swap(part_a, part_a_in, 0, s).start()
+        return carry
+
+    lax.fori_loop(0, slots, attn_out, 0)
+    for kind in (2, 3):
+        landed(UP, kind)
+
+    def feed(s, carry):
+        swap(part_a, part_a_in, 0, s).wait()
+        mid = tok[s].astype(F32) + (part_a[s] + part_a_in[s])
+        middle[s] = mid
+        low_out = norm_rows(mid, gain2[...], bias2[...])[0].astype(BF)
+        second[s] = low_out
+        rect = jnp.maximum(mm(low_out, wu[...], 1, 0), 0.0)
+        wide_a[s] = rect
+        act[s] = (rect * rect).astype(BF)
+        return carry
+
+    lax.fori_loop(0, slots, feed, 0)
+
+    def weight_grad(target, left, right):
+        def step(j, carry):
+            at = lanes_at(j * 128, 128)
+            rows = left.shape[0] * left.shape[1]
+            lhs = left[:, :, at].reshape(rows, 128)
+            rhs = right[...].reshape(rows, right.shape[2])
+            target[at, :] = mm(lhs, rhs, 0, 0).astype(BF)
+            return carry
+
+        lax.fori_loop(0, model // 128, step, 0)
+
+    grads = [g_down, g_up, g_out, g_qkv]
+    finals = [down_out, up_out, out_out]
+    inner = lax.rem(lax.div(c + 1, 2), 2)
+    z_outer = 3 * lax.div(c, 2)
+    z_near = jnp.where(c == 0, 1, jnp.where(c == 3, 2, 3 - c))
+
+    def size_of(w):
+        return rows_half // CUTS[w]
+
+    def rows_of(w, owner, side, u):
+        return span(owner * share + side * rows_half + u * size_of(w), size_of(w))
+
+    def cut(w, u):
+        return pl.ds(u * size_of(w), size_of(w))
+
+    def near_copy(w, kind, u):
+        owner = (fx, fd, fy, fd)[kind]
+        return remote(
+            grads[w].at[rows_of(w, owner, kind // 2, u)],
+            near[w].at[kind, cut(w, u)],
+            near_send[w].at[kind, u],
+            near_recv[w].at[kind, u],
+            (fx, c, t) if kind < 2 else (fy, c, t),
+        )
+
+    def far_copy(w, side, u):
+        return remote(
+            far_send[w].at[side, cut(w, u)],
+            far[w].at[side, cut(w, u)],
+            far_ssem[w].at[side, u],
+            far_recv[w].at[side, u],
+            (fy, c, t) if side == 0 else (fx, c, t),
+        )
+
+    def hop_one(w, kinds, u):
+        for kind in kinds:
+            near_copy(w, kind, u).start()
+
+    def hop_two(w, u):
+        for side in (0, 1):
+            kind = 1 + 2 * side
+            near_copy(w, kind, u).wait_recv()
+            owner = fy if side == 0 else fx
+            own = grads[w][rows_of(w, owner, side, u), :].astype(F32)
+            come = near[w][kind, cut(w, u), :].astype(F32)
+            far_send[w][side, cut(w, u), :] = (own + come).astype(BF)
+            far_copy(w, side, u).start()
+
+    def own_sum(w, side, u):
+        near_copy(w, 2 * side, u).wait_recv()
+        far_copy(w, side, u).wait_recv()
+        own = grads[w][rows_of(w, f, side, u), :].astype(F32)
+        return own + near[w][2 * side, cut(w, u), :] + far[w][side, cut(w, u), :]
+
+    def z_rows(w, side, u):
+        return pl.ds(side * rows_half + u * size_of(w), size_of(w))
+
+    def z_copy(w, stage, side, u):
+        view = z_rows(w, side, u)
+        source = (z_own[w], z_own[w], finals[w])[stage].at[view]
+        target = (z_in[w].at[0, view], z_in[w].at[1, view], finals[w].at[view])[stage]
+        return remote(
+            source, target, z_send[w].at[stage, side, u], z_recv[w].at[stage, side, u],
+            (f, (z_near, z_near, z_outer)[stage], t),
+        )
+
+    def z_one(w, u):
+        for side in (0, 1):
+            z_own[w][z_rows(w, side, u), :] = own_sum(w, side, u).astype(BF)
+
+            @pl.when(inner == 0)
+            def _():
+                z_copy(w, 0, side, u).start()
+
+    def z_two(w, u):
+        @pl.when(inner == 1)
+        def _():
+            for side in (0, 1):
+                z_copy(w, 0, side, u).wait_recv()
+                at = z_rows(w, side, u)
+                z_own[w][at, :] = (z_own[w][at, :].astype(F32) + z_in[w][0, at, :]).astype(BF)
+                z_copy(w, 1, side, u).start()
+
+    def z_three(w, u):
+        @pl.when(inner == 1)
+        def _():
+            for side in (0, 1):
+                z_copy(w, 1, side, u).wait_recv()
+                at = z_rows(w, side, u)
+                finals[w][at, :] = (z_own[w][at, :].astype(F32) + z_in[w][1, at, :]).astype(BF)
+                z_copy(w, 2, side, u).start()
+
+    def reduced(w):
+        for u in range(CUTS[w]):
+            for kind in range(4):
+                near_copy(w, kind, u).wait_send()
+            for side in (0, 1):
+                far_copy(w, side, u).wait_send()
+                if w == QKV:
+                    continue
+
+                @pl.when(inner == 1)
+                def _():
+                    z_copy(w, 1, side, u).wait_send()
+                    z_copy(w, 2, side, u).wait_send()
+
+                @pl.when(inner == 0)
+                def _():
+                    z_copy(w, 0, side, u).wait_send()
+                    z_copy(w, 2, side, u).wait_recv()
+
+    pass_on(DOWN)
+    weight_grad(g_down, grad_low, act)
+    hop_one(DOWN, (1, 3), 0)
+    hop_one(DOWN, (1, 3), 1)
+    for kind in (2, 3):
+        landed(DOWN, kind)
+
+    def feed_back(s, carry):
+        grad = (mm(grad_low[s], wd[...], 1, 0) * 2.0 * wide_a[s]).astype(BF)
+        up_grad[s] = grad
+        part_b[s] = mm(grad, wu[...], 1, 1)
+        swap(part_b, part_b_in, 1, s).start()
+        return carry
+
+    lax.fori_loop(0, slots, feed_back, 0)
+    weight_grad(g_up, second, up_grad)
+    hop_two(DOWN, 0)
+    hop_one(DOWN, (0, 2), 0)
+
+    def flat_copy(s, h):
+        return remote(
+            flat.at[s, h], flat_in.at[c], flat_send.at[s, h],
+            flat_recv.at[lax.rem(2 * s + h - c + 4, 4)], (f, 2 * s + h, t),
+        )
+
+    early[0] = jnp.zeros(early.shape[1:], F32)
+    in_half = (
+        lax.div(lax.broadcasted_iota(jnp.int32, (block_rows, 1), 0), half_rows) == t
+    ).astype(F32)
+
+    def norm_two_back(s, carry):
+        swap(part_b, part_b_in, 1, s).wait()
+        grad = part_b[s] + part_b_in[s]
+        _, normed, recip = norm_rows(middle[s], gain2[...], bias2[...])
+        kept = grad * in_half
+        early[0, 0:1, :] += jnp.sum(kept * normed, axis=0, keepdims=True)
+        early[0, 1:2, :] += jnp.sum(kept, axis=0, keepdims=True)
+        back = grad_low[s].astype(F32) + norm_back(grad, normed, recip, gain2[...])
+        middle_grad[s] = back
+        back = back.astype(BF)
+        middle_low[s] = back
+        flat_rows = mm(back, wo[...], 1, 0).T.astype(BF)
+        for h in (0, 1):
+            flat[s, h] = flat_rows[h * part_width : (h + 1) * part_width]
+
+            @pl.when(2 * s + h != c)
+            def _():
+                flat_copy(s, h).start()
+
+            @pl.when(2 * s + h == c)
+            def _():
+                flat_in[c] = flat[s, h]
+
+        return carry
+
+    lax.fori_loop(0, slots, norm_two_back, 0)
+    hop_two(DOWN, 1)
+    hop_one(DOWN, (0, 2), 1)
+    for u in (0, 1):
+        hop_one(UP, (1, 3), u)
+    for u in (0, 1):
+        hop_one(UP, (0, 2), u)
+    weight_grad(g_out, middle_low, low)
+    hop_one(OUT, (1, 3, 0, 2), 0)
+
+    def down(s, carry):
+        part_a[s] = mm(act[s], wd[...], 1, 1)
+        swap(part_a, part_a_in, 2, s).start()
+        return carry
+
+    lax.fori_loop(0, slots, down, 0)
+    key_acc[...] = jnp.zeros_like(key_acc)
+    value_acc[...] = jnp.zeros_like(value_acc)
+    later[...] = jnp.zeros_like(later)
+    conv_acc[...] = jnp.zeros_like(conv_acc)
+    for s in range(slots):
+        swap(part_a, part_a_in, 2, s).wait()
+        result[s] = (middle[s] + (part_a[s] + part_a_in[s])).astype(BF)
+
+    def fg_view(block, rows):
+        return wide_a.at[block // 2, rows, pl.ds(block % 2 * model, model)]
+
+    def own_copy(block):
+        return remote(
+            fg_view(block, theirs), fg_in.at[block], own_send.at[block], own_recv.at[block],
+            partner,
+        )
+
+    def fg_copy(block):
+        return remote(
+            fg_low.at[block], fg_all.at[c], fg_ssem.at[block],
+            fg_recv.at[lax.rem(block - c + 4, 4)], (f, block, t),
+        )
+
+    def hand_over(block):
+        own_copy(block).wait_recv()
+        fg_low[block] = (fg_view(block, mine)[...] + fg_in[block]).astype(BF)
+
+        @pl.when(block != c)
+        def _():
+            fg_copy(block).start()
+
+        @pl.when(block == c)
+        def _():
+            fg_all[c] = fg_low[block]
+
+    z_one(DOWN, 0)
+    for block in reversed(range(blocks)):
+
+        @pl.when(block != c)
+        def _():
+            arrived(flat_in.at[block], flat_recv.at[lax.rem(c - block + 4, 4)])
+
+        keys = (block + 1) * block_rows
+
+        def attend_back(n, carry, block=block, keys=keys):
+            head, piece = lax.div(n, tiles), lax.rem(n, tiles)
+            query, key, probs = soft(head, block * block_rows + piece * tile, keys)
+            lanes = lanes_at(piece * tile, tile)
+            channels = span(head * HD, HD)
+            grad_t = flat_in[block, channels, lanes]
+            prob_grad = mm(grad_t.T, heads[2 * count + head, 0:keys, :], 1, 1)
+            delta = jnp.sum(probs * prob_grad, axis=-1, keepdims=True)
+            score_grad = (probs * (prob_grad - delta)).astype(BF)
+            query_t[channels, lanes] = (mm(score_grad, key, 1, 0) * SCALING).T
+            key_acc[head, :, 0:keys] += mm(query.T, score_grad, 1, 0)
+            value_acc[head, :, 0:keys] += mm(grad_t, probs.astype(BF), 1, 0)
+            return carry
+
+        lax.fori_loop(0, count * tiles, attend_back, 0)
+        columns = slice(block * block_rows, (block + 1) * block_rows)
+        mixed_low[...] = jnp.concatenate(
+            [
+                query_t[...],
+                key_acc[:, :, columns].reshape(part_width, block_rows),
+                value_acc[:, :, columns].reshape(part_width, block_rows),
+            ],
+            axis=0,
+        ).T
+        mixed = mixed_low[...]
+        joined = jnp.concatenate([mixed, later[...]], axis=0)
+        next_one = pltpu.roll(joined, block_rows + 7, 0)[:block_rows]
+        next_two = pltpu.roll(joined, block_rows + 6, 0)[:block_rows]
+        later[...] = mixed[:8]
+        before = pre_all[block].astype(F32)
+        for at, moved in enumerate((mixed, next_one, next_two)):
+            conv_acc[at : at + 1, :] += jnp.sum(before * moved, axis=0, keepdims=True)
+        conv_acc[3:4, :] += jnp.sum(mixed, axis=0, keepdims=True)
+        grad = (taps[0:1] * mixed + taps[1:2] * next_one + taps[2:3] * next_two).astype(BF)
+        pre_grad[block] = grad
+        fg_view(block, pl.ds(0, block_rows))[...] = mm(grad, wq[...], 1, 1)
+        own_copy(block).start()
+        if block == 3:
+            z_one(DOWN, 1)
+            z_two(DOWN, 0)
+        if block == 2:
+            hand_over(3)
+            z_two(DOWN, 1)
+            hop_two(UP, 0)
+            hop_two(UP, 1)
+            z_three(DOWN, 0)
+        if block == 1:
+            hand_over(2)
+            z_three(DOWN, 1)
+            hop_two(OUT, 0)
+        if block == 0:
+            hand_over(1)
+
+    weight_grad(g_qkv, first_all, pre_grad)
+    for u in (0, 1):
+        hop_one(QKV, (1, 3), u)
+    for u in (0, 1):
+        hop_one(QKV, (0, 2), u)
+    hand_over(0)
+
+    smalls = [(early, early_xy, early_z), (late, late_xy, late_z)]
+
+    def tp_copy(k):
+        return remote(
+            smalls[k][0].at[0], smalls[k][0].at[1], sm_send.at[k, 0], sm_recv.at[k, 0], partner
+        )
+
+    def xy_copy(k, at):
+        view = smalls[k][1].at[f]
+        return remote(
+            view, view, sm_send.at[k, 1 + at], sm_recv.at[k, 1 + at], ((fx, fy, fd)[at], c, t)
+        )
+
+    def z_small(k, d):
+        view = smalls[k][2].at[c]
+        return remote(
+            view, view, sm_send.at[k, 3 + d], sm_recv.at[k, 3 + d], (f, lax.rem(c + d, 4), t)
+        )
+
+    def small_tp(k):
+        tp_copy(k).wait()
+        mixed_rows = 2 if k == 0 else smalls[k][0].shape[1]
+        total = smalls[k][0][0] + smalls[k][0][1]
+        smalls[k][1][f] = smalls[k][0][0]
+        smalls[k][1][f, 0:mixed_rows, :] = total[0:mixed_rows]
+        for at in range(3):
+            xy_copy(k, at).start()
+
+    def small_xy(k):
+        for at, owner in enumerate((fx, fy, fd)):
+            xy_copy(k, at).wait_send()
+            arrived(smalls[k][1].at[owner], sm_recv.at[k, 1 + at])
+        own = smalls[k][1]
+        smalls[k][2][c] = own[0] + own[1] + own[2] + own[3]
+        for d in (1, 2, 3):
+            z_small(k, d).start()
+
+    def small_z(k, out):
+        for d in (1, 2, 3):
+            z_small(k, d).wait_send()
+            arrived(smalls[k][2].at[lax.rem(c - d + 4, 4)], sm_recv.at[k, 3 + d])
+        own = smalls[k][2]
+        out[...] = own[0] + own[1] + own[2] + own[3]
+
+    for h in (0, 1):
+
+        @pl.when(half == h)
+        def _():
+            lanes = slice(h * part_width, (h + 1) * part_width)
+            for kind in range(3):
+                channels = slice(kind * part_width, (kind + 1) * part_width)
+                for tap in range(4):
+                    row = 2 + 3 * tap + kind
+                    early[0, row : row + 1, lanes] = conv_acc[tap : tap + 1, channels]
+
+    tp_copy(0).start()
+    z_one(UP, 0)
+    z_one(UP, 1)
+    small_tp(0)
+    z_one(OUT, 0)
+    hop_two(QKV, 0)
+    z_two(UP, 0)
+    hop_two(QKV, 1)
+    z_two(UP, 1)
+    z_two(OUT, 0)
+    small_xy(0)
+
+    def q_copy(stage, side, u):
+        view = z_rows(QKV, side, u)
+        if stage == 0:
+            source, target, device = q_own.at[view], q_in.at[view], lax.rem(c + 2, 4)
+        else:
+            source = target = q_sum.at[half, view]
+            device = c + 1 - 2 * half
+        return remote(
+            source, target, q_send.at[stage, side, u], q_recv.at[stage, side, u], (f, device, t)
+        )
+
+    def q_one(u):
+        for side in (0, 1):
+            q_own[z_rows(QKV, side, u), :] = own_sum(QKV, side, u).astype(BF)
+            q_copy(0, side, u).start()
+
+    def q_two(u):
+        for side in (0, 1):
+            q_copy(0, side, u).wait()
+            at = z_rows(QKV, side, u)
+            q_sum[half, at, :] = (q_own[at, :].astype(F32) + q_in[at, :]).astype(BF)
+            q_copy(1, side, u).start()
+
+    for d in (1, 2, 3):
+        arrived(fg_all.at[lax.rem(c - d + 4, 4)], fg_recv.at[d])
+    late[0] = jnp.zeros(late.shape[1:], F32)
+    lane = late.shape[2]
+
+    def in_copy(s):
+        view = input_grad.at[s, mine]
+        return remote(view, view, in_send.at[s], in_recv.at[s], partner)
+
+    for s in range(slots):
+        grad = fg_all[2 * s].astype(F32) + fg_all[2 * s + 1]
+        rows = tok[s, mine, :].astype(F32)
+        _, normed, recip = norm_rows(rows, gain1[...], bias1[...])
+        gain_sum = jnp.sum(grad * normed, axis=0, keepdims=True)
+        bias_sum = jnp.sum(grad, axis=0, keepdims=True)
+        for at in range(model // lane):
+            lanes = slice(at * lane, (at + 1) * lane)
+            late[0, at : at + 1, :] += gain_sum[:, lanes]
+            late[0, 4 + at : 5 + at, :] += bias_sum[:, lanes]
+        input_grad[s, mine, :] = middle_grad[s, mine, :] + norm_back(
+            grad, normed, recip, gain1[...]
+        )
+        in_copy(s).start()
+
+    tp_copy(1).start()
+    q_one(0)
+    small_tp(1)
+    z_three(UP, 0)
+    q_one(1)
+    z_three(UP, 1)
+    small_xy(1)
+    z_three(OUT, 0)
+    small_z(0, early_out)
+    q_two(0)
+    q_two(1)
+    small_z(1, late_out)
+
+    for w in range(4):
+        reduced(w)
+        for kind in (0, 1):
+            direct(w, kind).wait_send()
+        for kind in (2, 3):
+            relay(w, kind).wait_send()
+    for side in (0, 1):
+        for u in (0, 1):
+            q_copy(1, side, u).wait_send()
+            arrived(q_sum.at[1 - half, z_rows(QKV, side, u)], q_recv.at[1, side, u])
+    for d in (1, 2, 3):
+        tok_copy(d).wait_send()
+        tok_pass(lax.rem(c - d + 4, 4), d).wait_send()
+    for s in range(slots):
+        in_copy(s).wait_send()
+        arrived(input_grad.at[s, theirs], in_recv.at[s])
+        for h in (0, 1):
+
+            @pl.when(2 * s + h != c)
+            def _():
+                flat_copy(s, h).wait_send()
+
+    for block in range(blocks):
+        own_copy(block).wait_send()
+
+        @pl.when(block != c)
+        def _():
+            att_copy(block).wait_send()
+            fg_copy(block).wait_send()
+
+
+def layer_call(
+    lens, tok, cot, wq3, wo, wu, wd, gain1, bias1, gain2, bias2, taps3, shift3
+):
+    slots, block_rows, model = tok.shape
+    share, units, channels = wu.shape[0], wu.shape[1], wo.shape[1]
+    part = channels // 2
+    width = 3 * part
+    blocks = 4
+    tall = (slots, block_rows, model)
+    wide = (slots, block_rows, units)
+    half = block_rows // 2
+    columns = [units, units, channels, width]
+    dma = pltpu.SemaphoreType.DMA
+
+    def vmem(shape, kind=BF):
+        return pltpu.VMEM(tuple(shape), kind)
+
+    def struct(shape, kind=BF):
+        return jax.ShapeDtypeStruct(tuple(shape), kind)
+
+    return pl.pallas_call(
+        layer_kernel,
+        name="layer",
+        out_shape=[
+            struct(tall), struct(tall, F32), struct((share, units)), struct((share, units)),
+            struct((share, channels)), struct((2, share, width)), struct((16, model), F32),
+            struct((8, 256), F32),
+        ],
+        in_specs=[SMEM] + [ANY] * 6 + [VMEM] * 6,
+        out_specs=[VMEM] * 8,
+        scratch_shapes=[
+            vmem(tall), vmem(tall), vmem(wq3.shape), vmem((model, width)),
+            vmem((model, channels)), vmem((model, units)), vmem((model, units)),
+            vmem((8, width), F32), vmem((8, width), F32), vmem((8, width), F32),
+            vmem((blocks, block_rows, model)), vmem((blocks, block_rows, width)),
+            vmem((width // HD, blocks * block_rows, HD)),
+            vmem((blocks, part, block_rows)), vmem((blocks, part, block_rows)),
+            vmem((slots, block_rows, channels)), vmem(tall, F32), vmem(tall, F32),
+            vmem(tall, F32), vmem(tall, F32), vmem(wide, F32), vmem(tall, F32), vmem(tall, F32),
+            vmem(tall), vmem(tall), vmem(wide), vmem(wide), vmem(tall),
+            vmem((slots, 2, part, block_rows)), vmem((4, part, block_rows)),
+            vmem((model, units)), vmem((model, units)), vmem((model, channels)),
+            vmem((model, width)),
+            [vmem((4, share // 2, n)) for n in columns],
+            [vmem((2, share // 2, n)) for n in columns],
+            [vmem((2, share // 2, n)) for n in columns],
+            [vmem((share, n)) for n in columns[:3]],
+            [vmem((2, share, n)) for n in columns[:3]],
+            vmem((share, width)), vmem((share, width)),
+            vmem((part // HD, HD, blocks * block_rows), F32),
+            vmem((part // HD, HD, blocks * block_rows), F32),
+            vmem((part, block_rows), F32), vmem((8, width), F32),
+            vmem((block_rows, width), F32), vmem((blocks, block_rows, width)),
+            vmem((8, width), F32),
+            vmem((blocks, half, model), F32), vmem((blocks, half, model)),
+            vmem((blocks, half, model)),
+            vmem((2, 16, model), F32), vmem((4, 16, model), F32), vmem((4, 16, model), F32),
+            vmem((2, 8, 256), F32), vmem((4, 8, 256), F32), vmem((4, 8, 256), F32),
+            dma((6,)), dma((4,)), dma((4,)), dma((4,)), dma((4,)), dma((4, 4)), dma((4, 4)),
+            dma((4,)), dma((4,)),
+            dma((3, slots)), dma((3, slots)), dma((slots, 2)), dma((4,)),
+            [dma((4, n)) for n in CUTS], [dma((4, n)) for n in CUTS],
+            [dma((2, n)) for n in CUTS], [dma((2, n)) for n in CUTS],
+            [dma((3, 2, n)) for n in CUTS[:3]], [dma((3, 2, n)) for n in CUTS[:3]],
+            dma((2, 2, 2)), dma((2, 2, 2)),
+            dma((4,)), dma((4,)), dma((4,)), dma((4,)), dma((slots,)), dma((slots,)),
+            dma((2, 7)), dma((2, 7)),
+        ],
+        compiler_params=pltpu.CompilerParams(
+            collective_id=0, has_side_effects=True, vmem_limit_bytes=67043328
+        ),
+    )(lens, tok, cot, wq3, wo, wu, wd, gain1, bias1, gain2, bias2, taps3, shift3)
+
+
+def finish_kernel(
+    result_in, grad_in, down_in, up_in, out_in, qkv_in, early, late,
+    result, grad, gain1, bias1, qkv, taps, shift, out, gain2, bias2, up, down,
+):
+    result[...] = result_in[...]
+    grad[...] = grad_in[...]
+    down[...] = down_in[...].astype(F32)
+    up[...] = up_in[...].astype(F32)
+    out[...] = out_in[...].astype(F32)
+    part = qkv_in.shape[2] // 3
+    for kind in range(3):
+        for h in (0, 1):
+            qkv[kind, :, h * part : (h + 1) * part] = qkv_in[
+                h, :, kind * part : (kind + 1) * part
+            ].astype(F32)
+    lane = late.shape[1]
+    for at in range(gain1.shape[0] // lane):
+        lanes = slice(at * lane, (at + 1) * lane)
+        gain1[lanes] = late[at]
+        bias1[lanes] = late[4 + at]
+    gain2[...] = early[0]
+    bias2[...] = early[1]
+    for tap in range(3):
+        taps[tap] = early[2 + 3 * tap : 5 + 3 * tap, 0 : 2 * part]
+    shift[...] = early[11:14, 0 : 2 * part]
+
+
+def finish_call(result, grad, down, up, out, qkv, early, late):
+    channels, share, model = out.shape[1], out.shape[0], result.shape[2]
+
+    def struct(shape, kind=F32):
+        return jax.ShapeDtypeStruct(tuple(shape), kind)
+
+    vector = struct((model,))
+    return pl.pallas_call(
+        finish_kernel,
+        name="finish",
+        out_shape=[
+            struct(result.shape, BF), struct(grad.shape), vector, vector,
+            struct((3, share, channels)), struct((3, 3, channels)), struct((3, channels)),
+            struct(out.shape), vector, vector, struct(up.shape), struct(down.shape),
+        ],
+    )(result, grad, down, up, out, qkv, early, late)
 
 
 def local(
@@ -308,6 +1187,32 @@
     )
 
 
+def local_fast(
+    tokens,
+    lengths,
+    cotangent,
+    ln1_gain,
+    ln1_bias,
+    qkv_weight,
+    conv_kernel,
+    conv_bias,
+    out_weight,
+    ln2_gain,
+    ln2_bias,
+    up_weight,
+    down_weight,
+):
+    parts = layer_call(
+        lengths, tokens, cotangent, qkv_weight.transpose(1, 0, 2), out_weight.T, up_weight,
+        down_weight.T, ln1_gain, ln1_bias, ln2_gain, ln2_bias, conv_kernel, conv_bias,
+    )
+    result, grad, gain1, bias1, qkv, taps, shift, out, gain2, bias2, up, down = finish_call(*parts)
+    return (
+        result, grad, gain1, bias1, qkv.transpose(1, 0, 2), taps, shift, out.T, gain2, bias2, up,
+        down.T,
+    )
+
+
 def solution(mesh):
     placed = (
         P("fsdp", "ctx", None),
@@ -324,8 +1229,9 @@
         P("fsdp", "tp"),
         P("tp", "fsdp"),
     )
+    ctx, fsdp, tp = mesh.shape["ctx"], mesh.shape["fsdp"], mesh.shape["tp"]
     return jax.shard_map(
-        local,
+        local_fast if (fsdp, ctx, tp) == (4, 4, 2) else local,
         mesh=mesh,
         in_specs=placed,
         out_specs=(

time: 914 us -> 180 us (0.20)
  waiting for transfers between devices: 640 us -> 0 us
  Pallas kernels: 0 us -> 180 us
  blocking collectives: 93 us -> 0 us
  matrix products: 85.2 us -> 0 us
  other arithmetic: 36.6 us -> 0 us
  local copies, waits for them, and re-layouts: 29.8 us -> 0 us
  between operations: 14.8 us -> 0.66 us
    psum x4 -> x0, waiting for transfers between devices: 366 us -> none  [the longest x1 320 us: local(): lax.psum((qkv_wgrad, out_wgrad, up_wgrad, down_wgrad, gain_one_grad, bias...]
    pallas_call x0 -> x2, Pallas kernels: none -> 180 us  [the longest x1 175 us: layer_call(): pl.pallas_call(layer_kernel, name='layer', out_shape=[struct(tall), struc...]
    all_gather x4 -> x0, waiting for transfers between devices: 160 us -> none  [the longest x1 53.2 us: local(): whole_pairs = lax.all_gather(own_pairs, 'ctx', axis=1, tiled=True)]
    reduce_scatter x1 -> x0, waiting for transfers between devices: 112 us -> none  [local(): lax.psum_scatter(pair_terms, 'ctx', scatter_dimension=1, tiled=True)]
    dot_general x21 -> x0, matrix products: 85.2 us -> none  [the longest x3 15.1 us: tile_scores(): jnp.einsum('mqhd,mkhd->mhqk', query_part, key_part, preferred_element_typ...]
    psum x1 -> x0, blocking collectives: 82 us -> none  [local(): lax.psum((qkv_wgrad, out_wgrad, up_wgrad, down_wgrad, gain_one_grad, bias...]
    reduce_sum x8 -> x0, other arithmetic: 17.1 us -> none  [the longest x1 4.61 us: local(): jnp.sum(extended[:, 2 - offset:2 - offset + block_rows] * mixed_grad, axi...]
    all_gather x1 -> x0, blocking collectives: 11 us -> none  [local(): lax.all_gather(out_weight, 'fsdp', axis=1, tiled=True)]
  transfers between devices with their start and end apart: 11 -> 0, of which waited for: 10 -> 0; matrix products, arithmetic and copies ran while one was open for 4% -> 0% of each run, Pallas kernels for 0% -> 0%
where the time goes in v3:
time: 180 us
  Pallas kernels  180 us (100%)
    pallas_call x1, Pallas kernels, layer_call(): pl.pallas_call(layer_kernel, name='layer', out_shape=[struct(tall), struc...  175 us
    pallas_call x1, Pallas kernels, finish_call(): pl.pallas_call(finish_kernel, name='finish', out_shape=[struct(result.sha...  4.98 us

profile of v3, /device:TPU:0, one launch (start us, length us, event | category | flops | bytes accessed | tf_op | source)
XLA Modules:
  0.0 180.2 jit_solution(5445051135195300427)
XLA Ops:
  0.6 174.6 %layer.1 = (bf16[2,256,768]{2,1,0:T(8,128)(2,1)}, f32[2,256,768]{2,1,0:T(8,128)}, bf16[192,1536]{1,0:T(8,128)(2,1)}, bf16[192,1536]{1,0:T(8,128)(2,1)}, bf16[192...) custom-call(s32[2]{0:T(128)} %lens.1, bf16[2,256,768]{2,1,0:T(8,128)(2,1)} %tok_in.1, ...), custom_call_target="tpu_custom_call" | custom-call | tf_op jit(solution)/shard_map/layer/pallas_call | solution.py:838
  175.2 5.0 %finish.1 = (bf16[2,256,768]{2,1,0:T(8,128)(2,1)}, f32[2,256,768]{2,1,0:T(8,128)}, f32[768]{0:T(1024)}, f32[768]{0:T(1024)}, f32[3,192,384]{2,1,0:T(8,128)}, /*i...) custom-call(bf16[2,256,768]{2,1,0:T(8,128)(2,1)} %get-tuple-element., ...), custom_call_target="tpu_custom_call" | custom-call | tf_op jit(solution)/shard_map/finish/pallas_call | solution.py:926

commit v4 on v3

--- a/solution.py
+++ b/solution.py
@@ -108,12 +108,12 @@
     low, part_a, part_a_in, part_b, part_b_in, wide_a, middle, middle_grad,
     second, grad_low, act, up_grad, middle_low, flat, flat_in,
     g_down, g_up, g_out, g_qkv, near, far_send, far, z_own, z_in, q_own, q_in,
-    key_acc, value_acc, query_t, later, mixed_low, pre_grad, conv_acc,
-    fg_in, fg_low, fg_all, early, early_xy, early_z, late, late_xy, late_z,
+    key_bias, key_acc, value_acc, query_t, later, mixed_low, pre_grad, conv_acc,
+    fg_in, fg_low, pair_in, fg_own, fg_other, early, early_xy, early_z, late, late_xy, late_z,
     load_sem, tok_send, tok_recv, pass_send, pass_recv, w_send, w_recv, att_send, att_recv,
     part_send, part_recv, flat_send, flat_recv,
     near_send, near_recv, far_ssem, far_recv, z_send, z_recv, q_send, q_recv,
-    fg_ssem, fg_recv, own_send, own_recv, in_send, in_recv, sm_send, sm_recv,
+    fg_ssem, fg_recv, pair_send, pair_recv, own_send, own_recv, in_send, in_recv, sm_send, sm_recv,
 ):
     f, c, t = lax.axis_index("fsdp"), lax.axis_index("ctx"), lax.axis_index("tp")
     fx = f + 1 - 2 * lax.rem(f, 2)
@@ -134,8 +134,6 @@
     part_width = width // 3
     count = part_width // HD
     blocks = 4
-    tile = 128
-    tiles = block_rows // tile
     half_rows = block_rows // 2
     share = model // 4
     rows_half = share // 2
@@ -162,22 +160,36 @@
         loads[name].start()
     pl.semaphore_wait(barrier, len(peers))
 
-    def tok_copy(d):
-        target = lax.rem(c + d, 4)
-        return remote(
-            tok_in.at[lax.div(target, 2), mine],
+    inner = lax.rem(lax.div(c + 1, 2), 2)
+    mate = c + 1 - 2 * half
+    across = 2 - slot
+    far_side = 3 - 3 * slot
+
+    def tok_copy(k):
+        return remote(
+            tok_in.at[slot if k == 0 else 1 - slot, mine],
             first_all.at[c, mine],
-            tok_send.at[d],
-            tok_recv.at[d],
-            (f, target, t),
-        )
-
-    def tok_pass(source, d):
-        view = first_all.at[source, mine]
-        return remote(view, view, pass_send.at[d], pass_recv.at[d], partner)
-
-    for d in (1, 3, 2):
-        tok_copy(d).start()
+            tok_send.at[k],
+            tok_recv.at[c],
+            (f, mate if k == 0 else across, t),
+        )
+
+    def tok_order(k):
+        near_in, near_out = ((across, mate), (far_side, across), (mate, far_side))[k]
+        return inner * near_in + (1 - inner) * near_out
+
+    def tok_relay(k):
+        view = first_all.at[tok_order(k), mine]
+        return remote(
+            view, view, tok_send.at[2 + k], tok_recv.at[tok_order(k)], (f, mate, t)
+        )
+
+    def tok_pass(k):
+        view = first_all.at[tok_order(k), mine]
+        return remote(view, view, pass_send.at[k], pass_recv.at[k], partner)
+
+    for k in (0, 1):
+        tok_copy(k).start()
 
     def shard_part(owner, kind):
         if kind < 2:
@@ -221,33 +233,43 @@
                 for tap in range(3):
                     taps[tap : tap + 1, target] = taps3[tap, kind : kind + 1, lanes]
 
-    send_direct(QKV)
-    loads[OUT].wait()
-    send_direct(OUT)
-
     def first_norm(x):
         return norm_rows(x.astype(F32), gain1[...], bias1[...])[0].astype(BF)
 
-    loads["tok"].wait()
-    first_all[c] = first_norm(tok[slot])
-    loads[UP].wait()
-    pass_on(QKV)
-    send_direct(UP)
-    end = lax.div(c, 3)
-    start = lax.div(3 - c, 3)
-    for d in (1 + 2 * start, 3 - start - end, 2 - start + end):
-        source = lax.rem(c - d + 4, 4)
-        arrived(first_all.at[source, mine], tok_recv.at[d])
-        first_all[source, mine, :] = first_norm(first_all[source, mine, :])
-        tok_pass(source, d).start()
-
-    pass_on(OUT)
-    for d in (1 + 2 * start, 3 - start - end, 2 - start + end):
-        source = lax.rem(c - d + 4, 4)
-        arrived(first_all.at[source, theirs], pass_recv.at[d])
-    landed(QKV, 2)
-    landed(QKV, 3)
-    prev[...] = jnp.zeros_like(prev)
+    def own_norm():
+        loads["tok"].wait()
+        first_all[c] = first_norm(tok[slot])
+
+    def tokens():
+        for k in range(3):
+            source = tok_order(k)
+            arrived(first_all.at[source, mine], tok_recv.at[source])
+
+            @pl.when((inner == 1) | (k == 0))
+            def _():
+                first_all[source, mine, :] = first_norm(first_all[source, mine, :])
+
+            if k < 2:
+
+                @pl.when(inner == 1)
+                def _():
+                    tok_relay(k).start()
+
+            tok_pass(k).start()
+        for k in range(3):
+            arrived(first_all.at[tok_order(k), theirs], pass_recv.at[k])
+
+    def send_out():
+        loads[OUT].wait()
+        send_direct(OUT)
+
+    def send_up():
+        loads[UP].wait()
+        send_direct(UP)
+
+    def send_down():
+        loads[DOWN].wait()
+        send_direct(DOWN)
 
     def project(block, carry):
         pre = mm(first_all[block], wq[...], 1, 0).astype(BF)
@@ -269,16 +291,23 @@
             heads[head, at, :] = piece
         return carry
 
-    lax.fori_loop(0, blocks, project, 0)
-    length = lens[slot]
-
-    def soft(head, at, keys):
-        query = heads[head, span(at, tile), :]
-        key = heads[count + head, 0:keys, :]
-        scores = mm(query, key, 1, 1)
-        col = lax.broadcasted_iota(jnp.int32, scores.shape, 1)
-        row = at + lax.broadcasted_iota(jnp.int32, (tile, 1), 0)
-        scores = jnp.where(col < jnp.minimum(row + 1, length), scores, MASKED)
+    def projections():
+        landed(QKV, 2)
+        landed(QKV, 3)
+        prev[...] = jnp.zeros_like(prev)
+        lax.fori_loop(0, blocks, project, 0)
+        at = lax.broadcasted_iota(jnp.int32, key_bias.shape, 1)
+        key_bias[...] = jnp.where(at < lens[slot], 0.0, MASKED)
+
+    def soft(head, block):
+        at = block * block_rows
+        query = heads[head, at : at + block_rows, :]
+        key = heads[count + head, 0 : at + block_rows, :]
+        scores = mm(query, key, 1, 1) + key_bias[0:1, 0 : at + block_rows]
+        col = lax.broadcasted_iota(jnp.int32, (block_rows, block_rows), 1)
+        row = lax.broadcasted_iota(jnp.int32, (block_rows, 1), 0)
+        last = jnp.where(col <= row, scores[:, at:], MASKED)
+        scores = jnp.concatenate([scores[:, :at], last], axis=1) if block else last
         powers = jnp.exp(scores - jnp.max(scores, axis=-1, keepdims=True))
         probs = powers * (1.0 / jnp.sum(powers, axis=-1, keepdims=True))
         return query, key, probs
@@ -292,17 +321,16 @@
             (f, block, t),
         )
 
-    for block in reversed(range(blocks)):
+    def attention(block):
         keys = (block + 1) * block_rows
 
-        def attend(n, carry, block=block, keys=keys):
-            head, piece = lax.div(n, tiles), lax.rem(n, tiles)
-            _, _, probs = soft(head, block * block_rows + piece * tile, keys)
+        def attend(head, carry, block=block, keys=keys):
+            _, _, probs = soft(head, block)
             out = mm(probs.astype(BF), heads[2 * count + head, 0:keys, :], 1, 0)
-            att[block, span(head * HD, HD), lanes_at(piece * tile, tile)] = out.T.astype(BF)
+            att[block, span(head * HD, HD), :] = out.T.astype(BF)
             return carry
 
-        lax.fori_loop(0, count * tiles, attend, 0)
+        lax.fori_loop(0, count, attend, 0)
 
         @pl.when(block != c)
         def _():
@@ -311,30 +339,20 @@
         @pl.when(block == c)
         def _():
             attn[c] = att[block]
-
-        if block == 2:
-            pass_on(UP)
-            loads[DOWN].wait()
-            send_direct(DOWN)
-
-    loads["cot"].wait()
 
     def mask_grad(s, carry):
         row = c * block_rows + lax.broadcasted_iota(jnp.int32, (block_rows, 1), 0)
         grad_low[s] = jnp.where(row < lens[s], cot[s].astype(F32), 0.0).astype(BF)
         return carry
 
-    lax.fori_loop(0, slots, mask_grad, 0)
+    def masks():
+        loads["cot"].wait()
+        lax.fori_loop(0, slots, mask_grad, 0)
 
     def swap(source, target, kind, s):
         return remote(
             source.at[s], target.at[s], part_send.at[kind, s], part_recv.at[kind, s], partner
         )
-
-    for kind in (2, 3):
-        landed(OUT, kind)
-    for d in (1, 2, 3):
-        arrived(attn.at[lax.rem(c - d + 4, 4)], att_recv.at[d])
 
     def attn_out(s, carry):
         rows = jnp.concatenate([attn[2 * s], attn[2 * s + 1]], axis=0).T
@@ -343,9 +361,12 @@
         swap(part_a, part_a_in, 0, s).start()
         return carry
 
-    lax.fori_loop(0, slots, attn_out, 0)
-    for kind in (2, 3):
-        landed(UP, kind)
+    def out_projection():
+        for kind in (2, 3):
+            landed(OUT, kind)
+        for d in (1, 2, 3):
+            arrived(attn.at[lax.rem(c - d + 4, 4)], att_recv.at[d])
+        lax.fori_loop(0, slots, attn_out, 0)
 
     def feed(s, carry):
         swap(part_a, part_a_in, 0, s).wait()
@@ -358,7 +379,10 @@
         act[s] = (rect * rect).astype(BF)
         return carry
 
-    lax.fori_loop(0, slots, feed, 0)
+    def feed_forward():
+        for kind in (2, 3):
+            landed(UP, kind)
+        lax.fori_loop(0, slots, feed, 0)
 
     def weight_grad(target, left, right):
         def step(j, carry):
@@ -373,7 +397,6 @@
 
     grads = [g_down, g_up, g_out, g_qkv]
     finals = [down_out, up_out, out_out]
-    inner = lax.rem(lax.div(c + 1, 2), 2)
     z_outer = 3 * lax.div(c, 2)
     z_near = jnp.where(c == 0, 1, jnp.where(c == 3, 2, 3 - c))
 
@@ -482,24 +505,14 @@
                     z_copy(w, 0, side, u).wait_send()
                     z_copy(w, 2, side, u).wait_recv()
 
-    pass_on(DOWN)
-    weight_grad(g_down, grad_low, act)
-    hop_one(DOWN, (1, 3), 0)
-    hop_one(DOWN, (1, 3), 1)
-    for kind in (2, 3):
-        landed(DOWN, kind)
-
-    def feed_back(s, carry):
+    def feed_back(s):
+        if s == 0:
+            for kind in (2, 3):
+                landed(DOWN, kind)
         grad = (mm(grad_low[s], wd[...], 1, 0) * 2.0 * wide_a[s]).astype(BF)
         up_grad[s] = grad
         part_b[s] = mm(grad, wu[...], 1, 1)
         swap(part_b, part_b_in, 1, s).start()
-        return carry
-
-    lax.fori_loop(0, slots, feed_back, 0)
-    weight_grad(g_up, second, up_grad)
-    hop_two(DOWN, 0)
-    hop_one(DOWN, (0, 2), 0)
 
     def flat_copy(s, h):
         return remote(
@@ -507,12 +520,13 @@
             flat_recv.at[lax.rem(2 * s + h - c + 4, 4)], (f, 2 * s + h, t),
         )
 
-    early[0] = jnp.zeros(early.shape[1:], F32)
     in_half = (
         lax.div(lax.broadcasted_iota(jnp.int32, (block_rows, 1), 0), half_rows) == t
     ).astype(F32)
 
-    def norm_two_back(s, carry):
+    def norm_two_back(s):
+        if s == 0:
+            early[0] = jnp.zeros(early.shape[1:], F32)
         swap(part_b, part_b_in, 1, s).wait()
         grad = part_b[s] + part_b_in[s]
         _, normed, recip = norm_rows(middle[s], gain2[...], bias2[...])
@@ -535,31 +549,18 @@
             def _():
                 flat_in[c] = flat[s, h]
 
-        return carry
-
-    lax.fori_loop(0, slots, norm_two_back, 0)
-    hop_two(DOWN, 1)
-    hop_one(DOWN, (0, 2), 1)
-    for u in (0, 1):
-        hop_one(UP, (1, 3), u)
-    for u in (0, 1):
-        hop_one(UP, (0, 2), u)
-    weight_grad(g_out, middle_low, low)
-    hop_one(OUT, (1, 3, 0, 2), 0)
-
     def down(s, carry):
         part_a[s] = mm(act[s], wd[...], 1, 1)
         swap(part_a, part_a_in, 2, s).start()
         return carry
 
-    lax.fori_loop(0, slots, down, 0)
-    key_acc[...] = jnp.zeros_like(key_acc)
-    value_acc[...] = jnp.zeros_like(value_acc)
-    later[...] = jnp.zeros_like(later)
-    conv_acc[...] = jnp.zeros_like(conv_acc)
-    for s in range(slots):
-        swap(part_a, part_a_in, 2, s).wait()
-        result[s] = (middle[s] + (part_a[s] + part_a_in[s])).astype(BF)
+    def feed_down():
+        lax.fori_loop(0, slots, down, 0)
+
+    def put_result():
+        for s in range(slots):
+            swap(part_a, part_a_in, 2, s).wait()
+            result[s] = (middle[s] + (part_a[s] + part_a_in[s])).astype(BF)
 
     def fg_view(block, rows):
         return wide_a.at[block // 2, rows, pl.ds(block % 2 * model, model)]
@@ -570,26 +571,51 @@
             partner,
         )
 
+    def pair_copy(block):
+        return remote(
+            fg_low.at[block], pair_in.at[block], pair_send.at[block], pair_recv.at[block],
+            (f, mate, t),
+        )
+
     def fg_copy(block):
         return remote(
-            fg_low.at[block], fg_all.at[c], fg_ssem.at[block],
-            fg_recv.at[lax.rem(block - c + 4, 4)], (f, block, t),
-        )
+            fg_low.at[block], fg_other, fg_ssem.at[block], fg_recv.at[0], (f, block, t)
+        )
+
+    def collects(block):
+        return inner * (1 - (mate == block)) + (1 - inner) * (c == block) == 1
 
     def hand_over(block):
         own_copy(block).wait_recv()
-        fg_low[block] = (fg_view(block, mine)[...] + fg_in[block]).astype(BF)
-
-        @pl.when(block != c)
+        total = fg_view(block, mine)[...] + fg_in[block]
+        fg_in[block] = total
+
+        @pl.when(jnp.logical_not(collects(block)))
         def _():
-            fg_copy(block).start()
-
-        @pl.when(block == c)
+            fg_low[block] = total.astype(BF)
+            pair_copy(block).start()
+
+    def collect(block):
+        @pl.when(collects(block))
         def _():
-            fg_all[c] = fg_low[block]
-
-    z_one(DOWN, 0)
-    for block in reversed(range(blocks)):
+            arrived(pair_in.at[block], pair_recv.at[block])
+            total = fg_in[block] + pair_in[block]
+
+            @pl.when(block == c)
+            def _():
+                fg_own[...] = total
+
+            @pl.when(block != c)
+            def _():
+                fg_low[block] = total.astype(BF)
+                fg_copy(block).start()
+
+    def attention_back(block):
+        if block == blocks - 1:
+            key_acc[...] = jnp.zeros_like(key_acc)
+            value_acc[...] = jnp.zeros_like(value_acc)
+            later[...] = jnp.zeros_like(later)
+            conv_acc[...] = jnp.zeros_like(conv_acc)
 
         @pl.when(block != c)
         def _():
@@ -597,21 +623,19 @@
 
         keys = (block + 1) * block_rows
 
-        def attend_back(n, carry, block=block, keys=keys):
-            head, piece = lax.div(n, tiles), lax.rem(n, tiles)
-            query, key, probs = soft(head, block * block_rows + piece * tile, keys)
-            lanes = lanes_at(piece * tile, tile)
+        def attend_back(head, carry, block=block, keys=keys):
+            query, key, probs = soft(head, block)
             channels = span(head * HD, HD)
-            grad_t = flat_in[block, channels, lanes]
+            grad_t = flat_in[block, channels, :]
             prob_grad = mm(grad_t.T, heads[2 * count + head, 0:keys, :], 1, 1)
             delta = jnp.sum(probs * prob_grad, axis=-1, keepdims=True)
             score_grad = (probs * (prob_grad - delta)).astype(BF)
-            query_t[channels, lanes] = (mm(score_grad, key, 1, 0) * SCALING).T
+            query_t[channels, :] = (mm(score_grad, key, 1, 0) * SCALING).T
             key_acc[head, :, 0:keys] += mm(query.T, score_grad, 1, 0)
             value_acc[head, :, 0:keys] += mm(grad_t, probs.astype(BF), 1, 0)
             return carry
 
-        lax.fori_loop(0, count * tiles, attend_back, 0)
+        lax.fori_loop(0, count, attend_back, 0)
         columns = slice(block * block_rows, (block + 1) * block_rows)
         mixed_low[...] = jnp.concatenate(
             [
@@ -634,28 +658,6 @@
         pre_grad[block] = grad
         fg_view(block, pl.ds(0, block_rows))[...] = mm(grad, wq[...], 1, 1)
         own_copy(block).start()
-        if block == 3:
-            z_one(DOWN, 1)
-            z_two(DOWN, 0)
-        if block == 2:
-            hand_over(3)
-            z_two(DOWN, 1)
-            hop_two(UP, 0)
-            hop_two(UP, 1)
-            z_three(DOWN, 0)
-        if block == 1:
-            hand_over(2)
-            z_three(DOWN, 1)
-            hop_two(OUT, 0)
-        if block == 0:
-            hand_over(1)
-
-    weight_grad(g_qkv, first_all, pre_grad)
-    for u in (0, 1):
-        hop_one(QKV, (1, 3), u)
-    for u in (0, 1):
-        hop_one(QKV, (0, 2), u)
-    hand_over(0)
 
     smalls = [(early, early_xy, early_z), (late, late_xy, late_z)]
 
@@ -701,28 +703,22 @@
         own = smalls[k][2]
         out[...] = own[0] + own[1] + own[2] + own[3]
 
-    for h in (0, 1):
-
-        @pl.when(half == h)
-        def _():
-            lanes = slice(h * part_width, (h + 1) * part_width)
-            for kind in range(3):
-                channels = slice(kind * part_width, (kind + 1) * part_width)
-                for tap in range(4):
-                    row = 2 + 3 * tap + kind
-                    early[0, row : row + 1, lanes] = conv_acc[tap : tap + 1, channels]
-
-    tp_copy(0).start()
-    z_one(UP, 0)
-    z_one(UP, 1)
-    small_tp(0)
-    z_one(OUT, 0)
-    hop_two(QKV, 0)
-    z_two(UP, 0)
-    hop_two(QKV, 1)
-    z_two(UP, 1)
-    z_two(OUT, 0)
-    small_xy(0)
+    def small_start(k):
+        if k == 0:
+            for h in (0, 1):
+
+                @pl.when(half == h)
+                def _():
+                    for tap in range(4):
+                        for kind in range(3):
+                            at = 3 * tap + kind
+                            lane = (at % 2 * 2 + h) * part_width
+                            channels = slice(kind * part_width, (kind + 1) * part_width)
+                            early[0, 2 + at // 2 : 3 + at // 2, lane : lane + part_width] = (
+                                conv_acc[tap : tap + 1, channels]
+                            )
+
+        tp_copy(k).start()
 
     def q_copy(stage, side, u):
         view = z_rows(QKV, side, u)
@@ -747,19 +743,17 @@
             q_sum[half, at, :] = (q_own[at, :].astype(F32) + q_in[at, :]).astype(BF)
             q_copy(1, side, u).start()
 
-    for d in (1, 2, 3):
-        arrived(fg_all.at[lax.rem(c - d + 4, 4)], fg_recv.at[d])
-    late[0] = jnp.zeros(late.shape[1:], F32)
     lane = late.shape[2]
 
-    def in_copy(s):
-        view = input_grad.at[s, mine]
-        return remote(view, view, in_send.at[s], in_recv.at[s], partner)
-
-    for s in range(slots):
-        grad = fg_all[2 * s].astype(F32) + fg_all[2 * s + 1]
-        rows = tok[s, mine, :].astype(F32)
-        _, normed, recip = norm_rows(rows, gain1[...], bias1[...])
+    def norm_one_back(k):
+        s = slot if k == 0 else 1 - slot
+        if k == 0:
+            late[0] = jnp.zeros(late.shape[1:], F32)
+            grad = fg_own[...]
+        else:
+            arrived(fg_other, fg_recv.at[0])
+            grad = fg_other[...].astype(F32)
+        _, normed, recip = norm_rows(tok[s, mine, :].astype(F32), gain1[...], bias1[...])
         gain_sum = jnp.sum(grad * normed, axis=0, keepdims=True)
         bias_sum = jnp.sum(grad, axis=0, keepdims=True)
         for at in range(model // lane):
@@ -769,21 +763,102 @@
         input_grad[s, mine, :] = middle_grad[s, mine, :] + norm_back(
             grad, normed, recip, gain1[...]
         )
-        in_copy(s).start()
-
-    tp_copy(1).start()
+        in_copy(k).start()
+
+    def in_copy(k):
+        view = input_grad.at[slot if k == 0 else 1 - slot, mine]
+        return remote(view, view, in_send.at[k], in_recv.at[k], partner)
+
+    send_up()
+    send_direct(QKV)
+    own_norm()
+    send_out()
+    pass_on(QKV)
+    send_down()
+    tokens()
+    pass_on(OUT)
+    pass_on(UP)
+    projections()
+    attention(3)
+    attention(2)
+    attention(1)
+    pass_on(DOWN)
+    attention(0)
+    masks()
+    out_projection()
+    feed_forward()
+    weight_grad(g_down, grad_low, act)
+    hop_one(DOWN, (1, 3), 0)
+    feed_back(0)
+    feed_back(1)
+    hop_one(DOWN, (1, 3), 1)
+    norm_two_back(0)
+    hop_two(DOWN, 0)
+    norm_two_back(1)
+    weight_grad(g_up, second, up_grad)
+    hop_one(DOWN, (0, 2), 0)
+    weight_grad(g_out, middle_low, low)
+    hop_one(DOWN, (0, 2), 1)
+    attention_back(3)
+    z_one(DOWN, 0)
+    hop_two(DOWN, 1)
+    hop_one(UP, (1, 3), 0)
+    hop_one(UP, (0, 2), 0)
+    attention_back(2)
+    z_one(DOWN, 1)
+    attention_back(1)
+    z_two(DOWN, 0)
+    hop_two(UP, 0)
+    hand_over(2)
+    attention_back(0)
+    hand_over(0)
+    z_two(DOWN, 1)
+    hop_one(OUT, (0, 2), 0)
+    feed_down()
+    hop_one(UP, (1, 3), 1)
+    z_one(UP, 0)
+    z_three(DOWN, 0)
+    weight_grad(g_qkv, first_all, pre_grad)
+    hop_one(QKV, (1, 3), 0)
+    collect(2)
+    hop_one(QKV, (1, 3), 1)
+    collect(0)
+    hand_over(3)
+    put_result()
+    hop_one(QKV, (0, 2), 0)
+    hand_over(1)
+    z_two(UP, 0)
+    small_start(0)
+    hop_one(OUT, (1, 3), 0)
+    hop_one(UP, (0, 2), 1)
+    z_three(DOWN, 1)
+    hop_one(QKV, (0, 2), 1)
+    collect(3)
+    hop_two(QKV, 0)
+    hop_two(QKV, 1)
+    hop_two(OUT, 0)
+    z_three(UP, 0)
     q_one(0)
+    collect(1)
+    q_one(1)
+    small_tp(0)
+    hop_two(UP, 1)
+    z_one(OUT, 0)
+    norm_one_back(0)
+    z_one(UP, 1)
+    z_two(OUT, 0)
+    norm_one_back(1)
+    q_two(0)
+    small_start(1)
     small_tp(1)
-    z_three(UP, 0)
-    q_one(1)
+    small_xy(1)
+    small_xy(0)
+    q_two(1)
+    z_two(UP, 1)
+    z_three(OUT, 0)
     z_three(UP, 1)
-    small_xy(1)
-    z_three(OUT, 0)
     small_z(0, early_out)
-    q_two(0)
-    q_two(1)
     small_z(1, late_out)
-
     for w in range(4):
         reduced(w)
         for kind in (0, 1):
@@ -794,12 +869,19 @@
         for u in (0, 1):
             q_copy(1, side, u).wait_send()
             arrived(q_sum.at[1 - half, z_rows(QKV, side, u)], q_recv.at[1, side, u])
-    for d in (1, 2, 3):
-        tok_copy(d).wait_send()
-        tok_pass(lax.rem(c - d + 4, 4), d).wait_send()
+    for k in range(3):
+        tok_pass(k).wait_send()
+        if k < 2:
+            tok_copy(k).wait_send()
+
+            @pl.when(inner == 1)
+            def _():
+                tok_relay(k).wait_send()
+
     for s in range(slots):
         in_copy(s).wait_send()
-        arrived(input_grad.at[s, theirs], in_recv.at[s])
+        view = input_grad.at[slot if s == 0 else 1 - slot, theirs]
+        arrived(view, in_recv.at[s])
         for h in (0, 1):
 
             @pl.when(2 * s + h != c)
@@ -812,7 +894,16 @@
         @pl.when(block != c)
         def _():
             att_copy(block).wait_send()
-            fg_copy(block).wait_send()
+
+        @pl.when(jnp.logical_not(collects(block)))
+        def _():
+            pair_copy(block).wait_send()
+
+        @pl.when(collects(block))
+        def _():
+            @pl.when(block != c)
+            def _():
+                fg_copy(block).wait_send()
 
 
 def layer_call(
@@ -840,7 +931,7 @@
         name="layer",
         out_shape=[
             struct(tall), struct(tall, F32), struct((share, units)), struct((share, units)),
-            struct((share, channels)), struct((2, share, width)), struct((16, model), F32),
+            struct((share, channels)), struct((2, share, width)), struct((8, model), F32),
             struct((8, 256), F32),
         ],
         in_specs=[SMEM] + [ANY] * 6 + [VMEM] * 6,
@@ -864,14 +955,15 @@
             [vmem((share, n)) for n in columns[:3]],
             [vmem((2, share, n)) for n in columns[:3]],
             vmem((share, width)), vmem((share, width)),
+            vmem((8, blocks * block_rows), F32),
             vmem((part // HD, HD, blocks * block_rows), F32),
             vmem((part // HD, HD, blocks * block_rows), F32),
             vmem((part, block_rows), F32), vmem((8, width), F32),
             vmem((block_rows, width), F32), vmem((blocks, block_rows, width)),
             vmem((8, width), F32),
             vmem((blocks, half, model), F32), vmem((blocks, half, model)),
-            vmem((blocks, half, model)),
-            vmem((2, 16, model), F32), vmem((4, 16, model), F32), vmem((4, 16, model), F32),
+            vmem((blocks, half, model)), vmem((half, model), F32), vmem((half, model)),
+            vmem((2, 8, model), F32), vmem((4, 8, model), F32), vmem((4, 8, model), F32),
             vmem((2, 8, 256), F32), vmem((4, 8, 256), F32), vmem((4, 8, 256), F32),
             dma((6,)), dma((4,)), dma((4,)), dma((4,)), dma((4,)), dma((4, 4)), dma((4, 4)),
             dma((4,)), dma((4,)),
@@ -880,7 +972,8 @@
             [dma((2, n)) for n in CUTS], [dma((2, n)) for n in CUTS],
             [dma((3, 2, n)) for n in CUTS[:3]], [dma((3, 2, n)) for n in CUTS[:3]],
             dma((2, 2, 2)), dma((2, 2, 2)),
-            dma((4,)), dma((4,)), dma((4,)), dma((4,)), dma((slots,)), dma((slots,)),
+            dma((4,)), dma((1,)), dma((4,)), dma((4,)), dma((4,)), dma((4,)), dma((slots,)),
+            dma((slots,)),
             dma((2, 7)), dma((2, 7)),
         ],
         compiler_params=pltpu.CompilerParams(
@@ -911,9 +1004,14 @@
         bias1[lanes] = late[4 + at]
     gain2[...] = early[0]
     bias2[...] = early[1]
-    for tap in range(3):
-        taps[tap] = early[2 + 3 * tap : 5 + 3 * tap, 0 : 2 * part]
-    shift[...] = early[11:14, 0 : 2 * part]
+    for at in range(12):
+        lane = at % 2 * 2 * part
+        values = early[2 + at // 2 : 3 + at // 2, lane : lane + 2 * part]
+        tap, kind = at // 3, at % 3
+        if tap < 3:
+            taps[tap, kind : kind + 1, :] = values
+        else:
+            shift[kind : kind + 1, :] = values
 
 
 def finish_call(result, grad, down, up, out, qkv, early, late):

time: 180 us -> 154 us (0.86)
  Pallas kernels: 180 us -> 153 us
    pallas_call x1, Pallas kernels: 175 us -> 148 us  [layer_call(): pl.pallas_call(layer_kernel, name='layer', out_shape=[struct(tall), struc...]
where the time goes in v4:
time: 154 us; the launch traced here: 153 us
  Pallas kernels  153 us (99%)
    pallas_call x1, Pallas kernels, layer_call(): pl.pallas_call(layer_kernel, name='layer', out_shape=[struct(tall), struc...  148 us
    pallas_call x1, Pallas kernels, finish_call(): pl.pallas_call(finish_kernel, name='finish', out_shape=[struct(result.sha...  4.98 us

profile of v4, /device:TPU:0, one launch (start us, length us, event | category | flops | bytes accessed | tf_op | source)
XLA Modules:
  0.0 153.4 jit_solution(14896822865960447540)
XLA Ops:
  0.6 147.8 %layer.1 = (bf16[2,256,768]{2,1,0:T(8,128)(2,1)}, f32[2,256,768]{2,1,0:T(8,128)}, bf16[192,1536]{1,0:T(8,128)(2,1)}, bf16[192,1536]{1,0:T(8,128)(2,1)}, bf16[192...) custom-call(s32[2]{0:T(128)} %lens.1, bf16[2,256,768]{2,1,0:T(8,128)(2,1)} %tok_in.1, ...), custom_call_target="tpu_custom_call" | custom-call | tf_op jit(solution)/shard_map/layer/pallas_call | solution.py:929
  148.4 5.0 %finish.1 = (bf16[2,256,768]{2,1,0:T(8,128)(2,1)}, f32[2,256,768]{2,1,0:T(8,128)}, f32[768]{0:T(1024)}, f32[768]{0:T(1024)}, f32[3,192,384]{2,1,0:T(8,128)}, /*i...) custom-call(bf16[2,256,768]{2,1,0:T(8,128)(2,1)} %get-tuple-element., ...), custom_call_target="tpu_custom_call" | custom-call | tf_op jit(solution)/shard_map/finish/pallas_call | solution.py:1024

commit v5 on v4

--- a/solution.py
+++ b/solution.py
@@ -70,7 +70,7 @@
 ANY = pl.BlockSpec(memory_space=pl.ANY)
 VMEM = pl.BlockSpec(memory_space=pltpu.VMEM)
 SMEM = pl.BlockSpec(memory_space=pltpu.SMEM)
-CUTS = (2, 2, 1, 2)
+CUTS = (3, 3, 1, 2)
 DOWN, UP, OUT, QKV = range(4)
 
 
@@ -110,7 +110,7 @@
     g_down, g_up, g_out, g_qkv, near, far_send, far, z_own, z_in, q_own, q_in,
     key_bias, key_acc, value_acc, query_t, later, mixed_low, pre_grad, conv_acc,
     fg_in, fg_low, pair_in, fg_own, fg_other, early, early_xy, early_z, late, late_xy, late_z,
-    load_sem, tok_send, tok_recv, pass_send, pass_recv, w_send, w_recv, att_send, att_recv,
+    load_sem, tok_send, tok_recv, pass_send, pass_recv, mate_send, mate_recv, w_send, w_recv, att_send, att_recv,
     part_send, part_recv, flat_send, flat_recv,
     near_send, near_recv, far_ssem, far_recv, z_send, z_recv, q_send, q_recv,
     fg_ssem, fg_recv, pair_send, pair_recv, own_send, own_recv, in_send, in_recv, sm_send, sm_recv,
@@ -191,24 +191,28 @@
     for k in (0, 1):
         tok_copy(k).start()
 
-    def shard_part(owner, kind):
+
+    def shard_part(w, owner, kind):
+        start, size = owner * share, share
+        if w == DOWN:
+            start, size = start + half * rows_half, rows_half
         if kind < 2:
-            return span(owner * share, share)
-        return span(owner * share + (kind - 2) * rows_half, rows_half)
+            return span(start, size)
+        return span(start + (kind - 2) * (size // 2), size // 2)
 
     def direct(w, kind):
-        view = wholes[w].at[shard_rows]
+        view = wholes[w].at[shard_part(w, f, 0)]
         target = (fx, c, t) if kind == 0 else (fy, c, t)
         return remote(view, view, w_send.at[w, kind], w_recv.at[w, kind], target)
 
     def relay(w, kind):
         origin, target = (fx, (fy, c, t)) if kind == 2 else (fy, (fx, c, t))
-        view = wholes[w].at[shard_part(origin, kind)]
+        view = wholes[w].at[shard_part(w, origin, kind)]
         return remote(view, view, w_send.at[w, kind], w_recv.at[w, kind], target)
 
     def landed(w, kind):
         owner = (fx, fy, fd, fd)[kind]
-        arrived(wholes[w].at[shard_part(owner, kind)], w_recv.at[w, kind])
+        arrived(wholes[w].at[shard_part(w, owner, kind)], w_recv.at[w, kind])
 
     def send_direct(w):
         direct(w, 0).start()
@@ -219,6 +223,24 @@
         relay(w, 2).start()
         landed(w, 1)
         relay(w, 3).start()
+
+    def half_of(k, side):
+        return wd.at[span((fx, fy, fd)[k] * share + side * rows_half, rows_half)]
+
+    def mate_copy(k):
+        view = half_of(k, half)
+        return remote(view, view, mate_send.at[k], mate_recv.at[k], (f, mate, t))
+
+    def pass_down():
+        for k in (0, 1):
+            landed(DOWN, k)
+            relay(DOWN, 2 + k).start()
+            mate_copy(k).start()
+
+    def pass_down_last():
+        landed(DOWN, 2)
+        landed(DOWN, 3)
+        mate_copy(2).start()
 
     loads["wq"].wait()
     for h in (0, 1):
@@ -240,22 +262,23 @@
         loads["tok"].wait()
         first_all[c] = first_norm(tok[slot])
 
-    def tokens():
-        for k in range(3):
-            source = tok_order(k)
-            arrived(first_all.at[source, mine], tok_recv.at[source])
-
-            @pl.when((inner == 1) | (k == 0))
+    def tokens(k):
+        source = tok_order(k)
+        arrived(first_all.at[source, mine], tok_recv.at[source])
+
+        @pl.when((inner == 1) | (k == 0))
+        def _():
+            first_all[source, mine, :] = first_norm(first_all[source, mine, :])
+
+        if k < 2:
+
+            @pl.when(inner == 1)
             def _():
-                first_all[source, mine, :] = first_norm(first_all[source, mine, :])
-
-            if k < 2:
-
-                @pl.when(inner == 1)
-                def _():
-                    tok_relay(k).start()
-
-            tok_pass(k).start()
+                tok_relay(k).start()
+
+        tok_pass(k).start()
+
+    def tokens_passed():
         for k in range(3):
             arrived(first_all.at[tok_order(k), theirs], pass_recv.at[k])
 
@@ -384,16 +407,19 @@
             landed(UP, kind)
         lax.fori_loop(0, slots, feed, 0)
 
-    def weight_grad(target, left, right):
+    def weight_grad(target, left, right, part):
+        chunks = model // 256
+        first = chunks * lax.rem(lax.div(f, 2) + 1 - part, 2)
+
         def step(j, carry):
-            at = lanes_at(j * 128, 128)
+            at = lanes_at((first + j) * 128, 128)
             rows = left.shape[0] * left.shape[1]
             lhs = left[:, :, at].reshape(rows, 128)
             rhs = right[...].reshape(rows, right.shape[2])
             target[at, :] = mm(lhs, rhs, 0, 0).astype(BF)
             return carry
 
-        lax.fori_loop(0, model // 128, step, 0)
+        lax.fori_loop(0, chunks, step, 0)
 
     grads = [g_down, g_up, g_out, g_qkv]
     finals = [down_out, up_out, out_out]
@@ -507,8 +533,8 @@
 
     def feed_back(s):
         if s == 0:
-            for kind in (2, 3):
-                landed(DOWN, kind)
+            for k in range(3):
+                arrived(half_of(k, 1 - half), mate_recv.at[k])
         grad = (mm(grad_low[s], wd[...], 1, 0) * 2.0 * wide_a[s]).astype(BF)
         up_grad[s] = grad
         part_b[s] = mm(grad, wu[...], 1, 1)
@@ -769,96 +795,116 @@
         view = input_grad.at[slot if k == 0 else 1 - slot, mine]
         return remote(view, view, in_send.at[k], in_recv.at[k], partner)
 
+    send_out()
+    send_direct(QKV)
+    send_down()
+    tokens(0)
+    tokens(1)
+    pass_on(QKV)
     send_up()
-    send_direct(QKV)
     own_norm()
-    send_out()
-    pass_on(QKV)
-    send_down()
-    tokens()
+    pass_down()
+    tokens(2)
+    tokens_passed()
     pass_on(OUT)
-    pass_on(UP)
     projections()
     attention(3)
-    attention(2)
-    attention(1)
-    pass_on(DOWN)
     attention(0)
     masks()
+    attention(1)
+    pass_on(UP)
+    attention(2)
+    pass_down_last()
     out_projection()
     feed_forward()
-    weight_grad(g_down, grad_low, act)
+    feed_back(0)
+    weight_grad(g_down, grad_low, act, 0)
     hop_one(DOWN, (1, 3), 0)
-    feed_back(0)
+    hop_one(DOWN, (1, 3), 2)
     feed_back(1)
+    norm_two_back(0)
+    weight_grad(g_down, grad_low, act, 1)
     hop_one(DOWN, (1, 3), 1)
-    norm_two_back(0)
+    norm_two_back(1)
+    hop_one(DOWN, (0, 2), 0)
     hop_two(DOWN, 0)
-    norm_two_back(1)
-    weight_grad(g_up, second, up_grad)
-    hop_one(DOWN, (0, 2), 0)
-    weight_grad(g_out, middle_low, low)
+    hop_two(DOWN, 2)
+    weight_grad(g_up, second, up_grad, 0)
+    for part in (0, 1):
+        weight_grad(g_out, middle_low, low, part)
+    hop_one(DOWN, (0, 2), 2)
+    hop_two(DOWN, 1)
     hop_one(DOWN, (0, 2), 1)
+    hop_one(OUT, (1, 3), 0)
     attention_back(3)
     z_one(DOWN, 0)
-    hop_two(DOWN, 1)
+    attention_back(2)
+    z_one(DOWN, 2)
+    hop_one(UP, (1, 3), 1)
+    attention_back(1)
+    z_one(DOWN, 1)
     hop_one(UP, (1, 3), 0)
-    hop_one(UP, (0, 2), 0)
-    attention_back(2)
-    z_one(DOWN, 1)
-    attention_back(1)
+    hop_one(OUT, (0, 2), 0)
     z_two(DOWN, 0)
-    hop_two(UP, 0)
+    attention_back(0)
     hand_over(2)
-    attention_back(0)
+    hand_over(3)
+    weight_grad(g_qkv, first_all, pre_grad, 0)
     hand_over(0)
     z_two(DOWN, 1)
-    hop_one(OUT, (0, 2), 0)
+    hop_one(QKV, (1, 3), 1)
+    weight_grad(g_up, second, up_grad, 1)
+    z_three(DOWN, 0)
+    z_two(DOWN, 2)
+    hop_one(UP, (1, 3), 2)
     feed_down()
-    hop_one(UP, (1, 3), 1)
+    hop_two(OUT, 0)
+    hop_one(UP, (0, 2), 1)
+    hand_over(1)
+    hop_one(QKV, (1, 3), 0)
+    weight_grad(g_qkv, first_all, pre_grad, 1)
+    collect(0)
+    small_start(0)
+    collect(3)
+    collect(2)
+    hop_one(QKV, (0, 2), 1)
+    hop_two(UP, 0)
+    small_tp(0)
+    z_one(OUT, 0)
+    collect(1)
+    hop_two(QKV, 1)
+    hop_two(UP, 1)
+    hop_two(UP, 2)
+    z_three(DOWN, 1)
+    z_three(DOWN, 2)
+    norm_one_back(0)
+    hop_one(QKV, (0, 2), 0)
+    q_one(1)
+    norm_one_back(1)
+    small_xy(0)
+    hop_one(UP, (0, 2), 0)
+    hop_one(UP, (0, 2), 2)
+    z_one(UP, 1)
     z_one(UP, 0)
-    z_three(DOWN, 0)
-    weight_grad(g_qkv, first_all, pre_grad)
-    hop_one(QKV, (1, 3), 0)
-    collect(2)
-    hop_one(QKV, (1, 3), 1)
-    collect(0)
-    hand_over(3)
+    z_two(UP, 1)
+    q_two(1)
+    z_two(UP, 0)
+    small_z(0, early_out)
+    z_three(UP, 1)
+    z_two(OUT, 0)
+    hop_two(QKV, 0)
+    z_three(UP, 0)
+    small_start(1)
+    q_one(0)
+    small_tp(1)
+    z_three(OUT, 0)
+    small_xy(1)
+    z_one(UP, 2)
+    q_two(0)
+    z_two(UP, 2)
     put_result()
-    hop_one(QKV, (0, 2), 0)
-    hand_over(1)
-    z_two(UP, 0)
-    small_start(0)
-    hop_one(OUT, (1, 3), 0)
-    hop_one(UP, (0, 2), 1)
-    z_three(DOWN, 1)
-    hop_one(QKV, (0, 2), 1)
-    collect(3)
-    hop_two(QKV, 0)
-    hop_two(QKV, 1)
-    hop_two(OUT, 0)
-    z_three(UP, 0)
-    q_one(0)
-    collect(1)
-    q_one(1)
-    small_tp(0)
-    hop_two(UP, 1)
-    z_one(OUT, 0)
-    norm_one_back(0)
-    z_one(UP, 1)
-    z_two(OUT, 0)
-    norm_one_back(1)
-    q_two(0)
-    small_start(1)
-    small_tp(1)
-    small_xy(1)
-    small_xy(0)
-    q_two(1)
-    z_two(UP, 1)
-    z_three(OUT, 0)
-    z_three(UP, 1)
-    small_z(0, early_out)
     small_z(1, late_out)
+    z_three(UP, 2)
     for w in range(4):
         reduced(w)
         for kind in (0, 1):
@@ -866,10 +912,11 @@
         for kind in (2, 3):
             relay(w, kind).wait_send()
     for side in (0, 1):
-        for u in (0, 1):
+        for u in range(CUTS[QKV]):
             q_copy(1, side, u).wait_send()
             arrived(q_sum.at[1 - half, z_rows(QKV, side, u)], q_recv.at[1, side, u])
     for k in range(3):
+        mate_copy(k).wait_send()
         tok_pass(k).wait_send()
         if k < 2:
             tok_copy(k).wait_send()
@@ -965,13 +1012,14 @@
             vmem((blocks, half, model)), vmem((half, model), F32), vmem((half, model)),
             vmem((2, 8, model), F32), vmem((4, 8, model), F32), vmem((4, 8, model), F32),
             vmem((2, 8, 256), F32), vmem((4, 8, 256), F32), vmem((4, 8, 256), F32),
-            dma((6,)), dma((4,)), dma((4,)), dma((4,)), dma((4,)), dma((4, 4)), dma((4, 4)),
+            dma((6,)), dma((4,)), dma((4,)), dma((4,)), dma((4,)), dma((3,)), dma((3,)),
+            dma((4, 4)), dma((4, 4)),
             dma((4,)), dma((4,)),
             dma((3, slots)), dma((3, slots)), dma((slots, 2)), dma((4,)),
             [dma((4, n)) for n in CUTS], [dma((4, n)) for n in CUTS],
             [dma((2, n)) for n in CUTS], [dma((2, n)) for n in CUTS],
             [dma((3, 2, n)) for n in CUTS[:3]], [dma((3, 2, n)) for n in CUTS[:3]],
-            dma((2, 2, 2)), dma((2, 2, 2)),
+            dma((2, 2, CUTS[QKV])), dma((2, 2, CUTS[QKV])),
             dma((4,)), dma((1,)), dma((4,)), dma((4,)), dma((4,)), dma((4,)), dma((slots,)),
             dma((slots,)),
             dma((2, 7)), dma((2, 7)),
@@ -1021,8 +1069,37 @@
         return jax.ShapeDtypeStruct(tuple(shape), kind)
 
     vector = struct((model,))
+    steps = 4
+    rows = share // steps
+    cut = result.shape[1] * result.shape[0] // steps
+
+    def tall(index):
+        return index // 2, index % 2, 0
+
+    def whole(shape):
+        return pl.BlockSpec(shape, lambda index: (0,) * len(shape))
+
+    def block(width):
+        return pl.BlockSpec((rows, width), lambda index: (index, 0))
+
+    def triple(count, width):
+        return pl.BlockSpec((count, rows, width), lambda index: (0, index, 0))
+
+    tall_spec = pl.BlockSpec((1, cut, model), tall)
+    vector_spec = whole((model,))
+    units = up.shape[1]
     return pl.pallas_call(
         finish_kernel,
+        grid=(steps,),
+        in_specs=[
+            tall_spec, tall_spec, block(units), block(units), block(channels),
+            triple(2, qkv.shape[2]), whole(early.shape), whole(late.shape),
+        ],
+        out_specs=[
+            tall_spec, tall_spec, vector_spec, vector_spec, triple(3, channels),
+            whole((3, 3, channels)), whole((3, channels)), block(channels), vector_spec,
+            vector_spec, block(units), block(units),
+        ],
         name="finish",
         out_shape=[
             struct(result.shape, BF), struct(grad.shape), vector, vector,

time: 154 us -> 149 us (0.968)
  Pallas kernels: 153 us -> 148 us
    pallas_call x1, Pallas kernels: 148 us -> 143 us  [layer_call(): pl.pallas_call(layer_kernel, name='layer', out_shape=[struct(tall), struc...]
where the time goes in v5:
time: 149 us
  Pallas kernels  148 us (99%)
    pallas_call x1, Pallas kernels, layer_call(): pl.pallas_call(layer_kernel, name='layer', out_shape=[struct(tall), struc...  143 us
    pallas_call x1, Pallas kernels, finish_call(): pl.pallas_call(finish_kernel, grid=(steps,), in_specs=[tall_spec, tall_sp...  5.17 us

profile of v5, /device:TPU:0, one launch (start us, length us, event | category | flops | bytes accessed | tf_op | source)
XLA Modules:
  0.0 148.7 jit_solution(2987802400022568387)
XLA Ops:
  0.6 142.7 %layer.1 = (bf16[2,256,768]{2,1,0:T(8,128)(2,1)}, f32[2,256,768]{2,1,0:T(8,128)}, bf16[192,1536]{1,0:T(8,128)(2,1)}, bf16[192,1536]{1,0:T(8,128)(2,1)}, bf16[192...) custom-call(s32[2]{0:T(128)} %lens.1, bf16[2,256,768]{2,1,0:T(8,128)(2,1)} %tok_in.1, ...), custom_call_target="tpu_custom_call" | custom-call | tf_op jit(solution)/shard_map/layer/pallas_call | solution.py:976
  143.4 5.2 %finish.1 = (bf16[2,256,768]{2,1,0:T(8,128)(2,1)}, f32[2,256,768]{2,1,0:T(8,128)}, f32[768]{0:T(1024)}, f32[768]{0:T(1024)}, f32[3,192,384]{2,1,0:T(8,128)}, /*i...) custom-call(bf16[2,256,768]{2,1,0:T(8,128)(2,1)} %get-tuple-element., ...), custom_call_target="tpu_custom_call" | custom-call | tf_op jit(solution)/shard_map/finish/pallas_call | solution.py:1091

commit v6 on v5

--- a/solution.py
+++ b/solution.py
@@ -797,114 +797,114 @@
 
     send_out()
     send_direct(QKV)
+    tokens(0)
     send_down()
-    tokens(0)
+    pass_on(QKV)
     tokens(1)
-    pass_on(QKV)
     send_up()
+    tokens(2)
+    pass_down()
     own_norm()
-    pass_down()
-    tokens(2)
     tokens_passed()
     pass_on(OUT)
     projections()
+    attention(2)
+    attention(1)
+    attention(0)
     attention(3)
-    attention(0)
+    pass_on(UP)
     masks()
-    attention(1)
-    pass_on(UP)
-    attention(2)
+    out_projection()
     pass_down_last()
-    out_projection()
     feed_forward()
+    weight_grad(g_down, grad_low, act, 0)
+    hop_one(DOWN, (1, 3), 2)
+    hop_one(DOWN, (1, 3), 1)
     feed_back(0)
-    weight_grad(g_down, grad_low, act, 0)
-    hop_one(DOWN, (1, 3), 0)
-    hop_one(DOWN, (1, 3), 2)
+    weight_grad(g_down, grad_low, act, 1)
+    hop_one(DOWN, (0, 2), 2)
     feed_back(1)
     norm_two_back(0)
-    weight_grad(g_down, grad_low, act, 1)
-    hop_one(DOWN, (1, 3), 1)
+    hop_two(DOWN, 2)
+    hop_two(DOWN, 1)
+    hop_one(DOWN, (1, 3), 0)
+    hop_one(DOWN, (0, 2), 1)
     norm_two_back(1)
+    weight_grad(g_up, second, up_grad, 0)
+    weight_grad(g_up, second, up_grad, 1)
     hop_one(DOWN, (0, 2), 0)
+    z_one(DOWN, 2)
+    attention_back(3)
     hop_two(DOWN, 0)
-    hop_two(DOWN, 2)
-    weight_grad(g_up, second, up_grad, 0)
+    z_two(DOWN, 2)
+    hop_one(UP, (1, 3), 1)
+    z_one(DOWN, 1)
+    attention_back(2)
+    hop_one(UP, (1, 3), 2)
+    hop_one(UP, (1, 3), 0)
+    hop_one(UP, (0, 2), 0)
+    hop_one(UP, (0, 2), 2)
+    z_one(DOWN, 0)
+    hand_over(3)
+    z_two(DOWN, 1)
+    attention_back(1)
+    z_three(DOWN, 2)
+    hand_over(2)
+    attention_back(0)
+    z_two(DOWN, 0)
+    hop_two(UP, 0)
+    hand_over(0)
+    feed_down()
+    collect(3)
+    z_three(DOWN, 1)
+    hand_over(1)
+    hop_two(UP, 1)
+    hop_two(UP, 2)
+    collect(0)
+    collect(2)
+    small_start(0)
+    z_one(UP, 0)
+    weight_grad(g_qkv, first_all, pre_grad, 0)
+    hop_one(UP, (0, 2), 1)
+    put_result()
     for part in (0, 1):
         weight_grad(g_out, middle_low, low, part)
-    hop_one(DOWN, (0, 2), 2)
-    hop_two(DOWN, 1)
-    hop_one(DOWN, (0, 2), 1)
+    collect(1)
+    z_two(UP, 0)
+    z_three(DOWN, 0)
+    hop_one(QKV, (1, 3), 0)
+    z_one(UP, 2)
     hop_one(OUT, (1, 3), 0)
-    attention_back(3)
-    z_one(DOWN, 0)
-    attention_back(2)
-    z_one(DOWN, 2)
-    hop_one(UP, (1, 3), 1)
-    attention_back(1)
-    z_one(DOWN, 1)
-    hop_one(UP, (1, 3), 0)
+    z_one(UP, 1)
+    weight_grad(g_qkv, first_all, pre_grad, 1)
     hop_one(OUT, (0, 2), 0)
-    z_two(DOWN, 0)
-    attention_back(0)
-    hand_over(2)
-    hand_over(3)
-    weight_grad(g_qkv, first_all, pre_grad, 0)
-    hand_over(0)
-    z_two(DOWN, 1)
+    norm_one_back(0)
+    hop_one(QKV, (0, 2), 1)
+    hop_one(QKV, (0, 2), 0)
+    norm_one_back(1)
+    z_two(UP, 2)
+    z_three(UP, 0)
+    hop_two(OUT, 0)
     hop_one(QKV, (1, 3), 1)
-    weight_grad(g_up, second, up_grad, 1)
-    z_three(DOWN, 0)
-    z_two(DOWN, 2)
-    hop_one(UP, (1, 3), 2)
-    feed_down()
-    hop_two(OUT, 0)
-    hop_one(UP, (0, 2), 1)
-    hand_over(1)
-    hop_one(QKV, (1, 3), 0)
-    weight_grad(g_qkv, first_all, pre_grad, 1)
-    collect(0)
-    small_start(0)
-    collect(3)
-    collect(2)
-    hop_one(QKV, (0, 2), 1)
-    hop_two(UP, 0)
+    z_two(UP, 1)
+    z_three(UP, 2)
+    z_one(OUT, 0)
+    hop_two(QKV, 1)
+    z_three(UP, 1)
+    q_one(1)
+    small_start(1)
+    z_two(OUT, 0)
     small_tp(0)
-    z_one(OUT, 0)
-    collect(1)
-    hop_two(QKV, 1)
-    hop_two(UP, 1)
-    hop_two(UP, 2)
-    z_three(DOWN, 1)
-    z_three(DOWN, 2)
-    norm_one_back(0)
-    hop_one(QKV, (0, 2), 0)
-    q_one(1)
-    norm_one_back(1)
+    hop_two(QKV, 0)
+    q_two(1)
+    small_tp(1)
     small_xy(0)
-    hop_one(UP, (0, 2), 0)
-    hop_one(UP, (0, 2), 2)
-    z_one(UP, 1)
-    z_one(UP, 0)
-    z_two(UP, 1)
-    q_two(1)
-    z_two(UP, 0)
+    small_xy(1)
+    q_one(0)
+    z_three(OUT, 0)
+    q_two(0)
     small_z(0, early_out)
-    z_three(UP, 1)
-    z_two(OUT, 0)
-    hop_two(QKV, 0)
-    z_three(UP, 0)
-    small_start(1)
-    q_one(0)
-    small_tp(1)
-    z_three(OUT, 0)
-    small_xy(1)
-    z_one(UP, 2)
-    q_two(0)
-    z_two(UP, 2)
-    put_result()
     small_z(1, late_out)
-    z_three(UP, 2)
     for w in range(4):
         reduced(w)
         for kind in (0, 1):

time: 149 us -> 142 us (0.953)
  Pallas kernels: 148 us -> 141 us
    pallas_call x1, Pallas kernels: 143 us -> 136 us  [layer_call(): pl.pallas_call(layer_kernel, name='layer', out_shape=[struct(tall), struc...]
where the time goes in v6:
time: 142 us
  Pallas kernels  141 us (99%)
    pallas_call x1, Pallas kernels, layer_call(): pl.pallas_call(layer_kernel, name='layer', out_shape=[struct(tall), struc...  136 us
    pallas_call x1, Pallas kernels, finish_call(): pl.pallas_call(finish_kernel, grid=(steps,), in_specs=[tall_spec, tall_sp...  5.17 us

profile of v6, /device:TPU:0, one launch (start us, length us, event | category | flops | bytes accessed | tf_op | source)
XLA Modules:
  0.0 141.9 jit_solution(2952641333673713384)
XLA Ops:
  0.6 135.9 %layer.1 = (bf16[2,256,768]{2,1,0:T(8,128)(2,1)}, f32[2,256,768]{2,1,0:T(8,128)}, bf16[192,1536]{1,0:T(8,128)(2,1)}, bf16[192,1536]{1,0:T(8,128)(2,1)}, bf16[192...) custom-call(s32[2]{0:T(128)} %lens.1, bf16[2,256,768]{2,1,0:T(8,128)(2,1)} %tok_in.1, ...), custom_call_target="tpu_custom_call" | custom-call | tf_op jit(solution)/shard_map/layer/pallas_call | solution.py:976
  136.6 5.2 %finish.1 = (bf16[2,256,768]{2,1,0:T(8,128)(2,1)}, f32[2,256,768]{2,1,0:T(8,128)}, f32[768]{0:T(1024)}, f32[768]{0:T(1024)}, f32[3,192,384]{2,1,0:T(8,128)}, /*i...) custom-call(bf16[2,256,768]{2,1,0:T(8,128)(2,1)} %get-tuple-element., ...), custom_call_target="tpu_custom_call" | custom-call | tf_op jit(solution)/shard_map/finish/pallas_call | solution.py:1091

commit v7 on v6

--- a/solution.py
+++ b/solution.py
@@ -1069,12 +1069,12 @@
         return jax.ShapeDtypeStruct(tuple(shape), kind)
 
     vector = struct((model,))
-    steps = 4
+    steps = result.shape[0]
     rows = share // steps
     cut = result.shape[1] * result.shape[0] // steps
 
     def tall(index):
-        return index // 2, index % 2, 0
+        return index, 0, 0
 
     def whole(shape):
         return pl.BlockSpec(shape, lambda index: (0,) * len(shape))

time: 142 us -> 141 us (level)
  no operation moved by 1% of the time
where the time goes in v7:
time: 141 us
  Pallas kernels  140 us (99%)
    pallas_call x1, Pallas kernels, layer_call(): pl.pallas_call(layer_kernel, name='layer', out_shape=[struct(tall), struc...  136 us
    pallas_call x1, Pallas kernels, finish_call(): pl.pallas_call(finish_kernel, grid=(steps,), in_specs=[tall_spec, tall_sp...  4.24 us

profile of v7, /device:TPU:0, one launch (start us, length us, event | category | flops | bytes accessed | tf_op | source)
XLA Modules:
  0.0 141.0 jit_solution(14189592110016762476)
XLA Ops:
  0.6 135.9 %layer.1 = (bf16[2,256,768]{2,1,0:T(8,128)(2,1)}, f32[2,256,768]{2,1,0:T(8,128)}, bf16[192,1536]{1,0:T(8,128)(2,1)}, bf16[192,1536]{1,0:T(8,128)(2,1)}, bf16[192...) custom-call(s32[2]{0:T(128)} %lens.1, bf16[2,256,768]{2,1,0:T(8,128)(2,1)} %tok_in.1, ...), custom_call_target="tpu_custom_call" | custom-call | tf_op jit(solution)/shard_map/layer/pallas_call | solution.py:976
  136.6 4.2 %finish.1 = (bf16[2,256,768]{2,1,0:T(8,128)(2,1)}, f32[2,256,768]{2,1,0:T(8,128)}, f32[768]{0:T(1024)}, f32[768]{0:T(1024)}, f32[3,192,384]{2,1,0:T(8,128)}, /*i...) custom-call(bf16[2,256,768]{2,1,0:T(8,128)(2,1)} %get-tuple-element., ...), custom_call_target="tpu_custom_call" | custom-call | tf_op jit(solution)/shard_map/finish/pallas_call | solution.py:1091
